TPU v7x, 32 devices: a whole 2x2x4 slice. The times are simulated.
32 devices in a mesh: dp: 8 (over z, y), tensor: 4 (over x, core).
Axes of the slice: x: 2, y: 2, z: 4, core: 2. Of those that a mesh axis runs over, the one named last changes fastest.
Arguments:
- tokens: bfloat16 [7168, 1024], P(('dp', 'tensor')), may hold values from -6 to 6
- frames: bfloat16 [24000, 1024], P(('dp', 'tensor')), may hold values from -6 to 6, as said below
- cotangent: bfloat16 [7168, 1024], P(('dp', 'tensor')), may hold values from -6 to 6
- attention_weights: bfloat16 [2, 4, 1024, 1024], P(None, None, 'dp', 'tensor'), as said below
- dense_weights: bfloat16 [2, 1024, 4, 1024], P(None, 'dp', None, 'tensor'), may hold values from -0.1875 to 0.1875
- unit_bias: bfloat16 [16, 512], P('tensor', 'dp'), may hold values from -3 to 3, as said below
- norm_bias: bfloat16 [9, 1024], P(None, 'dp'), as said below
- attention_mean: float32 [2, 4, 1024, 1024], P(None, None, 'dp', 'tensor'), may hold values from -0.0625 to 0.0625
- dense_mean: float32 [2, 1024, 4, 1024], P(None, 'dp', None, 'tensor'), may hold values from -0.0625 to 0.0625
- unit_mean: float32 [16, 512], P('tensor', 'dp'), may hold values from -0.0625 to 0.0625
- norm_mean: float32 [9, 1024], P(None, 'dp'), may hold values from -0.0625 to 0.0625
- attention_square: float32 [2, 4, 1024, 1024], P(None, None, 'dp', 'tensor'), as said below
- dense_square: float32 [2, 1024, 4, 1024], P(None, 'dp', None, 'tensor'), as said below
- unit_square: float32 [16, 512], P('tensor', 'dp'), as said below
- norm_square: float32 [9, 1024], P(None, 'dp'), as said below
Outputs:
- layer_out: bfloat16 [7168, 1024], P(('dp', 'tensor'))
- input_gradient: float32 [7168, 1024], P(('dp', 'tensor'))
- frame_gradient: float32 [24000, 1024], P(('dp', 'tensor'))
- attention_gradient: float32 [2, 4, 1024, 1024], P(None, None, 'dp', 'tensor')
- dense_gradient: float32 [2, 1024, 4, 1024], P(None, 'dp', None, 'tensor')
- unit_gradient: float32 [16, 512], P('tensor', 'dp')
- norm_gradient: float32 [9, 1024], P(None, 'dp')
- attention_mean_new: float32 [2, 4, 1024, 1024], P(None, None, 'dp', 'tensor')
- dense_mean_new: float32 [2, 1024, 4, 1024], P(None, 'dp', None, 'tensor')
- unit_mean_new: float32 [16, 512], P('tensor', 'dp')
- norm_mean_new: float32 [9, 1024], P(None, 'dp')
- attention_square_new: float32 [2, 4, 1024, 1024], P(None, None, 'dp', 'tensor')
- dense_square_new: float32 [2, 1024, 4, 1024], P(None, 'dp', None, 'tensor')
- unit_square_new: float32 [16, 512], P('tensor', 'dp')
- norm_square_new: float32 [9, 1024], P(None, 'dp')
- attention_step: float32 [2, 4, 1024, 1024], P(None, None, 'dp', 'tensor')
- dense_step: float32 [2, 1024, 4, 1024], P(None, 'dp', None, 'tensor')
- unit_step: float32 [16, 512], P('tensor', 'dp')
- norm_step: float32 [9, 1024], P(None, 'dp')
- weight_norms: float32 [27], replicated
- step_norms: float32 [27], replicated
Inputs may be any that keep to these rules, and one draw needn't show every extreme that they name: `frames`: independent entries of spread about one. `attention_weights`: entries are independent and normal; the output matrices have a larger spread than the others. `unit_bias`: independent entries of spread about one half. `norm_bias`: gains (rows 0, 2, 4) lie between 0.5 and 1.5; the other rows are small and of both signs. `attention_square`: Positive. `dense_square`: Positive. `unit_square`: Positive. `norm_square`: Positive.
All inputs are finite; a program needn't handle non-finite values.
Results may differ from a plain program's by a relative error of at most 0.02.
Values may be sent and summed in bfloat16 or wider, within the bound.
A program may use at most 192 MiB of HBM per device.

v0:
```python
from functools import partial

import jax
import jax.numpy as jnp
from jax import lax
from jax.sharding import PartitionSpec as P

D = 1024
HEADS = 16
HD = 64
L = 448
FRAMES = 1500
CLIPS_DP = 2


learning_rate = 0.3


def norm_forward(values, gain_row, offset):
    centre = values - jnp.mean(values, axis=-1, keepdims=True)
    spread = jnp.mean(centre * centre, axis=-1, keepdims=True)
    scaled = lax.rsqrt(spread + 1e-05)
    normed = centre * scaled
    return (normed * gain_row + offset, normed, scaled)


def norm_backward(gradient, normed, scaled, gain_row):
    inner_grad = gradient * gain_row
    result = scaled * (
        inner_grad
        - jnp.mean(inner_grad, axis=-1, keepdims=True)
        - normed * jnp.mean(inner_grad * normed, axis=-1, keepdims=True)
    )
    return (result, jnp.sum(gradient * normed, axis=0), jnp.sum(gradient, axis=0))


def gelu_value(values):
    return 0.5 * values * (1.0 + jax.scipy.special.erf(values * 0.7071067811865476))


def gelu_slope(values):
    return (
        0.5 * (1.0 + jax.scipy.special.erf(values * 0.7071067811865476))
        + values * jnp.exp(-0.5 * values * values) * 0.3989422804014327
    )


def clip_scores(queries, key_rows, causal):
    scores = (
        jnp.einsum("qhd,khd->hqk", queries, key_rows, preferred_element_type=jnp.float32) * 0.125
    )
    if causal:
        allowed = lax.broadcasted_iota(jnp.int32, scores.shape, 1) >= lax.broadcasted_iota(
            jnp.int32, scores.shape, 2
        )
        scores = jnp.where(allowed, scores, -1e30)
    return scores


def clip_forward(causal, triple):
    queries, key_rows, values = triple
    scores = clip_scores(queries, key_rows, causal)
    row_max = jnp.max(scores, axis=-1, keepdims=True)
    shifted = jnp.exp(scores - row_max)
    row_sum = jnp.sum(shifted, axis=-1, keepdims=True)
    weights = (shifted / row_sum).astype(jnp.bfloat16)
    context = jnp.einsum("hqk,khd->qhd", weights, values, preferred_element_type=jnp.float32)
    return (context.astype(jnp.bfloat16), (row_max + jnp.log(row_sum))[..., 0])


def clip_backward(causal, members):
    queries, key_rows, values, log_total, context_grad = members
    scores = clip_scores(queries, key_rows, causal)
    probs = jnp.exp(scores - log_total[..., None])
    value_grad = jnp.einsum(
        "hqk,qhd->khd", probs.astype(jnp.bfloat16), context_grad, preferred_element_type=jnp.float32
    )
    prob_grad = jnp.einsum("qhd,khd->hqk", context_grad, values, preferred_element_type=jnp.float32)
    score_grad = (probs * (prob_grad - jnp.sum(probs * prob_grad, axis=-1, keepdims=True))).astype(
        jnp.bfloat16
    )
    query_grad = (
        jnp.einsum("hqk,khd->qhd", score_grad, key_rows, preferred_element_type=jnp.float32) * 0.125
    )
    key_grad = (
        jnp.einsum("hqk,qhd->khd", score_grad, queries, preferred_element_type=jnp.float32) * 0.125
    )
    return (
        query_grad.astype(jnp.bfloat16),
        key_grad.astype(jnp.bfloat16),
        value_grad.astype(jnp.bfloat16),
    )


def adapt(weight, gradient, moment, second, token_total):
    scaled_grad = gradient / token_total
    new_moment = 0.5 * moment + 0.5 * scaled_grad
    new_second = 0.5 * second + 0.5 * scaled_grad * scaled_grad
    direction = new_moment / (jnp.sqrt(new_second) + 1e-06) + 0.01 * weight
    return (new_moment, new_second, direction)


def contract_rows(left, right):
    return lax.dot_general(
        left, right, (((0,), (0,)), ((), ())), preferred_element_type=jnp.float32
    )


def shards(
    tokens,
    frames,
    cotangent,
    attention_weights,
    dense_weights,
    unit_bias,
    norm_bias,
    attention_mean,
    dense_mean,
    unit_mean,
    norm_mean,
    attention_square,
    dense_square,
    unit_square,
    norm_square,
):
    tensor_count = lax.axis_size("tensor")
    shard_count = lax.axis_size("dp")
    head_count = HEADS // tensor_count
    head_width = D // tensor_count
    unit_cols = unit_bias.shape[1]
    column_rows = (lax.axis_index("dp") * unit_cols + jnp.arange(unit_cols, dtype=jnp.int32)) // HD
    row_pick = (column_rows[:, None] == jnp.arange(8, dtype=jnp.int32)[None, :]).astype(jnp.float32)
    leader = (lax.axis_index("tensor") == 0).astype(jnp.float32)

    def square_rows(attn_part, dense_part, unit_part, norm_part):
        unit_sums = jnp.sum(jnp.sum(unit_part * unit_part, axis=0)[:, None] * row_pick, axis=0)
        return jnp.concatenate(
            [
                jnp.sum(attn_part * attn_part, axis=(2, 3)).reshape(8),
                jnp.sum(dense_part * dense_part, axis=(1, 2, 3)),
                unit_sums,
                jnp.sum(norm_part * norm_part, axis=1) * leader,
            ]
        )

    own_attn = attention_weights.astype(jnp.float32)
    own_dense = dense_weights.astype(jnp.float32)
    own_unit = unit_bias.astype(jnp.float32)
    own_norm = norm_bias.astype(jnp.float32)
    wide_attention, wide_dense, wide_unit, wide_norm = (
        lax.all_gather(attention_weights, "dp", axis=2, tiled=True),
        lax.all_gather(dense_weights, "dp", axis=1, tiled=True),
        lax.all_gather(unit_bias, "dp", axis=1, tiled=True),
        lax.all_gather(norm_bias, "dp", axis=1, tiled=True),
    )
    up_weight = wide_dense[0].reshape(D, 4 * head_width)
    down_weight = wide_dense[1].reshape(D, 4 * head_width)
    bias_rows = (
        wide_unit.reshape(head_count, 8, HD)
        .transpose(1, 0, 2)
        .reshape(8, head_width)
        .astype(jnp.float32)
    )
    norm_rows = wide_norm.astype(jnp.float32)

    def spread_rows(local_rows, stack):

        def project(block_rows, first_row):
            return (
                block_rows,
                jnp.einsum("rd,kde->rke", block_rows, stack, preferred_element_type=jnp.float32),
            )

        return project(lax.all_gather(local_rows, "tensor", axis=0, tiled=True), jnp.int32(0))

    def collect_rows(inputs, weight):

        def partial_rows(first_row, row_count):
            return lax.dot_general(
                inputs, weight, (((1,), (1,)), ((), ())), preferred_element_type=jnp.float32
            )

        return lax.psum_scatter(
            partial_rows(jnp.int32(0), inputs.shape[0] // tensor_count * lax.axis_size("tensor")),
            "tensor",
            scatter_dimension=0,
            tiled=True,
        )

    def spread_grads(local_grad, weight):

        def project(block_rows, first_row):
            return (block_rows, jnp.dot(block_rows, weight, preferred_element_type=jnp.float32))

        return project(lax.all_gather(local_grad, "tensor", axis=0, tiled=True), jnp.int32(0))

    def collect_grads(grads_in, stack):

        def partial_rows(first_row, row_count):
            return jnp.einsum("rke,kde->rd", grads_in, stack, preferred_element_type=jnp.float32)

        return lax.psum_scatter(
            partial_rows(jnp.int32(0), grads_in.shape[0] // tensor_count * lax.axis_size("tensor")),
            "tensor",
            scatter_dimension=0,
            tiled=True,
        )

    def by_clip(flat, length):
        return flat.reshape(CLIPS_DP, length, head_count, HD)

    row_data = tokens.astype(jnp.float32)
    first_in, first_normed, first_scale = norm_forward(row_data, norm_rows[0], norm_rows[1])
    first_all, first_proj = spread_rows(first_in.astype(jnp.bfloat16), wide_attention[0, :3])
    self_query = (first_proj[:, 0] + bias_rows[0]).astype(jnp.bfloat16)
    self_keys = first_proj[:, 1].astype(jnp.bfloat16)
    self_values = (first_proj[:, 2] + bias_rows[1]).astype(jnp.bfloat16)
    self_context, self_total = lax.map(
        partial(clip_forward, True),
        (by_clip(self_query, L), by_clip(self_keys, L), by_clip(self_values, L)),
    )
    self_flat = self_context.reshape(-1, head_width)
    hidden_one = row_data + norm_rows[6] + collect_rows(self_flat, wide_attention[0, 3])
    second_in, second_normed, second_scale = norm_forward(hidden_one, norm_rows[2], norm_rows[3])
    second_all, second_proj = spread_rows(second_in.astype(jnp.bfloat16), wide_attention[1, :1])
    cross_query = (second_proj[:, 0] + bias_rows[2]).astype(jnp.bfloat16)
    block_rows = lax.all_gather(frames, "tensor", axis=0, tiled=True)
    frame_proj = jnp.einsum(
        "rd,kde->rke", block_rows, wide_attention[1, 1:3], preferred_element_type=jnp.float32
    )
    cross_keys = frame_proj[:, 0].astype(jnp.bfloat16)
    cross_values = (frame_proj[:, 1] + bias_rows[3]).astype(jnp.bfloat16)
    cross_context, cross_total = lax.map(
        partial(clip_forward, False),
        (by_clip(cross_query, L), by_clip(cross_keys, FRAMES), by_clip(cross_values, FRAMES)),
    )
    cross_flat = cross_context.reshape(-1, head_width)
    hidden_two = hidden_one + norm_rows[7] + collect_rows(cross_flat, wide_attention[1, 3])
    third_in, third_normed, third_scale = norm_forward(hidden_two, norm_rows[4], norm_rows[5])
    third_all, third_proj = spread_rows(third_in.astype(jnp.bfloat16), up_weight[None])
    before = third_proj[:, 0] + bias_rows[4:8].reshape(4 * head_width)
    activated = gelu_value(before).astype(jnp.bfloat16)
    result_rows = hidden_two + norm_rows[8] + collect_rows(activated, down_weight)
    layer_out = result_rows.astype(jnp.bfloat16)
    out_grad = cotangent.astype(jnp.float32)
    third_grad_all, act_grad = spread_grads(cotangent, down_weight)
    down_grad = contract_rows(third_grad_all, activated)
    before_grad = (act_grad * gelu_slope(before)).astype(jnp.bfloat16)
    hidden_bias_grad = jnp.sum(before_grad, axis=0, dtype=jnp.float32)
    up_grad = contract_rows(third_all, before_grad)
    dense_grads = jnp.stack([up_grad, down_grad]).reshape(2, D, 4, head_width)
    third_back = collect_grads(before_grad[:, None, :], up_weight[None])
    third_input_grad, third_gain_grad, third_offset_grad = norm_backward(
        third_back, third_normed, third_scale, norm_rows[4]
    )
    two_grad = out_grad + third_input_grad
    second_grad_all, cross_ctx_grad = spread_grads(
        two_grad.astype(jnp.bfloat16), wide_attention[1, 3]
    )
    cross_out_grad = contract_rows(second_grad_all, cross_flat)
    cross_qgrad, cross_kgrad, cross_vgrad = lax.map(
        partial(clip_backward, False),
        (
            by_clip(cross_query, L),
            by_clip(cross_keys, FRAMES),
            by_clip(cross_values, FRAMES),
            cross_total,
            by_clip(cross_ctx_grad.astype(jnp.bfloat16), L),
        ),
    )
    cross_qflat = cross_qgrad.reshape(-1, head_width)
    frame_stack = jnp.stack(
        [cross_kgrad.reshape(-1, head_width), cross_vgrad.reshape(-1, head_width)], axis=1
    )
    cross_query_grad = contract_rows(second_all, cross_qflat)
    frame_weight_grad = jnp.einsum(
        "rd,rke->kde", block_rows, frame_stack, preferred_element_type=jnp.float32
    )
    cross_grads = jnp.concatenate(
        [cross_query_grad[None], frame_weight_grad, cross_out_grad[None]], axis=0
    )
    frame_gradient = lax.psum_scatter(
        jnp.einsum(
            "rke,kde->rd", frame_stack, wide_attention[1, 1:3], preferred_element_type=jnp.float32
        ).astype(jnp.bfloat16),
        "tensor",
        scatter_dimension=0,
        tiled=True,
    ).astype(jnp.float32)
    second_back = collect_grads(cross_qflat[:, None, :], wide_attention[1, :1])
    second_input_grad, second_gain_grad, second_offset_grad = norm_backward(
        second_back, second_normed, second_scale, norm_rows[2]
    )
    one_grad = two_grad + second_input_grad
    first_grad_all, self_ctx_grad = spread_grads(
        one_grad.astype(jnp.bfloat16), wide_attention[0, 3]
    )
    self_out_grad = contract_rows(first_grad_all, self_flat)
    self_qgrad, self_kgrad, self_vgrad = lax.map(
        partial(clip_backward, True),
        (
            by_clip(self_query, L),
            by_clip(self_keys, L),
            by_clip(self_values, L),
            self_total,
            by_clip(self_ctx_grad.astype(jnp.bfloat16), L),
        ),
    )
    self_stack = jnp.stack(
        [
            self_qgrad.reshape(-1, head_width),
            self_kgrad.reshape(-1, head_width),
            self_vgrad.reshape(-1, head_width),
        ],
        axis=1,
    )
    self_weight_grad = jnp.einsum(
        "rd,rke->kde", first_all, self_stack, preferred_element_type=jnp.float32
    )
    self_grads = jnp.concatenate([self_weight_grad, self_out_grad[None]], axis=0)
    first_back = collect_grads(self_stack, wide_attention[0, :3])
    first_input_grad, first_gain_grad, first_offset_grad = norm_backward(
        first_back, first_normed, first_scale, norm_rows[0]
    )
    input_gradient = one_grad + first_input_grad
    bias_sums = jnp.stack(
        [
            jnp.sum(self_stack[:, 0], axis=0, dtype=jnp.float32),
            jnp.sum(self_stack[:, 2], axis=0, dtype=jnp.float32),
            jnp.sum(cross_qflat, axis=0, dtype=jnp.float32),
            jnp.sum(frame_stack[:, 1], axis=0, dtype=jnp.float32),
        ],
        axis=0,
    )
    unit_rows_grad = jnp.concatenate([bias_sums, hidden_bias_grad.reshape(4, head_width)], axis=0)
    unit_grads = (
        unit_rows_grad.reshape(8, head_count, HD).transpose(1, 0, 2).reshape(head_count, 8 * HD)
    )
    norm_grads = jnp.stack(
        [
            first_gain_grad,
            first_offset_grad,
            second_gain_grad,
            second_offset_grad,
            third_gain_grad,
            third_offset_grad,
            jnp.sum(one_grad, axis=0),
            jnp.sum(two_grad, axis=0),
            jnp.sum(out_grad, axis=0),
        ]
    )
    attention_owned, dense_owned, unit_owned, norm_owned = (
        lax.psum_scatter(
            jnp.stack([self_grads, cross_grads]), "dp", scatter_dimension=2, tiled=True
        ),
        lax.psum_scatter(dense_grads, "dp", scatter_dimension=1, tiled=True),
        lax.psum_scatter(unit_grads, "dp", scatter_dimension=1, tiled=True),
        lax.psum_scatter(norm_grads, "dp", scatter_dimension=1, tiled=True),
    )
    norm_owned = lax.psum(norm_owned, "tensor")
    token_total = float(tokens.shape[0] * shard_count * tensor_count)
    attn_moment, attn_second, attn_dir = adapt(
        own_attn, attention_owned, attention_mean, attention_square, token_total
    )
    dense_moment, dense_second, dense_dir = adapt(
        own_dense, dense_owned, dense_mean, dense_square, token_total
    )
    unit_moment, unit_second, unit_dir = adapt(
        own_unit, unit_owned, unit_mean, unit_square, token_total
    )
    norm_moment, norm_second, norm_dir = adapt(
        own_norm, norm_owned, norm_mean, norm_square, token_total
    )
    weight_sums, step_sums = lax.psum(
        (
            square_rows(own_attn, own_dense, own_unit, own_norm),
            square_rows(attn_dir, dense_dir, unit_dir, norm_dir),
        ),
        ("dp", "tensor"),
    )
    weight_norms = jnp.sqrt(weight_sums)
    step_norms = jnp.sqrt(step_sums)
    trust = weight_norms / step_norms
    attention_step = -learning_rate * trust[0:8].reshape(2, 4, 1, 1) * attn_dir
    dense_step = -learning_rate * trust[8:10].reshape(2, 1, 1, 1) * dense_dir
    unit_factor = jnp.sum(row_pick * trust[10:18][None, :], axis=1)
    unit_step = -learning_rate * unit_factor[None, :] * unit_dir
    norm_step = -learning_rate * trust[18:27][:, None] * norm_dir
    return (
        layer_out,
        input_gradient,
        frame_gradient,
        attention_owned,
        dense_owned,
        unit_owned,
        norm_owned,
        attn_moment,
        dense_moment,
        unit_moment,
        norm_moment,
        attn_second,
        dense_second,
        unit_second,
        norm_second,
        attention_step,
        dense_step,
        unit_step,
        norm_step,
        weight_norms,
        step_norms,
    )


def solution(mesh):
    in_specs = (
        P(("dp", "tensor"), None),
        P(("dp", "tensor"), None),
        P(("dp", "tensor"), None),
        P(None, None, "dp", "tensor"),
        P(None, "dp", None, "tensor"),
        P("tensor", "dp"),
        P(None, "dp"),
        P(None, None, "dp", "tensor"),
        P(None, "dp", None, "tensor"),
        P("tensor", "dp"),
        P(None, "dp"),
        P(None, None, "dp", "tensor"),
        P(None, "dp", None, "tensor"),
        P("tensor", "dp"),
        P(None, "dp"),
    )
    out_specs = (
        P(("dp", "tensor"), None),
        P(("dp", "tensor"), None),
        P(("dp", "tensor"), None),
        P(None, None, "dp", "tensor"),
        P(None, "dp", None, "tensor"),
        P("tensor", "dp"),
        P(None, "dp"),
        P(None, None, "dp", "tensor"),
        P(None, "dp", None, "tensor"),
        P("tensor", "dp"),
        P(None, "dp"),
        P(None, None, "dp", "tensor"),
        P(None, "dp", None, "tensor"),
        P("tensor", "dp"),
        P(None, "dp"),
        P(None, None, "dp", "tensor"),
        P(None, "dp", None, "tensor"),
        P("tensor", "dp"),
        P(None, "dp"),
        P(),
        P(),
    )
    return jax.shard_map(shards, mesh=mesh, in_specs=in_specs, out_specs=out_specs, check_vma=False)
```

profile of v0, /device:TPU:0, one launch (start us, length us, event | category | flops | bytes accessed | tf_op | source)
XLA Modules:
  0.0 1260.9 jit_solution(15986176522912490597)
XLA Ops:
  7.2 28.0 %all_gather.33 = bf16[9,1024]{1,0:T(8,128)(2,1)S(1)} all-gather(bf16[9,128]{1,0:T(8,128)(2,1)} %param.29), channel_id=1, replica_groups=mesh['dp'=8,'tensor'=4] {'dp'}, dimensions={1}, use_global_device_ids=true | all-gather | bytes 20736 | tf_op jit(solution)/shard_map/all_gather | solution.py:154
  41.9 19.0 %all-gather = bf16[8,64,4]{1,2,0:T(4,128)(2,1)S(1)} all-gather(bf16[1,64,4]{1,2,0:T(4,128)(2,1)} %bitcast.411), channel_id=1, replica_groups=mesh['dp'=8,'tensor'=4] {'dp'}, dimensions={0}, use_global_device_ids=true | all-gather | bytes 4608 | tf_op jit(solution)/shard_map/all_gather | solution.py:153
  61.5 75.0 %all-gather.14.cloned.1.call-done = bf16[2,4,1024,256]{3,2,1,0:T(8,128)(2,1)} async-done(((bf16[2,4,128,256]{3,2,1,0:T(8,128)(2,1)}), bf16[2,4,1024,256]{3,2,1,0:T(8,128)(2,1)}) %all-gather.14.cloned.1.call-update) | async-done | bytes 4194320 | tf_op jit(solution)/shard_map/all_gather | solution.py:151
  147.3 4.1 while.52
  157.4 39.3 %reduce-scatter.18.cloned.1.call-done = f32[224,1024]{1,0:T(8,128)} async-done(((f32[896,1024]{1,0:T(8,128)}), f32[224,1024]{1,0:T(8,128)}) %reduce-scatter.18.cloned.1.call-update) | async-done | bytes 917520 | tf_op jit(solution)/shard_map/reduce_scatter | solution.py:183
  201.8 42.0 %all-gather.28.cloned.1.call-done = bf16[4,750,1024]{2,1,0:T(8,128)(2,1)} async-done(((bf16[1,750,1024]{2,1,0:T(8,128)(2,1)}), bf16[4,750,1024]{2,1,0:T(8,128)(2,1)}) %all-gather.28.cloned.1.call-update) | async-done | bytes 6144016 | tf_op jit(solution)/shard_map/all_gather | solution.py:227
  243.8 6.9 reshape.345
  250.7 5.9 fusion.132
  262.2 6.1 squeeze.85
  275.5 4.2 copy.294
  282.9 23.6 %while.53 = (s32[]{:T(128)}, bf16[2,448,4,64]{1,3,2,0:T(8,128)(2,1)}, f32[2,4,448]{2,1,0:T(4,128)S(1)}, bf16[2,1500,4,64]{1,3,2,0:T(8,128)(2,1)}, bf16[2,448,4,6...) while((s32[]{:T(128)}, bf16[2,448,4,64]{1,3,2,0:T(8,128)(2,1)}, ...), condition=%wide.region_12.13_spmd, body=%wide.region_9.12_spmd.sunk | while | flops 712432896 | bytes 40819820 | solution.py:233
  286.7 3.8 fusion.243
  294.3 3.8 fusion.243
  315.0 40.5 %reduce-scatter.20.cloned.1.call-done = f32[224,1024]{1,0:T(8,128)} async-done(((f32[896,1024]{1,0:T(8,128)}), f32[224,1024]{1,0:T(8,128)}) %reduce-scatter.20.cloned.1.call-update) | async-done | bytes 917520 | tf_op jit(solution)/shard_map/reduce_scatter | solution.py:183
  359.7 70.8 %all-gather.20.cloned.1.call-done = bf16[2,1024,4,256]{3,2,1,0:T(4,128)(2,1)} async-done(((bf16[2,128,4,256]{3,2,1,0:T(4,128)(2,1)}), bf16[2,1024,4,256]{3,2,1,0:T(4,128)(2,1)}) %all-gather.20.cloned.1.call-update) | async-done | bytes 4194320 | tf_op jit(solution)/shard_map/all_gather | solution.py:152
  437.2 15.1 %all-gather.18.cloned.1.call-done = bf16[896,1024]{1,0:T(8,128)(2,1)} async-done(((bf16[224,1024]{1,0:T(8,128)(2,1)}), bf16[896,1024]{1,0:T(8,128)(2,1)}) %all-gather.18.cloned.1.call-update) | async-done | bytes 1835024 | tf_op jit(solution)/shard_map/all_gather | solution.py:174
  452.3 6.8 multiply_convert_fusion.2
  459.0 15.9 %all-gather.22.cloned.1.call-done = bf16[896,1024]{1,0:T(8,128)(2,1)} async-done(((bf16[224,1024]{1,0:T(8,128)(2,1)}), bf16[896,1024]{1,0:T(8,128)(2,1)}) %all-gather.22.cloned.1.call-update) | async-done | bytes 1835024 | tf_op jit(solution)/shard_map/all_gather | solution.py:195
  475.0 6.5 convert_reduce_fusion
  482.7 3.9 fusion.167
  486.7 6.1 fusion.166
  492.9 35.2 %reduce-scatter.24.cloned.1.call-done = f32[224,1024]{1,0:T(8,128)} async-done(((f32[896,1024]{1,0:T(8,128)}), f32[224,1024]{1,0:T(8,128)}) %reduce-scatter.24.cloned.1.call-update) | async-done | bytes 917520 | tf_op jit(solution)/shard_map/reduce_scatter | solution.py:202
  530.3 41.5 %reduce-scatter.22.cloned.1.call-done = f32[224,1024]{1,0:T(8,128)} async-done(((f32[896,1024]{1,0:T(8,128)}), f32[224,1024]{1,0:T(8,128)}) %reduce-scatter.22.cloned.1.call-update) | async-done | bytes 917520 | tf_op jit(solution)/shard_map/reduce_scatter | solution.py:183
  577.2 21.0 %all-gather.24.cloned.1.call-done = bf16[896,1024]{1,0:T(8,128)(2,1)} async-done(((bf16[224,1024]{1,0:T(8,128)(2,1)}), bf16[896,1024]{1,0:T(8,128)(2,1)}) %all-gather.24.cloned.1.call-update) | async-done | bytes 1835024 | tf_op jit(solution)/shard_map/all_gather | solution.py:195
  603.3 29.8 %while.54 = (s32[]{:T(128)}, bf16[2,448,4,64]{1,3,2,0:T(8,128)(2,1)S(1)}, bf16[2,1500,4,64]{1,3,2,0:T(8,128)(2,1)}, bf16[2,1500,4,64]{1,3,2,0:T(8,128)(2,1)}, bf...) while((s32[]{:T(128)}, ...), condition=%wide.region_22.23_spmd, body=%wide.region_20.22_spmd.sunk | while | flops 1753955584 | bytes 108816640 | solution.py:261
  638.5 41.3 %reduce-scatter.26.cloned.1.call-done = f32[224,1024]{1,0:T(8,128)} async-done(((f32[896,1024]{1,0:T(8,128)}), f32[224,1024]{1,0:T(8,128)}) %reduce-scatter.26.cloned.1.call-update) | async-done | bytes 917520 | tf_op jit(solution)/shard_map/reduce_scatter | solution.py:202
  685.4 20.8 %all-gather.26.cloned.1.call-done = bf16[896,1024]{1,0:T(8,128)(2,1)} async-done(((bf16[224,1024]{1,0:T(8,128)(2,1)}), bf16[896,1024]{1,0:T(8,128)(2,1)}) %all-gather.26.cloned.1.call-update) | async-done | bytes 1835024 | tf_op jit(solution)/shard_map/all_gather | solution.py:195
  710.3 10.1 while.55
  726.6 5.2 convolution_bitcast_fusion
  733.3 5.9 fusion.168
  739.2 5.8 copy.321
  745.0 5.9 fusion.169
  750.9 5.3 copy.322
  756.2 7.6 copy_bitcast_fusion
  763.7 10.8 reshape.358
  775.3 5.1 copy.347
  783.3 5.2 copy.348
  817.5 8.6 pad_maximum_fusion
  828.0 6.5 bitcast_convert_fusion
  834.5 56.7 %fusion = bf16[752,1024]{1,0:T(8,128)(2,1)S(1)} fusion(bf16[3000,1024]{1,0:T(8,128)(2,1)} %bitcast_convert_fusion), kind=kCustom, calls=%all-reduce-scatter | all-reduce-scatter fusion | flops 3080193 | bytes 7684608
  905.9 18.3 %reduce-scatter.34.cloned.1.call-done = f32[128,2048]{1,0:T(8,128)} async-done(((f32[1024,2048]{1,0:T(8,128)}), f32[128,2048]{1,0:T(8,128)}) %reduce-scatter.34.cloned.1.call-update) | async-done | bytes 1048592
  927.2 5.3 multiply_reduce_fusion.3
  932.5 56.7 %reduce-scatter.36.cloned.1.call-done = f32[64,4]{1,0:T(8,128)} async-done(((f32[512,4]{1,0:T(8,128)}), f32[64,4]{1,0:T(8,128)}) %reduce-scatter.36.cloned.1.call-update) | async-done | bytes 1040
  991.5 54.5 %reduce-scatter.32.cloned.1.call-done = f32[9,128]{1,0:T(8,128)} async-done(((f32[9,1024]{1,0:T(8,128)}), f32[9,128]{1,0:T(8,128)}) %reduce-scatter.32.cloned.1.call-update) | async-done | bytes 4624 | tf_op jit(solution)/shard_map/reduce_scatter | solution.py:358
  1046.0 5.9 psum.21
  1052.7 143.9 %reduce-scatter.30.cloned.1.call-done = f32[2,4,128,256]{2,3,1,0:T(8,128)} async-done(((f32[2,4,1024,256]{2,3,1,0:T(8,128)}), f32[2,4,128,256]{2,3,1,0:T(8,128)}) %reduce-scatter.30.cloned.1.call-update) | async-done | bytes 1048592 | tf_op jit(solution)/shard_map/reduce_scatter | solution.py:353
  1196.5 4.2 multiply_reduce_fusion.4
  1203.5 39.3 %all-reduce.2 = (f32[27]{0:T(128)S(1)}, f32[27]{0:T(128)S(1)}) all-reduce(f32[27]{0:T(128)S(1)} %pad_maximum_fusion.2, f32[27]{0:T(128)S(1)} %pad_maximum_fusion.3), channel_id=1, replica_groups=mesh['dp'=8,'tensor'=4] {'dp','tensor'}, use_global_device_ids=true, to_apply=%region_57.58 | all-reduce | flops 54 | bytes 432 | tf_op jit(solution)/shard_map/psum | solution.py:374
  (442 shorter events, 219.7 us)
Async XLA Ops:
  7.2 54.4 %all-gather.12.cloned.1.call-start = ((), (), s32[]{:S(2)}) async-start(), calls=%async_computation.10 | async-start | bytes 2293760 | tf_op jit(solution)/shard_map/all_gather | solution.py:174
  35.9 162.5 %copy-start.56 = (f32[1,1024]{1,0:T(1,128)}, f32[1,1024]{1,0:T(1,128)S(1)}, u32[]{:S(2)}) copy-start(f32[1,1024]{1,0:T(1,128)S(1)} %get-tuple-element.625) | copy-start | bytes 12292
  41.1 95.4 %all-gather.14.cloned.1.call-start = ((), (), s32[]{:S(2)}) async-start(), calls=%async_computation.11 | async-start | bytes 4718592 | tf_op jit(solution)/shard_map/all_gather | solution.py:151
  41.9 154.9 %reduce-scatter.18.cloned.1.call-start = ((), (), s32[]{:S(2)}) async-start(), calls=%async_computation.12 | async-start | bytes 4587520 | tf_op jit(solution)/shard_map/reduce_scatter | solution.py:183
  61.1 75.4 %copy-start.54 = (f32[4,8,64]{2,1,0:T(8,128)}, f32[4,8,64]{2,1,0:T(8,128)S(1)}, u32[]{:S(2)}) copy-start(f32[4,8,64]{2,1,0:T(8,128)S(1)} %reshape.338) | copy-start | bytes 24580
  156.8 87.0 %all-gather.28.cloned.1.call-start = ((), (), s32[]{:S(2)}) async-start(), calls=%async_computation.26 | async-start | bytes 7700480 | tf_op jit(solution)/shard_map/all_gather | solution.py:227
  157.4 122.4 %all-gather.16.cloned.1.call-start = ((), (), s32[]{:S(2)}) async-start(), calls=%async_computation.13 | async-start | bytes 2293760 | tf_op jit(solution)/shard_map/all_gather | solution.py:174
  198.1 157.4 %copy-start = (f32[224,1024]{1,0:T(8,128)}, f32[224,1024]{1,0:T(8,128)S(1)}, u32[]{:S(2)}) copy-start(f32[224,1024]{1,0:T(8,128)S(1)} %get-tuple-element.604) | copy-start | bytes 2752516
  198.1 52.6 %copy-start.63 = (f32[224]{0:T(256)}, f32[224]{0:T(256)S(1)}, u32[]{:S(2)}) copy-start(f32[224]{0:T(256)S(1)} %broadcast_multiply_fusion.11) | copy-start | bytes 2692
  198.4 52.3 %copy-start.68 = (f32[224]{0:T(256)}, f32[224]{0:T(256)S(1)}, u32[]{:S(2)}) copy-start(f32[224]{0:T(256)S(1)} %add_rsqrt_fusion.1) | copy-start | bytes 2692
  199.4 156.0 %reduce-scatter.20.cloned.1.call-start = ((), (), s32[]{:S(2)}) async-start(), calls=%async_computation.14 | async-start | bytes 4587520 | tf_op jit(solution)/shard_map/reduce_scatter | solution.py:183
  310.4 45.0 %copy-start.73 = (f32[1,1024]{1,0:T(1,128)S(1)}, f32[1,1024]{1,0:T(1,128)}, u32[]{:S(2)}) copy-start(f32[1,1024]{1,0:T(1,128)} %get-tuple-element.624) | copy-start | bytes 12292
  314.1 45.4 %copy-start.55 = (f32[4,8,64]{2,1,0:T(8,128)S(1)}, f32[4,8,64]{2,1,0:T(8,128)}, u32[]{:S(2)}) copy-start(f32[4,8,64]{2,1,0:T(8,128)} %copy-done.54) | copy-start | bytes 24580
  314.2 116.3 %all-gather.20.cloned.1.call-start = ((), (), s32[]{:S(2)}) async-start(), calls=%async_computation.16 | async-start | bytes 4718592 | tf_op jit(solution)/shard_map/all_gather | solution.py:152
  314.9 137.4 %all-gather.18.cloned.1.call-start = ((), (), s32[]{:S(2)}) async-start(), calls=%async_computation.15 | async-start | bytes 2293760 | tf_op jit(solution)/shard_map/all_gather | solution.py:174
  358.8 116.2 %all-gather.22.cloned.1.call-start = ((), (), s32[]{:S(2)}) async-start(), calls=%async_computation.18 | async-start | bytes 2293760 | tf_op jit(solution)/shard_map/all_gather | solution.py:195
  359.5 168.5 %reduce-scatter.24.cloned.1.call-start = ((), (), s32[]{:S(2)}) async-start(), calls=%async_computation.19 | async-start | bytes 4587520 | tf_op jit(solution)/shard_map/reduce_scatter | solution.py:202
  486.7 85.2 %reduce-scatter.22.cloned.1.call-start = ((), (), s32[]{:S(2)}) async-start(), calls=%async_computation.17 | async-start | bytes 4587520 | tf_op jit(solution)/shard_map/reduce_scatter | solution.py:183
  492.8 79.0 %copy-start.44 = (bf16[224,1024]{1,0:T(8,128)(2,1)S(1)}, bf16[224,1024]{1,0:T(8,128)(2,1)}, u32[]{:S(2)}) copy-start(bf16[224,1024]{1,0:T(8,128)(2,1)} %param.25) | copy-start | bytes 1376260
  492.8 79.0 %copy-start.75 = (f32[1,1024]{1,0:T(1,128)S(1)}, f32[1,1024]{1,0:T(1,128)}, u32[]{:S(2)}) copy-start(f32[1,1024]{1,0:T(1,128)} %get-tuple-element.621) | copy-start | bytes 12292
  492.8 105.4 %all-gather.24.cloned.1.call-start = ((), (), s32[]{:S(2)}) async-start(), calls=%async_computation.20 | async-start | bytes 2293760 | tf_op jit(solution)/shard_map/all_gather | solution.py:195
  577.0 102.9 %reduce-scatter.26.cloned.1.call-start = ((), (), s32[]{:S(2)}) async-start(), calls=%async_computation.21 | async-start | bytes 4587520 | tf_op jit(solution)/shard_map/reduce_scatter | solution.py:202
  634.8 45.0 %copy-start.69 = (f32[224]{0:T(256)S(1)}, f32[224]{0:T(256)}, u32[]{:S(2)}) copy-start(f32[224]{0:T(256)} %copy-done.68) | copy-start | bytes 2692
  638.5 67.6 %all-gather.26.cloned.1.call-start = ((), (), s32[]{:S(2)}) async-start(), calls=%async_computation.22 | async-start | bytes 2293760 | tf_op jit(solution)/shard_map/all_gather | solution.py:195
  684.9 129.0 %reduce-scatter.28.cloned.1.call-start = ((), (), s32[]{:S(2)}) async-start(), calls=%async_computation.23 | async-start | bytes 4587520 | tf_op jit(solution)/shard_map/reduce_scatter | solution.py:202
  731.8 192.4 %reduce-scatter.34.cloned.1.call-start = ((), (), s32[]{:S(2)}) async-start(), calls=%async_computation.27 | async-start | bytes 9437184
  774.6 214.6 %reduce-scatter.36.cloned.1.call-start = ((), (), s32[]{:S(2)}) async-start(), calls=%async_computation.28 | async-start | bytes 294912
  806.8 239.2 %reduce-scatter.32.cloned.1.call-start = ((), (), s32[]{:S(2)}) async-start(), calls=%async_computation.25 | async-start | bytes 73728 | tf_op jit(solution)/shard_map/reduce_scatter | solution.py:358
  817.5 379.1 %reduce-scatter.30.cloned.1.call-start = ((), (), s32[]{:S(2)}) async-start(), calls=%async_computation.24 | async-start | bytes 9437184 | tf_op jit(solution)/shard_map/reduce_scatter | solution.py:353
  834.5 59.1 %copy-start.38 = (bf16[2,4,128,256]{3,2,1,0:T(8,128)(2,1)S(1)}, bf16[2,4,128,256]{3,2,1,0:T(8,128)(2,1)}, u32[]{:S(2)}) copy-start(bf16[2,4,128,256]{3,2,1,0:T(8,128)(2,1)} %param.26) | copy-start | bytes 1572868
  891.2 9.7 collective-permute-start
  927.1 62.9 %copy-start.81 = (bf16[4,64]{1,0:T(4,128)(2,1)S(1)}, bf16[4,64]{1,0:T(4,128)(2,1)}, u32[]{:S(2)}) copy-start(bf16[4,64]{1,0:T(4,128)(2,1)} %param.28) | copy-start | bytes 1540
  927.1 62.9 %copy-start.85 = (f32[4,64]{1,0:T(4,128)S(1)}, f32[4,64]{1,0:T(4,128)}, u32[]{:S(2)}) copy-start(f32[4,64]{1,0:T(4,128)} %param.36) | copy-start | bytes 3076
  927.1 62.9 %copy-start.86 = (f32[4,64]{1,0:T(4,128)S(1)}, f32[4,64]{1,0:T(4,128)}, u32[]{:S(2)}) copy-start(f32[4,64]{1,0:T(4,128)} %param.32) | copy-start | bytes 3076
  927.1 64.3 %copy-start.84 = (f32[224]{0:T(256)S(1)}, f32[224]{0:T(256)}, u32[]{:S(2)}) copy-start(f32[224]{0:T(256)} %get-tuple-element.506) | copy-start | bytes 2692
  927.1 64.3 %copy-start.83 = (f32[224]{0:T(256)S(1)}, f32[224]{0:T(256)}, u32[]{:S(2)}) copy-start(f32[224]{0:T(256)} %get-tuple-element.507) | copy-start | bytes 2692
  927.1 124.7 %copy-start.74 = (bf16[9,128]{1,0:T(8,128)(2,1)S(1)}, bf16[9,128]{1,0:T(8,128)(2,1)}, u32[]{:S(2)}) copy-start(bf16[9,128]{1,0:T(8,128)(2,1)} %param.29) | copy-start | bytes 6916
  927.2 124.7 %copy-start.79 = (f32[9,128]{1,0:T(8,128)S(1)}, f32[9,128]{1,0:T(8,128)}, u32[]{:S(2)}) copy-start(f32[9,128]{1,0:T(8,128)} %param.37) | copy-start | bytes 13828
  927.2 124.7 %copy-start.80 = (f32[9,128]{1,0:T(8,128)S(1)}, f32[9,128]{1,0:T(8,128)}, u32[]{:S(2)}) copy-start(f32[9,128]{1,0:T(8,128)} %param.33) | copy-start | bytes 13828
  927.2 269.4 %copy-start.28 = (f32[2,4,128,256]{2,3,1,0:T(8,128)S(1)}, f32[2,4,128,256]{2,3,1,0:T(8,128)}, u32[]{:S(2)}) copy-start(f32[2,4,128,256]{2,3,1,0:T(8,128)} %copy.324) | copy-start | bytes 3145732
  932.5 268.5 %copy-start.15 = (f32[224,1024]{1,0:T(8,128)S(1)}, f32[224,1024]{1,0:T(8,128)}, u32[]{:S(2)}) copy-start(f32[224,1024]{1,0:T(8,128)} %copy-done.14) | copy-start | bytes 2752516
  932.5 268.5 %copy-start.53 = (f32[1,1024]{1,0:T(1,128)S(1)}, f32[1,1024]{1,0:T(1,128)}, u32[]{:S(2)}) copy-start(f32[1,1024]{1,0:T(1,128)} %copy-done.51) | copy-start | bytes 12292
  932.5 268.5 %copy-start.62 = (f32[224]{0:T(256)S(1)}, f32[224]{0:T(256)}, u32[]{:S(2)}) copy-start(f32[224]{0:T(256)} %copy-done.60) | copy-start | bytes 2692
  932.5 268.5 %copy-start.67 = (f32[224]{0:T(256)S(1)}, f32[224]{0:T(256)}, u32[]{:S(2)}) copy-start(f32[224]{0:T(256)} %copy-done.65) | copy-start | bytes 2692
  990.0 213.5 %copy-start.78 = (f32[4,64]{1,0:T(4,128)}, f32[4,64]{1,0:T(4,128)S(1)}, u32[]{:S(2)}) copy-start(f32[4,64]{1,0:T(4,128)S(1)} %copy.352) | copy-start | bytes 3076
  1051.9 151.6 %copy-start.59 = (f32[9,128]{1,0:T(8,128)}, f32[9,128]{1,0:T(8,128)S(1)}, u32[]{:S(2)}) copy-start(f32[9,128]{1,0:T(8,128)S(1)} %psum.21) | copy-start | bytes 13828
  1052.7 190.9 %copy-start.88 = (s32[64]{0:T(128)S(1)}, s32[64]{0:T(128)}, u32[]{:S(2)}) copy-start(s32[64]{0:T(128)} %and_select_fusion) | copy-start | bytes 772
  1203.5 45.6 %copy-start.29 = (f32[2,4,128,256]{2,3,1,0:T(8,128)S(1)}, f32[2,4,128,256]{2,3,1,0:T(8,128)}, u32[]{:S(2)}) copy-start(f32[2,4,128,256]{2,3,1,0:T(8,128)} %get-tuple-element.582) | copy-start | bytes 3145732
  (74 other events, 642.2 us)
Sparse Core Ops, SparseCore 0:
  41.2 20.2 all-gather.11
  63.7 72.7 all-gather.13
  156.9 39.7 reduce-scatter.17
  198.1 45.5 all-gather.27
  245.8 21.0 all-gather.15
  314.3 41.1 reduce-scatter.19
  357.6 72.7 all-gather.19
  432.6 19.6 all-gather.17
  453.8 21.0 all-gather.21
  486.8 41.2 reduce-scatter.23
  530.6 41.2 reduce-scatter.21
  577.1 21.0 all-gather.23
  638.6 41.2 reduce-scatter.25
  685.0 21.0 all-gather.25
  732.0 41.2 reduce-scatter.27
  776.7 147.4 reduce-scatter.33
  928.0 61.1 reduce-scatter.35
  992.2 53.7 reduce-scatter.31
  1049.6 146.8 reduce-scatter.29
where the time goes:
time: 1270 us; the launch traced here: 1260 us
  waiting for transfers between devices  735 us (58%)
  blocking collectives  149 us (12%)
  local copies, waits for them, and re-layouts  132 us (10%)
  matrix products  131 us (10%)
  other arithmetic  85.1 us (7%)
  between operations  16.2 us (1%)
    reduce_scatter x1, waiting for transfers between devices, shards(): lax.psum_scatter(jnp.stack([self_grads, cross_grads]), 'dp', scatter_dime...  144 us
    reduce_scatter x3, waiting for transfers between devices, collect_rows(): lax.psum_scatter(partial_rows(jnp.int32(0), inputs.shape[0] // tensor_cou...  121 us
    unnamed x22, waiting for transfers between devices  77.9 us
    reduce_scatter x3, waiting for transfers between devices, collect_grads(): lax.psum_scatter(partial_rows(jnp.int32(0), grads_in.shape[0] // tensor_c...  76.5 us
    all_gather x1, waiting for transfers between devices, shards(): lax.all_gather(attention_weights, 'dp', axis=2, tiled=True)  75 us
    all_gather x1, waiting for transfers between devices, shards(): lax.all_gather(dense_weights, 'dp', axis=1, tiled=True)  70.8 us
    all_gather x3, waiting for transfers between devices, spread_grads(): lax.all_gather(local_grad, 'tensor', axis=0, tiled=True)  57.7 us
    unnamed x1, blocking collectives  56.7 us
  transfers between devices with their start and end apart: 20, of which 17 were waited for; matrix products, arithmetic and copies ran while one was open for 19% of the time, Pallas kernels for 0%

commit v1 on v0

v1 whole, which is shorter than its diff:
```python
from functools import partial

import jax
import jax.numpy as jnp
from jax import lax
from jax.experimental import pallas as pl
from jax.experimental.pallas import tpu as pltpu
from jax.sharding import Mesh, PartitionSpec as P

D = 1024
HEADS = 16
HD = 64
L = 448
FRAMES = 1500
MATS = 16
COLS = 256

learning_rate = 0.3
DT = pl.DeviceIdType.MESH
AXES = ("dp", "side", "core")


def place():
    dp = lax.axis_index("dp")
    return dp // 2, lax.rem(dp, 2), lax.axis_index("side"), lax.axis_index("core")


def device(z, y, x, c):
    return (z * 2 + y, x, c)


def greet_neighbours(levels):
    z, y, x, c = place()
    bar = pltpu.get_barrier_semaphore()
    pl.semaphore_signal(bar, inc=1, device_id=device(z, y, 1 - x, c), device_id_type=DT)
    pl.semaphore_signal(bar, inc=1, device_id=device(z, 1 - y, x, c), device_id_type=DT)

    @pl.when(z > 0)
    def _():
        pl.semaphore_signal(bar, inc=1, device_id=device(z - 1, y, x, c), device_id_type=DT)

    @pl.when(z < levels - 1)
    def _():
        pl.semaphore_signal(bar, inc=1, device_id=device(z + 1, y, x, c), device_id_type=DT)

    pl.semaphore_wait(
        bar, 2 + jnp.where(z > 0, 1, 0) + jnp.where(z < levels - 1, 1, 0)
    )


def gather_kernel(levels, groups, shard, wide, own_sem, z_send, z_recv, x_send, x_recv, y_send, y_recv):
    z, y, x, c = place()
    size = MATS // groups
    greet_neighbours(levels)
    local = pltpu.make_async_copy(shard, wide.at[:, x, z, y], own_sem)
    local.start()

    def block(g, xx, zz, yy):
        return wide.at[pl.ds(g * size, size), xx, zz, yy]

    def source(g, zz, own):
        return shard.at[pl.ds(g * size, size)] if own else block(g, x, zz, y)

    def z_copy(g, zz, target, own):
        return pltpu.make_async_remote_copy(
            source(g, zz, own), block(g, x, zz, y), z_send.at[g, zz, jnp.where(target > z, 1, 0)],
            z_recv.at[g, zz], device_id=device(target, y, x, c), device_id_type=DT,
        )

    def x_copy(g, zz, yy, own):
        src = source(g, zz, True) if own else block(g, x, zz, yy)
        return pltpu.make_async_remote_copy(
            src, block(g, x, zz, yy), x_send.at[g, zz, yy], x_recv.at[g, zz, yy],
            device_id=device(z, y, 1 - x, c), device_id_type=DT,
        )

    def y_copy(g, zz, xx, own):
        src = source(g, zz, True) if own else block(g, xx, zz, y)
        return pltpu.make_async_remote_copy(
            src, block(g, xx, zz, y), y_send.at[g, zz, xx], y_recv.at[g, zz, xx],
            device_id=device(z, 1 - y, x, c), device_id_type=DT,
        )

    def spread(g, zz, own):
        if g % 2 == 0:
            x_copy(g, zz, y, own).start()
            y_copy(g, zz, x, own).start()
        else:
            y_copy(g, zz, x, own).start()
            x_copy(g, zz, y, own).start()

    def first(g):
        @pl.when(z < levels - 1)
        def _():
            z_copy(g, z, z + 1, True).start()

        @pl.when(z > 0)
        def _():
            z_copy(g, z, z - 1, True).start()

        spread(g, z, True)
        for d in range(1, levels):
            @pl.when(z - d >= 0)
            def _():
                z_copy(g, z - d, z - 1, False).wait_recv()

                @pl.when(z < levels - 1)
                def _():
                    z_copy(g, z - d, z + 1, False).start()

                spread(g, z - d, False)

            @pl.when(z + d < levels)
            def _():
                z_copy(g, z + d, z + 1, False).wait_recv()

                @pl.when(z > 0)
                def _():
                    z_copy(g, z + d, z - 1, False).start()

                spread(g, z + d, False)

    def order(body):
        def run(d, carry):
            @pl.when(z - d >= 0)
            def _():
                body(z - d)

            if True:
                @pl.when((z + d < levels) & (d > 0))
                def _():
                    body(z + d)

            return carry

        lax.fori_loop(0, levels, run, 0)

    def second(g):
        def relay(zz):
            if g % 2 == 0:
                x_copy(g, zz, y, False).wait_recv()
                y_copy(g, zz, 1 - x, False).start()
            else:
                y_copy(g, zz, x, False).wait_recv()
                x_copy(g, zz, 1 - y, False).start()

        order(relay)

    def third(g):
        def finish(zz):
            if g % 2 == 0:
                y_copy(g, zz, x, False).wait_recv()
                y_copy(g, zz, 1 - x, False).wait_recv()
            else:
                x_copy(g, zz, y, False).wait_recv()
                x_copy(g, zz, 1 - y, False).wait_recv()

        order(finish)

    def drain(g):
        def sent(zz):
            if g % 2 == 0:
                x_copy(g, zz, y, False).wait_send()
                y_copy(g, zz, x, False).wait_send()
                y_copy(g, zz, 1 - x, False).wait_send()
            else:
                y_copy(g, zz, x, False).wait_send()
                x_copy(g, zz, y, False).wait_send()
                x_copy(g, zz, 1 - y, False).wait_send()

            @pl.when((z < levels - 1) & (zz <= z))
            def _():
                z_copy(g, zz, z + 1, False).wait_send()

            @pl.when((z > 0) & (zz >= z))
            def _():
                z_copy(g, zz, z - 1, False).wait_send()

        order(sent)

    for step in range(groups + 1):
        if step < groups:
            first(step)
        if step >= 1:
            second(step - 1)
    for g in range(groups):
        third(g)
        drain(g)
    local.wait()


def gather_weights(shard, shards):
    rows = shard.shape[1]
    levels = shards // 2
    groups = 8 if levels <= 4 else 2
    sem = pltpu.SemaphoreType.DMA
    wide = pl.pallas_call(
        partial(gather_kernel, levels, groups),
        out_shape=jax.ShapeDtypeStruct((MATS, 2, levels, 2, rows, COLS), jnp.bfloat16),
        in_specs=[pl.BlockSpec(memory_space=pltpu.VMEM)],
        out_specs=pl.BlockSpec(memory_space=pl.ANY),
        scratch_shapes=[
            sem, sem((groups, levels, 2)), sem((groups, levels)), sem((groups, levels, 2)),
            sem((groups, levels, 2)), sem((groups, levels, 2)), sem((groups, levels, 2)),
        ],
        compiler_params=pltpu.CompilerParams(collective_id=0, has_side_effects=True),
        name="gather_weights",
    )(shard)
    return wide.reshape(MATS, 2, D, COLS)


def scatter_kernel(levels, groups, part, out, even, odd, two, line, s1, r1, s2, r2, s3, r3):
    z, y, x, c = place()
    size = MATS // groups
    greet_neighbours(levels)

    def span(g):
        return pl.ds(g * size, size)

    def first(g):
        if g % 2 == 0:
            src, dev = part.at[span(g), :, :, 1 - y], device(z, 1 - y, x, c)
        else:
            src, dev = part.at[span(g), 1 - x, :, :], device(z, y, 1 - x, c)
        return pltpu.make_async_remote_copy(
            src, (odd if g % 2 else even).at[g // 2], s1.at[g], r1.at[g], device_id=dev, device_id_type=DT
        )

    def second(g):
        if g % 2 == 0:
            dev = device(z, y, 1 - x, c)
            src = part.at[span(g), 1 - x, :, y]
        else:
            dev = device(z, 1 - y, x, c)
            src = part.at[span(g), x, :, 1 - y]
        return pltpu.make_async_remote_copy(
            src, two.at[g], s2.at[g], r2.at[g], device_id=dev, device_id_type=DT
        )

    def add_first(g):
        for m in range(size):
            for k in range(2):
                def body(zz, carry):
                    if g % 2 == 0:
                        at = (g * size + m, k, zz, y)
                    else:
                        at = (g * size + m, x, zz, k)
                    got = even[g // 2, m, k, zz] if g % 2 == 0 else odd[g // 2, m, zz, k]
                    part[at] = (part[at].astype(jnp.float32) + got.astype(jnp.float32)).astype(jnp.bfloat16)
                    return carry

                lax.fori_loop(0, levels, body, 0)

    def add_second(g):
        for m in range(size):
            def body(zz, carry):
                at = (g * size + m, x, zz, y)
                part[at] = (part[at].astype(jnp.float32) + two[g, m, zz].astype(jnp.float32)).astype(jnp.bfloat16)
                return carry

            lax.fori_loop(0, levels, body, 0)

    def z_copy(g, zz, up):
        return pltpu.make_async_remote_copy(
            part.at[span(g), x, zz, y], line.at[g, up, zz], s3.at[g, zz], r3.at[g, up, zz],
            device_id=device(z + 1 if up else z - 1, y, x, c), device_id_type=DT,
        )

    def add_line(g, zz, up):
        for m in range(size):
            at = (g * size + m, x, zz, y)
            part[at] = (part[at].astype(jnp.float32) + line[g, up, zz, m].astype(jnp.float32)).astype(jnp.bfloat16)

    def third(g):
        def run(k, carry):
            top = levels - 1 - k

            @pl.when(top > z)
            def _():
                @pl.when(z > 0)
                def _():
                    z_copy(g, top, 1).wait_recv()
                    add_line(g, top, 1)

                z_copy(g, top, 1).start()

            @pl.when(k < z)
            def _():
                @pl.when(z < levels - 1)
                def _():
                    z_copy(g, k, 0).wait_recv()
                    add_line(g, k, 0)

                z_copy(g, k, 0).start()

            return carry

        lax.fori_loop(0, levels, run, 0)

    def last(g):
        @pl.when(z > 0)
        def _():
            z_copy(g, z, 1).wait_recv()

        @pl.when(z < levels - 1)
        def _():
            z_copy(g, z, 0).wait_recv()

        for m in range(size):
            i = g * size + m
            own = part[i, x, z, y].astype(jnp.float32)
            below = jnp.where(z > 0, line[g, 1, z, m].astype(jnp.float32), 0.0)
            above = jnp.where(z < levels - 1, line[g, 0, z, m].astype(jnp.float32), 0.0)
            out[i] = own + below + above

    def drain(g):
        first(g).wait_send()
        second(g).wait_send()

        def run(zz, carry):
            @pl.when(zz > z)
            def _():
                z_copy(g, zz, 1).wait_send()

            @pl.when(zz < z)
            def _():
                z_copy(g, zz, 0).wait_send()

            return carry

        lax.fori_loop(0, levels, run, 0)

    for g in range(groups):
        first(g).start()
    for step in range(groups + 2):
        if step < groups:
            first(step).wait_recv()
            add_first(step)
            second(step).start()
        if 1 <= step <= groups:
            second(step - 1).wait_recv()
            add_second(step - 1)
            third(step - 1)
        if step >= 2:
            last(step - 2)
    for g in range(groups):
        drain(g)


def scatter_grads(part, shards):
    levels = shards // 2
    rows = D // shards
    groups = 8
    size = MATS // groups
    sem = pltpu.SemaphoreType.DMA
    bf = jnp.bfloat16
    vm = pl.BlockSpec(memory_space=pltpu.VMEM)

    def kernel(levels, groups, given, out, part, *rest):
        load = pltpu.make_async_copy(given, part, rest[-1])
        load.start()
        load.wait()
        scatter_kernel(levels, groups, part, out, *rest[:-1])

    return pl.pallas_call(
        partial(kernel, levels, groups),
        out_shape=jax.ShapeDtypeStruct((MATS, rows, COLS), jnp.float32),
        in_specs=[pl.BlockSpec(memory_space=pl.ANY)],
        out_specs=vm,
        scratch_shapes=[
            pltpu.VMEM((MATS, 2, levels, 2, rows, COLS), bf),
            pltpu.VMEM((groups // 2, size, 2, levels, rows, COLS), bf),
            pltpu.VMEM((groups // 2, size, levels, 2, rows, COLS), bf),
            pltpu.VMEM((groups, size, levels, rows, COLS), bf),
            pltpu.VMEM((groups, 2, levels, size, rows, COLS), bf),
            sem((groups,)), sem((groups,)), sem((groups,)), sem((groups,)),
            sem((groups, levels)), sem((groups, 2, levels)), sem,
        ],
        compiler_params=pltpu.CompilerParams(
            collective_id=1, has_side_effects=True, vmem_limit_bytes=62 * 2**20
        ),
        name="scatter_grads",
    )(part.reshape(MATS, 2, levels, 2, rows, COLS))


def small_kernel(shards, every, scatter, src, out, own_sem, send_sem, recv_sem):
    dp, x, c = (lax.axis_index(a) for a in AXES)
    cores = 2 if every else 1
    count = shards * 2 * cores
    me = (dp * 2 + x) * cores + (c if every else 0)

    def peer(i):
        if every:
            return (i // 4, lax.rem(i // 2, 2), lax.rem(i, 2))
        return (i // 2, lax.rem(i, 2), c)

    bar = pltpu.get_barrier_semaphore()

    def greet(k, carry):
        pl.semaphore_signal(bar, inc=1, device_id=peer(lax.rem(me + k, count)), device_id_type=DT)
        return carry

    lax.fori_loop(1, count, greet, 0)
    pl.semaphore_wait(bar, count - 1)

    def copy(k):
        i = lax.rem(me + k, count)
        return pltpu.make_async_remote_copy(
            src.at[i] if scatter else src, out.at[me], send_sem.at[k], recv_sem.at[me],
            device_id=peer(i), device_id_type=DT,
        )

    def send(k, carry):
        copy(k).start()
        return carry

    own = pltpu.make_async_copy(src.at[me] if scatter else src, out.at[me], own_sem)
    own.start()
    lax.fori_loop(1, count, send, 0)
    own.wait()

    def finish(k, carry):
        i = lax.rem(me + k, count)
        pltpu.make_async_remote_copy(
            src.at[i] if scatter else src, out.at[i], send_sem.at[k], recv_sem.at[i],
            device_id=peer(i), device_id_type=DT,
        ).wait_recv()
        copy(k).wait_send()
        return carry

    lax.fori_loop(1, count, finish, 0)


def small_exchange(src, shards, every, scatter, call_id):
    count = shards * 2 * (2 if every else 1)
    shape = src.shape[1:] if scatter else src.shape
    sem = pltpu.SemaphoreType.DMA
    vm = pl.BlockSpec(memory_space=pltpu.VMEM)
    return pl.pallas_call(
        partial(small_kernel, shards, every, scatter),
        out_shape=jax.ShapeDtypeStruct((count, *shape), src.dtype),
        in_specs=[vm],
        out_specs=vm,
        scratch_shapes=[sem, sem((count,)), sem((count,))],
        compiler_params=pltpu.CompilerParams(collective_id=call_id, has_side_effects=True),
        name=f"small_exchange_{call_id}",
    )(src)


def pair_kernel(src, out, own_sem, send_sem, recv_sem):
    dp, x, c = (lax.axis_index(a) for a in AXES)
    bar = pltpu.get_barrier_semaphore()
    pl.semaphore_signal(bar, inc=1, device_id=(dp, x, 1 - c), device_id_type=DT)
    pl.semaphore_wait(bar, 1)
    copy = pltpu.make_async_remote_copy(
        src, out.at[c], send_sem, recv_sem, device_id=(dp, x, 1 - c), device_id_type=DT
    )
    copy.start()
    own = pltpu.make_async_copy(src, out.at[c], own_sem)
    own.start()
    own.wait()
    copy.wait_send()
    pltpu.make_async_remote_copy(
        src, out.at[1 - c], send_sem, recv_sem, device_id=(dp, x, 1 - c), device_id_type=DT
    ).wait_recv()


def pair_gather(src, call_id):
    sem = pltpu.SemaphoreType.DMA
    vm = pl.BlockSpec(memory_space=pltpu.VMEM)
    return pl.pallas_call(
        pair_kernel,
        out_shape=jax.ShapeDtypeStruct((2, *src.shape), src.dtype),
        in_specs=[vm],
        out_specs=vm,
        scratch_shapes=[sem, sem, sem],
        compiler_params=pltpu.CompilerParams(collective_id=call_id, has_side_effects=True),
        name=f"pair_gather_{call_id}",
    )(src)


def pair_sum(part, call_id):
    both = pair_gather(part.astype(jnp.bfloat16), call_id)
    return both[0].astype(jnp.float32) + both[1].astype(jnp.float32)


def norm_forward(values, gain_row, offset):
    centre = values - jnp.mean(values, axis=-1, keepdims=True)
    spread = jnp.mean(centre * centre, axis=-1, keepdims=True)
    scaled = lax.rsqrt(spread + 1e-05)
    normed = centre * scaled
    return (normed * gain_row + offset, normed, scaled)


def norm_backward(gradient, normed, scaled, gain_row):
    inner_grad = gradient * gain_row
    result = scaled * (
        inner_grad
        - jnp.mean(inner_grad, axis=-1, keepdims=True)
        - normed * jnp.mean(inner_grad * normed, axis=-1, keepdims=True)
    )
    return (result, jnp.sum(gradient * normed, axis=0), jnp.sum(gradient, axis=0))


def gelu_value(values):
    return 0.5 * values * (1.0 + jax.scipy.special.erf(values * 0.7071067811865476))


def gelu_slope(values):
    return (
        0.5 * (1.0 + jax.scipy.special.erf(values * 0.7071067811865476))
        + values * jnp.exp(-0.5 * values * values) * 0.3989422804014327
    )


def clip_scores(queries, key_rows, causal):
    scores = (
        jnp.einsum("qhd,khd->hqk", queries, key_rows, preferred_element_type=jnp.float32) * 0.125
    )
    if causal:
        allowed = lax.broadcasted_iota(jnp.int32, scores.shape, 1) >= lax.broadcasted_iota(
            jnp.int32, scores.shape, 2
        )
        scores = jnp.where(allowed, scores, -1e30)
    return scores


def clip_forward(causal, queries, key_rows, values):
    scores = clip_scores(queries, key_rows, causal)
    row_max = jnp.max(scores, axis=-1, keepdims=True)
    shifted = jnp.exp(scores - row_max)
    row_sum = jnp.sum(shifted, axis=-1, keepdims=True)
    weights = (shifted / row_sum).astype(jnp.bfloat16)
    context = jnp.einsum("hqk,khd->qhd", weights, values, preferred_element_type=jnp.float32)
    return (context.astype(jnp.bfloat16), (row_max + jnp.log(row_sum))[..., 0])


def clip_backward(causal, queries, key_rows, values, log_total, context_grad):
    scores = clip_scores(queries, key_rows, causal)
    probs = jnp.exp(scores - log_total[..., None])
    value_grad = jnp.einsum(
        "hqk,qhd->khd", probs.astype(jnp.bfloat16), context_grad, preferred_element_type=jnp.float32
    )
    prob_grad = jnp.einsum("qhd,khd->hqk", context_grad, values, preferred_element_type=jnp.float32)
    score_grad = (probs * (prob_grad - jnp.sum(probs * prob_grad, axis=-1, keepdims=True))).astype(
        jnp.bfloat16
    )
    query_grad = (
        jnp.einsum("hqk,khd->qhd", score_grad, key_rows, preferred_element_type=jnp.float32) * 0.125
    )
    key_grad = (
        jnp.einsum("hqk,qhd->khd", score_grad, queries, preferred_element_type=jnp.float32) * 0.125
    )
    return (
        query_grad.astype(jnp.bfloat16),
        key_grad.astype(jnp.bfloat16),
        value_grad.astype(jnp.bfloat16),
    )


def adapt(weight, gradient, moment, second, token_total):
    scaled_grad = gradient / token_total
    new_moment = 0.5 * moment + 0.5 * scaled_grad
    new_second = 0.5 * second + 0.5 * scaled_grad * scaled_grad
    direction = new_moment / (jnp.sqrt(new_second) + 1e-06) + 0.01 * weight
    return (new_moment, new_second, direction)


def shards_fn(
    tokens, frames, cotangent, attention_weights, dense_weights, unit_bias, norm_bias,
    attention_mean, dense_mean, unit_mean, norm_mean,
    attention_square, dense_square, unit_square, norm_square,
):
    f32, bf = jnp.float32, jnp.bfloat16
    shards = lax.axis_size("dp")
    rows = D // shards
    c = lax.axis_index("core")
    unit_cols = unit_bias.shape[1]
    column_rows = (lax.axis_index("dp") * unit_cols + jnp.arange(unit_cols, dtype=jnp.int32)) // HD
    row_pick = (column_rows[:, None] == jnp.arange(8, dtype=jnp.int32)[None, :]).astype(f32)
    leader = ((lax.axis_index("side") == 0) & (c == 0)).astype(f32)

    def square_rows(attn_part, dense_part, unit_part, norm_part):
        unit_sums = jnp.sum(jnp.sum(unit_part * unit_part, axis=0)[:, None] * row_pick, axis=0)
        return jnp.concatenate(
            [
                jnp.sum(attn_part * attn_part, axis=(2, 3)).reshape(8),
                jnp.sum(dense_part * dense_part, axis=(1, 2, 3)),
                unit_sums,
                jnp.sum(norm_part * norm_part, axis=1) * leader,
            ]
        )

    own_attn = attention_weights.astype(f32)
    own_dense = dense_weights.astype(f32)
    own_unit = unit_bias.astype(f32)
    own_norm = norm_bias.astype(f32)

    pack = jnp.concatenate([norm_bias.reshape(-1), unit_bias.reshape(-1)])
    pack = jnp.pad(pack, (0, 2048 - pack.shape[0])).reshape(16, 128)
    packs = small_exchange(pack, shards, False, False, 2).reshape(shards, 2, 2048)
    norm_rows = (
        packs[:, 0, : 9 * rows].reshape(shards, 9, rows).transpose(1, 0, 2).reshape(9, D).astype(f32)
    )
    unit_all = packs[:, :, 9 * rows : 9 * rows + 4 * unit_cols].reshape(shards, 2, 4, unit_cols)
    bias_rows = (
        unit_all.transpose(1, 2, 0, 3).reshape(8, 8, HD).transpose(1, 0, 2).reshape(8, 512).astype(f32)
    )

    shard = jnp.concatenate(
        [attention_weights.reshape(8, rows, COLS), dense_weights.transpose(0, 2, 1, 3).reshape(8, rows, COLS)]
    )
    wide = gather_weights(shard, shards)

    def project(left, mat):
        return jnp.einsum("rd,xde->rxe", left, wide[mat], preferred_element_type=f32).reshape(-1, 512)

    def project_hidden(left, base):
        return jnp.einsum("rd,mxde->rmxe", left, wide[base : base + 4], preferred_element_type=f32).reshape(-1, 2048)

    def collect(left, mat):
        return jnp.einsum("rxe,xde->rd", left.reshape(-1, 2, COLS), wide[mat], preferred_element_type=f32)

    def collect_hidden(left, base):
        return jnp.einsum("rmxe,mxde->rd", left.reshape(-1, 4, 2, COLS), wide[base : base + 4], preferred_element_type=f32)

    def weight_grad(left, right):
        return jnp.einsum("rd,rme->mde", left, right.reshape(right.shape[0], -1, COLS), preferred_element_type=f32).astype(bf)

    def by_head(flat):
        return flat.reshape(-1, 8, HD)

    row_data = pair_gather(tokens, 3).reshape(L, D).astype(f32)
    out_grad_low = pair_gather(cotangent, 4).reshape(L, D)
    frame_rows = pair_gather(frames, 5).reshape(FRAMES, D)

    first_in, first_normed, first_scale = norm_forward(row_data, norm_rows[0], norm_rows[1])
    first_in = first_in.astype(bf)
    self_query = (project(first_in, 0) + bias_rows[0]).astype(bf)
    self_keys = project(first_in, 1).astype(bf)
    self_values = (project(first_in, 2) + bias_rows[1]).astype(bf)
    self_context, self_total = clip_forward(
        True, by_head(self_query), by_head(self_keys), by_head(self_values)
    )
    self_flat = self_context.reshape(L, 512)
    hidden_one = row_data + norm_rows[6] + pair_sum(collect(self_flat, 3), 6)
    second_in, second_normed, second_scale = norm_forward(hidden_one, norm_rows[2], norm_rows[3])
    second_in = second_in.astype(bf)
    cross_query = (project(second_in, 4) + bias_rows[2]).astype(bf)
    cross_keys = project(frame_rows, 5).astype(bf)
    cross_values = (project(frame_rows, 6) + bias_rows[3]).astype(bf)
    cross_context, cross_total = clip_forward(
        False, by_head(cross_query), by_head(cross_keys), by_head(cross_values)
    )
    cross_flat = cross_context.reshape(L, 512)
    hidden_two = hidden_one + norm_rows[7] + pair_sum(collect(cross_flat, 7), 7)
    third_in, third_normed, third_scale = norm_forward(hidden_two, norm_rows[4], norm_rows[5])
    third_in = third_in.astype(bf)
    before = project_hidden(third_in, 8) + bias_rows[4:8].reshape(2048)
    activated = gelu_value(before).astype(bf)
    result_rows = hidden_two + norm_rows[8] + pair_sum(collect_hidden(activated, 12), 8)
    layer_out = lax.dynamic_slice_in_dim(result_rows, c * (L // 2), L // 2, 0).astype(bf)

    out_grad = out_grad_low.astype(f32)
    act_grad = project_hidden(out_grad_low, 12)
    down_grad = weight_grad(out_grad_low, activated)
    before_grad = (act_grad * gelu_slope(before)).astype(bf)
    hidden_bias_grad = jnp.sum(before_grad, axis=0, dtype=f32)
    up_grad = weight_grad(third_in, before_grad)
    third_back = pair_sum(collect_hidden(before_grad, 8), 9)
    third_input_grad, third_gain_grad, third_offset_grad = norm_backward(
        third_back, third_normed, third_scale, norm_rows[4]
    )
    two_grad = out_grad + third_input_grad
    two_low = two_grad.astype(bf)
    cross_ctx_grad = project(two_low, 7).astype(bf)
    cross_out_grad = weight_grad(two_low, cross_flat)
    cross_qgrad, cross_kgrad, cross_vgrad = clip_backward(
        False, by_head(cross_query), by_head(cross_keys), by_head(cross_values), cross_total,
        by_head(cross_ctx_grad),
    )
    cross_qflat = cross_qgrad.reshape(L, 512)
    cross_kflat = cross_kgrad.reshape(FRAMES, 512)
    cross_vflat = cross_vgrad.reshape(FRAMES, 512)
    frame_part = collect(cross_kflat, 5) + collect(cross_vflat, 6)
    frame_both = pair_gather(frame_part.astype(bf), 10)
    frame_gradient = jnp.sum(
        lax.dynamic_slice_in_dim(frame_both, c * (FRAMES // 2), FRAMES // 2, 1).astype(f32), axis=0
    )
    second_back = pair_sum(collect(cross_qflat, 4), 11)
    second_input_grad, second_gain_grad, second_offset_grad = norm_backward(
        second_back, second_normed, second_scale, norm_rows[2]
    )
    one_grad = two_grad + second_input_grad
    one_low = one_grad.astype(bf)
    self_ctx_grad = project(one_low, 3).astype(bf)
    self_out_grad = weight_grad(one_low, self_flat)
    self_qgrad, self_kgrad, self_vgrad = clip_backward(
        True, by_head(self_query), by_head(self_keys), by_head(self_values), self_total,
        by_head(self_ctx_grad),
    )
    self_qflat, self_kflat, self_vflat = (v.reshape(L, 512) for v in (self_qgrad, self_kgrad, self_vgrad))
    first_back = pair_sum(
        collect(self_qflat, 0) + collect(self_kflat, 1) + collect(self_vflat, 2), 12
    )
    first_input_grad, first_gain_grad, first_offset_grad = norm_backward(
        first_back, first_normed, first_scale, norm_rows[0]
    )
    input_gradient = lax.dynamic_slice_in_dim(one_grad + first_input_grad, c * (L // 2), L // 2, 0)

    parts = jnp.concatenate(
        [
            weight_grad(first_in, self_qflat), weight_grad(first_in, self_kflat),
            weight_grad(first_in, self_vflat), self_out_grad,
            weight_grad(second_in, cross_qflat), weight_grad(frame_rows, cross_kflat),
            weight_grad(frame_rows, cross_vflat), cross_out_grad, up_grad, down_grad,
        ]
    )
    owned = scatter_grads(parts, shards)
    attention_owned = owned[:8].reshape(2, 4, rows, COLS)
    dense_owned = owned[8:].reshape(2, 4, rows, COLS).transpose(0, 2, 1, 3)

    def column(v):
        return jnp.sum(v, axis=0, dtype=f32)

    unit_rows_grad = jnp.concatenate(
        [
            jnp.stack([column(self_qflat), column(self_vflat), column(cross_qflat), column(cross_vflat)]),
            hidden_bias_grad.reshape(4, 512),
        ]
    )
    unit_grads = (
        unit_rows_grad.reshape(8, 2, 4, HD).transpose(1, 2, 0, 3).reshape(2, 4, shards, unit_cols)
        .transpose(2, 0, 1, 3).reshape(shards, 2, 4 * unit_cols)
    )
    norm_grads = jnp.stack(
        [
            first_gain_grad, first_offset_grad, second_gain_grad, second_offset_grad,
            third_gain_grad, third_offset_grad, column(one_grad), column(two_grad), column(out_grad),
        ]
    )
    norm_parts = norm_grads.reshape(9, shards, rows).transpose(1, 0, 2).reshape(shards, 1, 9 * rows)
    small = jnp.concatenate([jnp.broadcast_to(norm_parts, (shards, 2, 9 * rows)), unit_grads], axis=2)
    small = jnp.pad(small, ((0, 0), (0, 0), (0, 2048 - small.shape[2]))).reshape(shards * 2, 16, 128)
    small = jnp.sum(small_exchange(small, shards, False, True, 13), axis=0).reshape(2048)
    norm_owned = small[: 9 * rows].reshape(9, rows)
    unit_owned = small[9 * rows : 9 * rows + 4 * unit_cols].reshape(4, unit_cols)

    token_total = float(tokens.shape[0] * shards * 4)
    attn_moment, attn_second, attn_dir = adapt(
        own_attn, attention_owned, attention_mean, attention_square, token_total
    )
    dense_moment, dense_second, dense_dir = adapt(
        own_dense, dense_owned, dense_mean, dense_square, token_total
    )
    unit_moment, unit_second, unit_dir = adapt(
        own_unit, unit_owned, unit_mean, unit_square, token_total
    )
    norm_moment, norm_second, norm_dir = adapt(
        own_norm, norm_owned, norm_mean, norm_square, token_total
    )
    sums = jnp.concatenate(
        [
            square_rows(own_attn, own_dense, own_unit, own_norm),
            square_rows(attn_dir, dense_dir, unit_dir, norm_dir),
        ]
    )
    sums = jnp.pad(sums, (0, 1024 - 54)).reshape(8, 128)
    sums = jnp.sum(small_exchange(sums, shards, True, False, 14), axis=0).reshape(1024)
    weight_norms = jnp.sqrt(sums[:27])
    step_norms = jnp.sqrt(sums[27:54])
    trust = weight_norms / step_norms
    attention_step = -learning_rate * trust[0:8].reshape(2, 4, 1, 1) * attn_dir
    dense_step = -learning_rate * trust[8:10].reshape(2, 1, 1, 1) * dense_dir
    unit_factor = jnp.sum(row_pick * trust[10:18][None, :], axis=1)
    unit_step = -learning_rate * unit_factor[None, :] * unit_dir
    norm_step = -learning_rate * trust[18:27][:, None] * norm_dir
    return (
        layer_out, input_gradient, frame_gradient,
        attention_owned, dense_owned, unit_owned, norm_owned,
        attn_moment, dense_moment, unit_moment, norm_moment,
        attn_second, dense_second, unit_second, norm_second,
        attention_step, dense_step, unit_step, norm_step,
        weight_norms, step_norms,
    )


def solution(mesh):
    shards = mesh.shape["dp"]
    inner = Mesh(mesh.devices.reshape(shards, 2, 2), AXES)
    tensor = ("side", "core")
    rows = P(("dp", *tensor), None)
    state = (P(None, None, "dp", tensor), P(None, "dp", None, tensor), P(tensor, "dp"), P(None, "dp"))
    return jax.shard_map(
        shards_fn,
        mesh=inner,
        in_specs=(rows, rows, rows) + state * 3,
        out_specs=(rows, rows, rows) + state * 4 + (P(), P()),
        check_vma=False,
    )
```

time: 1270 us -> 801 us (0.63)
  waiting for transfers between devices: 735 us -> 0 us
  Pallas kernels: 0 us -> 431 us
  blocking collectives: 149 us -> 0 us
  matrix products: 131 us -> 153 us
  local copies, waits for them, and re-layouts: 132 us -> 112 us
  between operations: 16.2 us -> 2.18 us
    pallas_call x0 -> x15, Pallas kernels: none -> 431 us  [the longest x1 199 us: scatter_grads(): pl.pallas_call(partial(kernel, levels, groups), out_shape=jax.ShapeDtypeS...]
    reduce_scatter x8 -> x0, waiting for transfers between devices: 396 us -> none  [the longest x1 144 us: shards(): lax.psum_scatter(jnp.stack([self_grads, cross_grads]), 'dp', scatter_dime...]
    all_gather x9 -> x0, waiting for transfers between devices: 261 us -> none  [the longest x1 75 us: shards(): lax.all_gather(attention_weights, 'dp', axis=2, tiled=True)]
    unnamed x22 -> x0, waiting for transfers between devices: 77.9 us -> none
    unnamed x1 -> x0, blocking collectives: 56.7 us -> none
    all_gather x2 -> x0, blocking collectives: 47.1 us -> none  [the longest x1 28 us: shards(): lax.all_gather(norm_bias, 'dp', axis=1, tiled=True)]
    psum x2 -> x0, blocking collectives: 45.2 us -> none  [the longest x1 39.3 us: shards(): lax.psum((square_rows(own_attn, own_dense, own_unit, own_norm), square_ro...]
    unnamed x196 -> x164, local copies, waits for them, and re-layouts: 54.8 us -> 12.3 us
  transfers between devices with their start and end apart: 20 -> 0, of which waited for: 17 -> 0; matrix products, arithmetic and copies ran while one was open for 19% -> 0% of each run, Pallas kernels for 0% -> 0%
where the time goes in v1:
time: 801 us; the launch traced here: 790 us
  Pallas kernels  431 us (54%)
  matrix products  153 us (19%)
  local copies, waits for them, and re-layouts  112 us (14%)
  other arithmetic  91.1 us (11%)
    pallas_call x1, Pallas kernels, scatter_grads(): pl.pallas_call(partial(kernel, levels, groups), out_shape=jax.ShapeDtypeS...  199 us
    pallas_call x1, Pallas kernels, gather_weights(): pl.pallas_call(partial(gather_kernel, levels, groups), out_shape=jax.Shap...  150 us
    pallas_call x10, Pallas kernels, pair_gather(): pl.pallas_call(pair_kernel, out_shape=jax.ShapeDtypeStruct((2, *src.shape...  53.8 us
    pallas_call x3, Pallas kernels, small_exchange(): pl.pallas_call(partial(small_kernel, shards, every, scatter), out_shape=j...  27.4 us
    dot_general x10, matrix products, weight_grad(): jnp.einsum('rd,rme->mde', left, right.reshape(right.shape[0], -1, COLS),...  24.6 us
    dot_general x8, matrix products, project(): jnp.einsum('rd,xde->rxe', left, wide[mat], preferred_element_type=f32)  24 us
    dot_general x2, matrix products, clip_backward(): jnp.einsum('qhd,khd->hqk', context_grad, values, preferred_element_type=j...  23.4 us
    concatenate x1, local copies, waits for them, and re-layouts, shards_fn(): jnp.concatenate([weight_grad(first_in, self_qflat), weight_grad(first_in,...  22.5 us

profile of v1, /device:TPU:0, one launch (start us, length us, event | category | flops | bytes accessed | tf_op | source)
XLA Modules:
  0.0 789.5 jit_solution(10946136830059433799)
XLA Ops:
  3.9 150.4 %gather_weights.1 = bf16[16,2,4,2,128,256]{5,4,3,2,1,0:T(8,128)(2,1)} custom-call(bf16[16,128,256]{2,1,0:T(8,128)(2,1)} %pad_maximum_fusion.shard), custom_call_target="tpu_custom_call" | custom-call | tf_op jit(solution)/shard_map/gather_weights/pallas_call | solution.py:197
  154.3 6.0 fusion.113
  160.4 3.8 pair_gather_4.1
  164.2 4.5 convolution_bitcast_fusion.1
  168.7 4.6 copy.137
  173.3 5.8 reshape.1183
  179.8 8.8 %small_exchange_2.1 = bf16[16,16,128]{2,1,0:T(8,128)(2,1)} custom-call(bf16[16,128]{1,0:T(8,128)(2,1)} %fusion.96.src), custom_call_target="tpu_custom_call" | custom-call | tf_op jit(solution)/shard_map/small_exchange_2/pallas_call | solution.py:439
  189.7 3.8 pair_gather_3.1
  198.0 5.9 fusion.114
  226.2 4.9 pair_gather_6.1
  241.5 6.5 pair_gather_5.1
  248.0 4.1 reshape.1203
  252.1 5.1 fusion.23
  260.1 4.6 fusion.118
  264.7 5.7 fusion
  280.5 10.3 %fusion.72 = bf16[8,64,448]{2,1,0:T(8,128)(2,1)S(1)} fusion(f32[8,448,1500]{2,1,0:T(8,128)} %copy-done, f32[8,448]{1,0:T(8,128)S(1)} %fusion, f32[8,448]{1,0:T(8,128)S(1)} %get-tuple-element.109, f32[1500,8,64]{0,2,1:T(8,128)} %bitcast.363, f32[8,64]{1,0:T(8,128)S(1)} %get-tuple-element.99), kind=kOutput, calls=%fused_computation.146 | convolution fusion | flops 706021376 | bytes 25065472 | tf_op jit(solution)/shard_map/hqk,khd->qhd/dot_general | solution.py:534
  293.4 4.9 pair_gather_7.1
  302.2 6.3 copy.135
  308.6 7.6 convert_reduce_fusion.1
  316.2 5.6 reshape.1181
  321.8 5.8 bitcast_convert_fusion.1.src
  327.6 4.9 pair_gather_8.1
  335.8 4.0 subtract_multiply_fusion
  342.0 5.5 reshape.1184
  347.5 5.8 bitcast_convert_fusion.src
  353.3 5.0 pair_gather_9.1
  358.4 4.5 fusion.31
  375.8 15.6 %multiply_reduce_fusion = (f32[8,448]{1,0:T(8,128)S(1)}, f32[8,448,1500]{2,1,0:T(8,128)}) fusion(f32[8,448,1500]{2,1,0:T(8,128)} %copy-done, f32[8,448]{1,0:T(8,128)S(1)} %log_add_fusion.1, bf16[448,8,64]{0,2,1:T(8,128)(2,1)} %bitcast.382, f32[1500,8,64]{0,2,1:T(8,128)} %bitcast.364, f32[8,64]{1,0:T(8,128)S(1)} %get-tuple-element.99), kind=kOutput, calls=%fused_computation.1 | convolution fusion | flops 705788416 | bytes 46569472 | tf_op jit(solution)/shard_map/qhd,khd->hqk/dot_general | solution.py:544
  391.4 14.8 %multiply_convert_fusion = bf16[8,448,1500]{2,1,0:T(8,128)(2,1)S(1)} fusion(f32[8,448,1500]{2,1,0:T(8,128)} %get-tuple-element.112, f32[8,448,1500]{2,1,0:T(8,128)} %copy-done, f32[8,448]{1,0:T(8,128)S(1)} %get-tuple-element.111, f32[8,448]{1,0:T(8,128)S(1)} %log_add_fusion.1), kind=kLoop, calls=%fused_computation | loop fusion | flops 21504000 | bytes 53788672 | tf_op jit(solution)/shard_map/convert_element_type | solution.py:545
  406.2 4.2 convert_reduce_fusion.5
  413.5 4.9 pair_gather_11.1
  418.4 3.8 fusion.30
  431.2 7.8 multiply_reduce_fusion.1
  439.0 5.2 multiply_convert_fusion.1
  454.0 5.0 pair_gather_12.1
  465.2 6.2 fusion.22
  474.4 9.4 %convert_reduce_fusion.2 = (f32[8,64]{1,0:T(8,128)S(1)}, bf16[8,64,1500]{2,1,0:T(8,128)(2,1)S(1)}) fusion(bf16[448,8,64]{0,2,1:T(8,128)(2,1)S(1)} %bitcast.383, f32[8,448,1500]{2,1,0:T(8,128)} %copy-done, f32[8,448]{1,0:T(8,128)S(1)} %log_add_fusion.1), kind=kOutput, calls=%fused_computation.40 | convolution fusion | flops 701183488 | bytes 23515136 | tf_op jit(solution)/shard_map/hqk,qhd->khd/dot_general | solution.py:541
  483.8 3.6 fusion.7.src
  487.5 10.1 %pair_gather_10.1 = bf16[2,1500,1024]{2,1,0:T(8,128)(2,1)} custom-call(bf16[1500,1024]{1,0:T(8,128)(2,1)} %fusion.7.src), custom_call_target="tpu_custom_call" | custom-call | tf_op jit(solution)/shard_map/pair_gather_10/pallas_call | solution.py:471
  497.6 4.8 convert_reduce_fusion
  518.6 4.4 bitcast_dynamic-update-slice_fusion.1
  522.9 4.3 bitcast_dynamic-update-slice_fusion
  527.3 22.5 %copy.162 = bf16[32,1024,256]{2,1,0:T(8,128)(2,1)} copy(bf16[32,1024,256]{1,2,0:T(8,128)(2,1)} %bitcast_dynamic-update-slice_fusion) | data formatting | bytes 33554432 | tf_op jit(solution)/shard_map/concatenate | solution.py:711
  549.8 199.4 %scatter_grads.1 = f32[16,128,256]{2,1,0:T(8,128)} custom-call(bf16[16,2,4,2,128,256]{5,4,3,2,1,0:T(8,128)(2,1)} %bitcast.358), custom_call_target="tpu_custom_call" | custom-call | tf_op jit(solution)/shard_map/scatter_grads/pallas_call | solution.py:365
  752.1 3.7 multiply_reduce_fusion.7
  757.4 9.1 %small_exchange_13.1 = f32[16,16,128]{2,1,0:T(8,128)} custom-call(f32[16,16,128]{2,1,0:T(8,128)} %reshape.1192.src), custom_call_target="tpu_custom_call" | custom-call | tf_op jit(solution)/shard_map/small_exchange_13/pallas_call | solution.py:439
  768.3 4.0 multiply_reduce_fusion.8
  774.0 9.5 %small_exchange_14.1 = f32[32,8,128]{2,1,0:T(8,128)} custom-call(f32[8,128]{1,0:T(8,128)} %pad_bitcast_fusion.src), custom_call_target="tpu_custom_call" | custom-call | tf_op jit(solution)/shard_map/small_exchange_14/pallas_call | solution.py:439
  (312 shorter events, 140.3 us)
Async XLA Ops:
  173.3 5.8 copy-start.68
  173.3 5.9 copy-start.61
  193.5 3.1 copy-start.3
  193.6 4.4 copy-start.59
  203.9 5.1 copy-start.13
  209.1 12.1 %copy-start.36 = (bf16[448,512]{0,1:T(8,128)(2,1)}, bf16[448,512]{0,1:T(8,128)(2,1)S(1)}, u32[]{:S(2)}) copy-start(bf16[448,512]{0,1:T(8,128)(2,1)S(1)} %copy.123) | copy-start | bytes 1376260
  210.5 4.3 copy-start.15
  214.7 3.9 copy-start.38
  220.1 3.0 copy-start.1
  224.5 6.7 copy-start.70
  264.7 8.8 %copy-start = (f32[8,448,1500]{2,1,0:T(8,128)}, f32[8,448,1500]{2,1,0:T(8,128)S(1)}, u32[]{:S(2)}) copy-start(f32[8,448,1500]{2,1,0:T(8,128)S(1)} %get-tuple-element.110) | copy-start | bytes 64512004
  264.7 8.8 %copy-start.24 = (bf16[1,2,4,2,128,256]{5,4,3,2,1,0:T(8,128)(2,1)S(1)}, bf16[1,2,4,2,128,256]{5,4,3,2,1,0:T(8,128)(2,1)}, u32[]{:S(2)}) copy-start(bf16[1,2,4,2,128,256]{5,4,3,2,1,0:T(8,128)(2,1)} %get-tuple-element.71) | copy-start | bytes 3145732
  264.7 8.8 %copy-start.31 = (bf16[1500,1024,1]{1,0,2:T(8,128)(2,1)S(1)}, bf16[1500,1024,1]{1,0,2:T(8,128)(2,1)}, u32[]{:S(2)}) copy-start(bf16[1500,1024,1]{1,0,2:T(8,128)(2,1)} %reshape.1203) | copy-start | bytes 9216004
  280.5 11.2 %copy-start.27 = (bf16[1,2,4,2,128,256]{5,4,3,2,1,0:T(8,128)(2,1)S(1)}, bf16[1,2,4,2,128,256]{5,4,3,2,1,0:T(8,128)(2,1)}, u32[]{:S(2)}) copy-start(bf16[1,2,4,2,128,256]{5,4,3,2,1,0:T(8,128)(2,1)} %get-tuple-element.68) | copy-start | bytes 3145732
  335.8 5.2 copy-start.30
  391.4 14.8 %copy-start.6 = (bf16[1500,2,256]{0,2,1:T(8,128)(2,1)S(1)}, bf16[1500,2,256]{0,2,1:T(8,128)(2,1)}, u32[]{:S(2)}) copy-start(bf16[1500,2,256]{0,2,1:T(8,128)(2,1)} %copy.133) | copy-start | bytes 4608004
  406.2 4.2 copy-start.2
  431.1 7.8 copy-start.22
  431.1 7.8 slice-start
  431.2 7.8 slice-start.1
  454.0 5.0 copy-start.12
  454.0 5.0 copy-start.60
  459.0 3.3 copy-start.11
  459.0 3.3 copy-start.19
  459.1 3.3 copy-start.28
  459.1 3.4 copy-start.29
  465.2 7.4 copy-start.52
  474.4 9.4 %copy-start.25 = (bf16[1,2,4,2,128,256]{5,4,3,2,1,0:T(8,128)(2,1)S(1)}, bf16[1,2,4,2,128,256]{5,4,3,2,1,0:T(8,128)(2,1)}, u32[]{:S(2)}) copy-start(bf16[1,2,4,2,128,256]{5,4,3,2,1,0:T(8,128)(2,1)} %get-tuple-element.71) | copy-start | bytes 3145732
  497.5 4.9 copy-start.45
  497.6 4.9 copy-start.54
  505.9 3.4 copy-start.58
  507.6 3.4 copy-start.32
  513.8 2.9 copy-start.57
  513.8 2.9 copy-start.73
  518.6 4.4 copy-start.20
  518.6 4.4 copy-start.48
  749.2 2.9 copy-start.35
  749.2 2.9 copy-start.50
  749.2 2.9 copy-start.51
  752.1 4.1 copy-start.7
  755.8 11.8 %copy-start.62 = (bf16[9,128]{1,0:T(8,128)(2,1)S(1)}, bf16[9,128]{1,0:T(8,128)(2,1)}, u32[]{:S(2)}) copy-start(bf16[9,128]{1,0:T(8,128)(2,1)} %param.21) | copy-start | bytes 6916
  755.8 11.8 %copy-start.63 = (f32[9,128]{1,0:T(8,128)S(1)}, f32[9,128]{1,0:T(8,128)}, u32[]{:S(2)}) copy-start(f32[9,128]{1,0:T(8,128)} %param.29) | copy-start | bytes 13828
  755.8 11.8 %copy-start.64 = (f32[9,128]{1,0:T(8,128)S(1)}, f32[9,128]{1,0:T(8,128)}, u32[]{:S(2)}) copy-start(f32[9,128]{1,0:T(8,128)} %param.25) | copy-start | bytes 13828
  755.8 12.5 %copy-start.39 = (bf16[2,4,128,256]{3,2,1,0:T(8,128)(2,1)S(1)}, bf16[2,4,128,256]{3,2,1,0:T(8,128)(2,1)}, u32[]{:S(2)}) copy-start(bf16[2,4,128,256]{3,2,1,0:T(8,128)(2,1)} %param.18) | copy-start | bytes 1572868
  767.6 4.8 copy-start.65
  768.3 4.0 copy-start.66
  768.3 4.0 copy-start.67
  768.3 4.0 copy-start.69
  (28 other events, 46.2 us)

commit v2 on v1

--- a/solution.py
+++ b/solution.py
@@ -48,165 +48,610 @@
     )
 
 
-def gather_kernel(levels, groups, shard, wide, own_sem, z_send, z_recv, x_send, x_recv, y_send, y_recv):
+def start_when(cond, copy):
+    @pl.when(cond)
+    def _():
+        copy.start()
+
+
+class Gather:
+    def __init__(self, levels, groups, shard, wide, sems):
+        self.levels, self.groups, self.size = levels, groups, MATS // groups
+        self.shard, self.wide = shard, wide
+        self.own, self.zs, self.zr, self.xs, self.xr, self.ys, self.yr = sems
+        self.at = place()
+        self.done = 0
+        self.total = (groups + 1) * levels
+
+    @staticmethod
+    def semaphores(levels, groups):
+        sem = pltpu.SemaphoreType.DMA
+        pair = sem((groups, levels, 2))
+        return [sem, pair, sem((groups, levels)), pair, pair, pair, pair]
+
+    def block(self, g, xx, zz, yy):
+        return self.wide.at[pl.ds(g * self.size, self.size), xx, zz, yy]
+
+    def source(self, g, xx, zz, yy, own):
+        return self.shard.at[pl.ds(g * self.size, self.size)] if own else self.block(g, xx, zz, yy)
+
+    def z_copy(self, g, zz, up, own):
+        z, y, x, c = self.at
+        return pltpu.make_async_remote_copy(
+            self.source(g, x, zz, y, own), self.block(g, x, zz, y), self.zs.at[g, zz, up], self.zr.at[g, zz],
+            device_id=device(z + 1 if up else z - 1, y, x, c), device_id_type=DT,
+        )
+
+    def x_copy(self, g, zz, yy, own):
+        z, y, x, c = self.at
+        return pltpu.make_async_remote_copy(
+            self.source(g, x, zz, yy, own), self.block(g, x, zz, yy), self.xs.at[g, zz, yy],
+            self.xr.at[g, zz, yy], device_id=device(z, y, 1 - x, c), device_id_type=DT,
+        )
+
+    def y_copy(self, g, zz, xx, own):
+        z, y, x, c = self.at
+        return pltpu.make_async_remote_copy(
+            self.source(g, xx, zz, y, own), self.block(g, xx, zz, y), self.ys.at[g, zz, xx],
+            self.yr.at[g, zz, xx], device_id=device(z, 1 - y, x, c), device_id_type=DT,
+        )
+
+    def begin(self):
+        z, y, x, c = self.at
+        self.local = pltpu.make_async_copy(self.shard, self.wide.at[:, x, z, y], self.own)
+        self.local.start()
+
+    def first(self, g, d):
+        z, y, x, c = self.at
+        top = self.levels - 1
+
+        @pl.when(d == 0)
+        def _():
+            start_when(z < top, self.z_copy(g, z, 1, True))
+            start_when(z > 0, self.z_copy(g, z, 0, True))
+            self.x_copy(g, z, y, True).start()
+            self.y_copy(g, z, x, True).start()
+
+        for up in (1, 0):
+            zz = z - d if up else z + d
+            here = (zz >= 0) if up else (zz <= top)
+
+            @pl.when((d > 0) & here)
+            def _():
+                self.z_copy(g, zz, up, False).wait_recv()
+                start_when((z < top) if up else (z > 0), self.z_copy(g, zz, up, False))
+                self.x_copy(g, zz, y, False).start()
+                self.y_copy(g, zz, x, False).start()
+
+    def second(self, g, d):
+        z, y, x, c = self.at
+        even = lax.rem(g, 2) == 0
+        for up in (1, 0):
+            zz = z - d if up else z + d
+            here = (zz >= 0) if up else ((zz < self.levels) & (d > 0))
+
+            @pl.when(here & even)
+            def _():
+                self.x_copy(g, zz, y, False).wait_recv()
+                self.y_copy(g, zz, 1 - x, False).start()
+
+            @pl.when(here & jnp.logical_not(even))
+            def _():
+                self.y_copy(g, zz, x, False).wait_recv()
+                self.x_copy(g, zz, 1 - y, False).start()
+
+    def tick(self, t):
+        g, d = t // self.levels, lax.rem(t, self.levels)
+
+        @pl.when(g < self.groups)
+        def _():
+            self.first(g, d)
+
+        @pl.when(g >= 1)
+        def _():
+            self.second(g - 1, d)
+
+    def run(self, count):
+        count = max(0, min(count, self.total - self.done))
+        start = self.done
+        self.done += count
+        if count:
+            def body(i, carry):
+                self.tick(start + i)
+                return carry
+
+            lax.fori_loop(0, count, body, 0)
+
+    def reserve(self, count):
+        if self.total - self.done < count:
+            return lambda i: None
+        start = self.done
+        self.done += count
+        return lambda i: self.tick(start + i)
+
+    def need(self, g):
+        self.run((g + 2) * self.levels - self.done)
+        z, y, x, c = self.at
+
+        def body(zz, carry):
+            if g % 2 == 0:
+                self.y_copy(g, zz, x, False).wait_recv()
+                self.y_copy(g, zz, 1 - x, False).wait_recv()
+            else:
+                self.x_copy(g, zz, y, False).wait_recv()
+                self.x_copy(g, zz, 1 - y, False).wait_recv()
+            return carry
+
+        lax.fori_loop(0, self.levels, body, 0)
+        if g == 0:
+            self.local.wait()
+
+    def drain(self):
+        z, y, x, c = self.at
+
+        def group(g, carry):
+            def sent(zz, inner):
+                self.x_copy(g, zz, y, False).wait_send()
+                self.y_copy(g, zz, x, False).wait_send()
+
+                @pl.when(lax.rem(g, 2) == 0)
+                def _():
+                    self.y_copy(g, zz, 1 - x, False).wait_send()
+
+                @pl.when(lax.rem(g, 2) == 1)
+                def _():
+                    self.x_copy(g, zz, 1 - y, False).wait_send()
+
+                @pl.when((z < self.levels - 1) & (zz <= z))
+                def _():
+                    self.z_copy(g, zz, 1, False).wait_send()
+
+                @pl.when((z > 0) & (zz >= z))
+                def _():
+                    self.z_copy(g, zz, 0, False).wait_send()
+
+                return inner
+
+            return lax.fori_loop(0, self.levels, sent, carry)
+
+        lax.fori_loop(0, self.groups, group, 0)
+
+
+HALF = L // 2
+KEYS = 768
+HALF_FRAMES = FRAMES // 2
+BLOCK = 32
+
+
+def dot(a, b, dims):
+    return lax.dot_general(a, b, (dims, ((), ())), preferred_element_type=jnp.float32)
+
+
+NN, NT, TN = ((1,), (0,)), ((1,), (1,)), ((0,), (0,))
+
+
+def flat_panel(ref, mat, side):
+    return ref[mat, side].reshape(D, COLS)
+
+
+def rows_loop(count, body):
+    def run(i, carry):
+        body(pl.ds(pl.multiple_of(i * BLOCK, BLOCK), BLOCK), i)
+        return carry
+
+    lax.fori_loop(0, count // BLOCK, run, 0)
+
+
+def loop(count, body):
+    def run(i, carry):
+        body(i)
+        return carry
+
+    lax.fori_loop(0, count, run, 0)
+
+
+def normed_block(values):
+    centre = values - jnp.mean(values, axis=-1, keepdims=True)
+    spread = jnp.mean(centre * centre, axis=-1, keepdims=True)
+    scaled = lax.rsqrt(spread + 1e-05)
+    return centre * scaled, scaled
+
+
+def panels_row(ref, rows):
+    return jnp.concatenate([ref[j, rows, :].astype(jnp.float32) for j in range(4)], axis=1)
+
+
+def forward_kernel(levels, groups, fast, *refs):
+    f32, bf = jnp.float32, jnp.bfloat16
+    names = FORWARD_IN + (("pack",) if fast else ("norm_in", "bias_in")) + tuple(n for n, _, _ in FORWARD_OUT) + (
+        "wide", "x", "dy", "e", "norm", "bias", "a1", "a2", "a3", "h1", "h2", "qkv", "c1", "q2", "c2", "ek", "ev",
+        "lse1", "lse2", "z", "slope", "s", "p", "acc", "part", "got", "packs", "padrow", "outrows",
+        "in_sem", "swap_send", "swap_recv", "part_send", "part_recv", "pack_send", "pack_recv", "out_sem",
+    )
+    r = dict(zip(names, refs))
+    gather = Gather(levels, groups, r["shard"], r["wide"], refs[len(names):])
     z, y, x, c = place()
-    size = MATS // groups
-    greet_neighbours(levels)
-    local = pltpu.make_async_copy(shard, wide.at[:, x, z, y], own_sem)
-    local.start()
-
-    def block(g, xx, zz, yy):
-        return wide.at[pl.ds(g * size, size), xx, zz, yy]
-
-    def source(g, zz, own):
-        return shard.at[pl.ds(g * size, size)] if own else block(g, x, zz, y)
-
-    def z_copy(g, zz, target, own):
-        return pltpu.make_async_remote_copy(
-            source(g, zz, own), block(g, x, zz, y), z_send.at[g, zz, jnp.where(target > z, 1, 0)],
-            z_recv.at[g, zz], device_id=device(target, y, x, c), device_id_type=DT,
-        )
-
-    def x_copy(g, zz, yy, own):
-        src = source(g, zz, True) if own else block(g, x, zz, yy)
-        return pltpu.make_async_remote_copy(
-            src, block(g, x, zz, yy), x_send.at[g, zz, yy], x_recv.at[g, zz, yy],
-            device_id=device(z, y, 1 - x, c), device_id_type=DT,
-        )
-
-    def y_copy(g, zz, xx, own):
-        src = source(g, zz, True) if own else block(g, xx, zz, y)
-        return pltpu.make_async_remote_copy(
-            src, block(g, xx, zz, y), y_send.at[g, zz, xx], y_recv.at[g, zz, xx],
-            device_id=device(z, 1 - y, x, c), device_id_type=DT,
-        )
-
-    def spread(g, zz, own):
-        if g % 2 == 0:
-            x_copy(g, zz, y, own).start()
-            y_copy(g, zz, x, own).start()
-        else:
-            y_copy(g, zz, x, own).start()
-            x_copy(g, zz, y, own).start()
-
-    def first(g):
-        @pl.when(z < levels - 1)
+    dp = z * 2 + y
+    mate = (dp, x, 1 - c)
+    count = levels * 4
+    me = dp * 2 + x
+
+    def peer(i):
+        return (i // 2, lax.rem(i, 2), c)
+
+    bar = pltpu.get_barrier_semaphore()
+    loop(count - 1, lambda k: pl.semaphore_signal(
+        bar, inc=1, device_id=peer(lax.rem(me + k + 1, count)), device_id_type=DT))
+    pl.semaphore_signal(bar, inc=1, device_id=mate, device_id_type=DT)
+    pl.semaphore_wait(bar, count)
+
+    def remote(src, dst, send, recv, dev):
+        return pltpu.make_async_remote_copy(src, dst, send, recv, device_id=dev, device_id_type=DT)
+
+    inputs = (("tokens", "x"), ("frames", "e"), ("cotangent", "dy"))
+
+    def swap(k, slot):
+        src, dst = inputs[k]
+        return remote(r[src], r[dst].at[slot], r["swap_send"].at[k], r["swap_recv"].at[k], mate)
+
+    def local(k):
+        src, dst = inputs[k]
+        return pltpu.make_async_copy(r[src], r[dst].at[c], r["in_sem"].at[k])
+
+    if fast:
+        def pack_copy(k, slot):
+            return remote(r["pack"], r["packs"].at[slot], r["pack_send"].at[k], r["pack_recv"].at[slot],
+                          peer(lax.rem(me + k + 1, count)))
+
+        loop(count - 1, lambda k: pack_copy(k, me).start())
+        own_pack = pltpu.make_async_copy(r["pack"], r["packs"].at[me], r["in_sem"].at[3])
+        own_pack.start()
+    swap(0, c).start()
+    local(0).start()
+    gather.begin()
+    gather.run(1)
+    for k in (1, 2):
+        swap(k, c).start()
+        local(k).start()
+
+    def arrived(k):
+        local(k).wait()
+        swap(k, 1 - c).wait_recv()
+
+    outs = {}
+
+    def emit(out, scratch):
+        k = len(outs)
+        outs[out] = pltpu.make_async_copy(scratch, r[out], r["out_sem"].at[k])
+        outs[out].start()
+
+    if fast:
+        own_pack.wait()
+        loop(count - 1, lambda k: pack_copy(k, lax.rem(me + k + 1, count)).wait_recv())
+        for i in range(2 * levels):
+            for xx in range(2):
+                block = r["packs"][i * 2 + xx]
+                if xx == 0:
+                    r["norm"][:, i * 128 : (i + 1) * 128] = block
+                r["bias"][i * 2 + xx : i * 2 + xx + 1, 0:128] = block[9:10]
+                r["bias"][i * 2 + xx : i * 2 + xx + 1, 128:256] = block[10:11]
+    else:
+        r["norm"][...] = r["norm_in"][...]
+        r["bias"][...] = r["bias_in"][...]
+    emit("norm_out", r["norm"])
+
+    def norm_row(k):
+        return r["norm"][k : k + 1, :]
+
+    def bias_row(k, side):
+        return r["bias"][pl.ds(k * 2 + side, 1), :]
+
+    key = lax.broadcasted_iota(jnp.int32, (1, 2 * KEYS), 1)
+    real = lax.rem(key, KEYS) < HALF_FRAMES
+    r["padrow"][0:1, :] = jnp.where(real, 0.0, -1e30).astype(f32)
+    for i in range(3):
+        for side in range(2):
+            r["qkv"][i, side, L:512, :] = jnp.zeros((512 - L, COLS), bf)
+
+    arrived(0)
+
+    def ln1(half):
+        def body(rows, i):
+            normed, _ = normed_block(r["x"][half, rows, :].astype(f32))
+            out = (normed * norm_row(0) + norm_row(1)).astype(bf)
+            r["a1"][pl.ds(pl.multiple_of(half * HALF + i * BLOCK, BLOCK), BLOCK), :] = out
+
+        rows_loop(HALF, body)
+
+    ln1(0)
+    ln1(1)
+    emit("a1_out", r["a1"])
+    emit("x_out", r["x"])
+
+    def project_one(i, side):
+        bias = bias_row(0, side) if i == 0 else bias_row(1, side)
+        acc = dot(r["a1"][...], flat_panel(r["wide"], i, side), NN)
+        if i != 1:
+            acc = acc + bias
+        r["qkv"][i, side, 0:L, :] = acc.astype(bf)
+
+    gather.need(0)
+    for i in range(2):
+        loop(2, lambda side: project_one(i, side))
+    gather.need(1)
+    loop(2, lambda side: project_one(2, side))
+    emit("qkv_out", r["qkv"])
+
+    lane = lax.broadcasted_iota(jnp.int32, (1, 128), 1)
+    low = lane < HD
+
+    def attend(query, key_parts, values, width, causal, lse, ctx, tick):
+        def body(t):
+            side, half = t // 2, lax.rem(t, 2)
+            lanes = pl.ds(pl.multiple_of(half * 128, 128), 128)
+            q = query(side, lanes)
+            found = []
+            for sub in range(2):
+                mine = low if sub == 0 else jnp.logical_not(low)
+                qh = jnp.where(mine, q.astype(f32) * 0.125, 0.0).astype(bf)
+                for n, part in enumerate(key_parts(side, lanes)):
+                    r["s"][:, n * width : (n + 1) * width] = dot(qh, part, NT)
+                total = width * len(key_parts(side, lanes))
+
+                def rows_body(rows, i):
+                    s = r["s"][rows, 0:total]
+                    if causal:
+                        row = i * BLOCK + lax.broadcasted_iota(jnp.int32, (BLOCK, total), 0)
+                        col = lax.broadcasted_iota(jnp.int32, (BLOCK, total), 1)
+                        s = jnp.where(col <= row, s, -1e30)
+                    else:
+                        s = s + r["padrow"][0:1, 0:total]
+                    top = jnp.max(s, axis=-1, keepdims=True)
+                    e = jnp.exp(s - top)
+                    weight = jnp.sum(e, axis=-1, keepdims=True)
+                    r["p"][rows, 0:total] = (e * (1.0 / weight)).astype(bf)
+                    lse[t * 2 + sub, rows, :] = top + jnp.log(weight)
+
+                rows_loop(L, rows_body)
+                acc = None
+                for n, part in enumerate(values(side, lanes)):
+                    more = dot(r["p"][:, n * width : (n + 1) * width], part, NN)
+                    acc = more if acc is None else acc + more
+                found.append(acc)
+                tick(t * 2 + sub)
+            ctx[side, :, lanes] = jnp.where(low, found[0], found[1]).astype(bf)
+
+        loop(4, body)
+
+    attend(
+        lambda side, lanes: r["qkv"][0, side, 0:L, lanes],
+        lambda side, lanes: [r["qkv"][1, side, :, lanes]],
+        lambda side, lanes: [r["qkv"][2, side, :, lanes]],
+        512, True, r["lse1"], r["c1"], gather.reserve(8) if levels == 4 else (lambda i: None),
+    )
+    emit("lse1_out", r["lse1"])
+    emit("c1_out", r["c1"])
+
+    def collect(n, ctx, mat):
+        def body(j):
+            rows = pl.ds(pl.multiple_of(j * COLS, COLS), COLS)
+            acc = None
+            for side in range(2):
+                w = r["wide"].at[mat, side]
+                per = COLS // w.shape[2] if w.shape[2] < COLS else 1
+                tile = flat_rows(w, j)
+                more = dot(ctx[side], tile, NT)
+                acc = more if acc is None else acc + more
+            r["part"][n, j] = acc.astype(bf)
+            trade(n, j).start()
+
+        loop(4, body)
+
+    def flat_rows(w, j):
+        depth = w.shape[2]
+        if 2 * depth >= COLS:
+            per = COLS // (2 * depth)
+            return w[pl.ds(j * per, per)].reshape(COLS, COLS)
+        per = COLS // (2 * depth)
+        return w[pl.ds(j * per, per)].reshape(COLS, COLS)
+
+    def trade(n, j):
+        return remote(r["part"].at[n, j], r["got"].at[n, j], r["part_send"].at[n, j], r["part_recv"].at[n, j], mate)
+
+    def traded(n):
+        loop(4, lambda j: trade(n, j).wait_recv())
+
+    def residual(n, base, bias_k, out, gain_k, normed_out):
+        def body(rows, i):
+            v = base(rows, i) + norm_row(bias_k) + (panels_row(r["part"].at[n], rows) + panels_row(r["got"].at[n], rows))
+            out[rows, :] = v
+            normed, _ = normed_block(v)
+            normed_out[rows, :] = (normed * norm_row(gain_k) + norm_row(gain_k + 1)).astype(bf)
+
+        rows_loop(L, body)
+
+    def x_rows(rows, i):
+        half = i // (HALF // BLOCK)
+        inner = pl.ds(pl.multiple_of((i - half * (HALF // BLOCK)) * BLOCK, BLOCK), BLOCK)
+        return r["x"][half, inner, :].astype(f32)
+
+    collect(0, r["c1"], 3)
+    traded(0)
+    residual(0, x_rows, 6, r["h1"], 2, r["a2"])
+    emit("h1_out", r["h1"])
+    emit("a2_out", r["a2"])
+
+    gather.need(2)
+
+    def query_two(side):
+        acc = dot(r["a2"][...], flat_panel(r["wide"], 4, side), NN) + bias_row(2, side)
+        r["q2"][side] = acc.astype(bf)
+
+    loop(2, query_two)
+    emit("q2_out", r["q2"])
+    arrived(1)
+    emit("e_out", r["e"])
+
+    def frame_keys(t):
+        side, half = t // 2, lax.rem(t, 2)
+        r["ek"][side, half] = dot(r["e"][half], flat_panel(r["wide"], 5, side), NN).astype(bf)
+
+    loop(4, frame_keys)
+    emit("ek_out", r["ek"])
+    gather.need(3)
+
+    def frame_values(t):
+        side, half = t // 2, lax.rem(t, 2)
+        acc = dot(r["e"][half], flat_panel(r["wide"], 6, side), NN) + bias_row(3, side)
+        r["ev"][side, half] = acc.astype(bf)
+
+    loop(4, frame_values)
+    emit("ev_out", r["ev"])
+    attend(
+        lambda side, lanes: r["q2"][side, :, lanes],
+        lambda side, lanes: [r["ek"][side, half, :, lanes] for half in range(2)],
+        lambda side, lanes: [r["ev"][side, half, :, lanes] for half in range(2)],
+        KEYS, False, r["lse2"], r["c2"], gather.reserve(8) if levels == 4 else (lambda i: None),
+    )
+    emit("lse2_out", r["lse2"])
+    emit("c2_out", r["c2"])
+    collect(1, r["c2"], 7)
+    traded(1)
+    residual(1, lambda rows, i: r["h1"][rows, :], 7, r["h2"], 4, r["a3"])
+    emit("h2_out", r["h2"])
+    emit("a3_out", r["a3"])
+    arrived(2)
+    emit("dy_out", r["dy"])
+
+    def hidden(t):
+        m, side = t // 2, lax.rem(t, 2)
+        u = dot(r["a3"][...], flat_panel(r["wide"], 8 + m, side), NN) + bias_row(4 + m, side)
+        half = 0.5 * (1.0 + lax.erf(u * 0.7071067811865476))
+        r["z"][t] = (u * half).astype(bf)
+        r["slope"][t] = (half + u * jnp.exp(-0.5 * u * u) * 0.3989422804014327).astype(bf)
+
+    def result(t):
+        m, side = t // 2, lax.rem(t, 2)
+
+        def tile(j):
+            cols = pl.ds(pl.multiple_of(j * COLS, COLS), COLS)
+            more = dot(r["z"][t], flat_rows(r["wide"].at[12 + m, side], j), NT)
+
+            @pl.when(t == 0)
+            def _():
+                r["acc"][:, cols] = more
+
+            @pl.when(t > 0)
+            def _():
+                r["acc"][:, cols] += more
+
+        loop(4, tile)
+
+    per = groups // 4
+    mats = MATS // groups
+    for k in range(max(1, groups // 4)):
+        gather.need(groups // 2 + k)
+        span = 8 // max(1, groups // 4)
+        loop(span, lambda t: hidden(k * span + t))
+    emit("z_out", r["z"])
+    emit("slope_out", r["slope"])
+    for k in range(max(1, groups // 4)):
+        gather.need(groups * 3 // 4 + k if groups >= 4 else groups - 1)
+        span = 8 // max(1, groups // 4)
+        loop(span, lambda t: result(k * span + t))
+
+    emit("wide_out", r["wide"])
+
+    for half in range(2):
+        @pl.when(c == half)
         def _():
-            z_copy(g, z, z + 1, True).start()
-
-        @pl.when(z > 0)
-        def _():
-            z_copy(g, z, z - 1, True).start()
-
-        spread(g, z, True)
-        for d in range(1, levels):
-            @pl.when(z - d >= 0)
-            def _():
-                z_copy(g, z - d, z - 1, False).wait_recv()
-
-                @pl.when(z < levels - 1)
-                def _():
-                    z_copy(g, z - d, z + 1, False).start()
-
-                spread(g, z - d, False)
-
-            @pl.when(z + d < levels)
-            def _():
-                z_copy(g, z + d, z + 1, False).wait_recv()
-
-                @pl.when(z > 0)
-                def _():
-                    z_copy(g, z + d, z - 1, False).start()
-
-                spread(g, z + d, False)
-
-    def order(body):
-        def run(d, carry):
-            @pl.when(z - d >= 0)
-            def _():
-                body(z - d)
-
-            if True:
-                @pl.when((z + d < levels) & (d > 0))
-                def _():
-                    body(z + d)
-
-            return carry
-
-        lax.fori_loop(0, levels, run, 0)
-
-    def second(g):
-        def relay(zz):
-            if g % 2 == 0:
-                x_copy(g, zz, y, False).wait_recv()
-                y_copy(g, zz, 1 - x, False).start()
-            else:
-                y_copy(g, zz, x, False).wait_recv()
-                x_copy(g, zz, 1 - y, False).start()
-
-        order(relay)
-
-    def third(g):
-        def finish(zz):
-            if g % 2 == 0:
-                y_copy(g, zz, x, False).wait_recv()
-                y_copy(g, zz, 1 - x, False).wait_recv()
-            else:
-                x_copy(g, zz, y, False).wait_recv()
-                x_copy(g, zz, 1 - y, False).wait_recv()
-
-        order(finish)
-
-    def drain(g):
-        def sent(zz):
-            if g % 2 == 0:
-                x_copy(g, zz, y, False).wait_send()
-                y_copy(g, zz, x, False).wait_send()
-                y_copy(g, zz, 1 - x, False).wait_send()
-            else:
-                y_copy(g, zz, x, False).wait_send()
-                x_copy(g, zz, y, False).wait_send()
-                x_copy(g, zz, 1 - y, False).wait_send()
-
-            @pl.when((z < levels - 1) & (zz <= z))
-            def _():
-                z_copy(g, zz, z + 1, False).wait_send()
-
-            @pl.when((z > 0) & (zz >= z))
-            def _():
-                z_copy(g, zz, z - 1, False).wait_send()
-
-        order(sent)
-
-    for step in range(groups + 1):
-        if step < groups:
-            first(step)
-        if step >= 1:
-            second(step - 1)
-    for g in range(groups):
-        third(g)
-        drain(g)
-    local.wait()
-
-
-def gather_weights(shard, shards):
-    rows = shard.shape[1]
-    levels = shards // 2
-    groups = 8 if levels <= 4 else 2
+            far = (1 - half) * HALF
+
+            def body(j):
+                cols = pl.ds(pl.multiple_of(j * COLS, COLS), COLS)
+                r["part"][2, j, 0:HALF, :] = r["acc"][far : far + HALF, cols].astype(bf)
+
+            loop(4, body)
+
+    last = remote(
+        r["part"].at[2, :, 0:HALF], r["got"].at[2, :, 0:HALF], r["part_send"].at[2, 0], r["part_recv"].at[2, 0], mate
+    )
+    last.start()
+    last.wait_recv()
+
+    def finish(rows, i):
+        here = pl.ds(pl.multiple_of(c * HALF + i * BLOCK, BLOCK), BLOCK)
+        own = r["acc"][here, :].astype(bf).astype(f32)
+        v = r["h2"][here, :] + norm_row(8) + (own + panels_row(r["got"].at[2], rows))
+        r["outrows"][rows, :] = v.astype(bf)
+
+    rows_loop(HALF, finish)
+    emit("layer_out", r["outrows"])
+
+    for k in range(3):
+        swap(k, c).wait_send()
+    if fast:
+        loop(count - 1, lambda k: pack_copy(k, me).wait_send())
+    for n in range(2):
+        loop(4, lambda j: trade(n, j).wait_send())
+    last.wait_send()
+    gather.drain()
+    for copy in outs.values():
+        copy.wait()
+
+
+FORWARD_IN = ("shard", "tokens", "frames", "cotangent")
+FORWARD_OUT = (
+    ("layer_out", (HALF, D), jnp.bfloat16), ("norm_out", (16, D), jnp.float32),
+    ("a1_out", (L, D), jnp.bfloat16), ("x_out", (2, HALF, D), jnp.bfloat16),
+    ("qkv_out", (3, 2, 512, COLS), jnp.bfloat16), ("lse1_out", (8, L, 1), jnp.float32),
+    ("c1_out", (2, L, COLS), jnp.bfloat16), ("h1_out", (L, D), jnp.float32), ("a2_out", (L, D), jnp.bfloat16),
+    ("q2_out", (2, L, COLS), jnp.bfloat16), ("e_out", (2, KEYS, D), jnp.bfloat16),
+    ("ek_out", (2, 2, KEYS, COLS), jnp.bfloat16), ("ev_out", (2, 2, KEYS, COLS), jnp.bfloat16),
+    ("lse2_out", (8, L, 1), jnp.float32), ("c2_out", (2, L, COLS), jnp.bfloat16),
+    ("h2_out", (L, D), jnp.float32), ("a3_out", (L, D), jnp.bfloat16), ("dy_out", (2, HALF, D), jnp.bfloat16),
+    ("z_out", (8, L, COLS), jnp.bfloat16), ("slope_out", (8, L, COLS), jnp.bfloat16), ("wide_out", None, jnp.bfloat16),
+)
+
+
+def forward(shard, tokens, frames, cotangent, small, shards):
+    levels, rows = shards // 2, D // shards
+    groups = 8 if levels <= 4 else 4
+    fast = len(small) == 1
+    f32, bf = jnp.float32, jnp.bfloat16
     sem = pltpu.SemaphoreType.DMA
-    wide = pl.pallas_call(
-        partial(gather_kernel, levels, groups),
-        out_shape=jax.ShapeDtypeStruct((MATS, 2, levels, 2, rows, COLS), jnp.bfloat16),
-        in_specs=[pl.BlockSpec(memory_space=pltpu.VMEM)],
-        out_specs=pl.BlockSpec(memory_space=pl.ANY),
-        scratch_shapes=[
-            sem, sem((groups, levels, 2)), sem((groups, levels)), sem((groups, levels, 2)),
-            sem((groups, levels, 2)), sem((groups, levels, 2)), sem((groups, levels, 2)),
-        ],
-        compiler_params=pltpu.CompilerParams(collective_id=0, has_side_effects=True),
-        name="gather_weights",
-    )(shard)
-    return wide.reshape(MATS, 2, D, COLS)
+    vm, hbm = pl.BlockSpec(memory_space=pltpu.VMEM), pl.BlockSpec(memory_space=pl.ANY)
+    wide = (MATS, 2, levels, 2, rows, COLS)
+    shapes = [(n, wide if s is None else s, t) for n, s, t in FORWARD_OUT]
+    peers = shards * 2
+    scratch = [
+        pltpu.VMEM(wide, bf), pltpu.VMEM((2, HALF, D), bf), pltpu.VMEM((2, HALF, D), bf), pltpu.VMEM((2, KEYS, D), bf),
+        pltpu.VMEM((16, D), f32), pltpu.VMEM((16, COLS), f32),
+        pltpu.VMEM((L, D), bf), pltpu.VMEM((L, D), bf), pltpu.VMEM((L, D), bf),
+        pltpu.VMEM((L, D), f32), pltpu.VMEM((L, D), f32),
+        pltpu.VMEM((3, 2, 512, COLS), bf), pltpu.VMEM((2, L, COLS), bf), pltpu.VMEM((2, L, COLS), bf),
+        pltpu.VMEM((2, L, COLS), bf), pltpu.VMEM((2, 2, KEYS, COLS), bf), pltpu.VMEM((2, 2, KEYS, COLS), bf),
+        pltpu.VMEM((8, L, 1), f32), pltpu.VMEM((8, L, 1), f32),
+        pltpu.VMEM((8, L, COLS), bf), pltpu.VMEM((8, L, COLS), bf),
+        pltpu.VMEM((L, 2 * KEYS), f32), pltpu.VMEM((L, 2 * KEYS), bf), pltpu.VMEM((L, D), f32),
+        pltpu.VMEM((3, 4, L, COLS), bf), pltpu.VMEM((3, 4, L, COLS), bf),
+        pltpu.VMEM((peers, 16, 128) if fast else (1, 16, 128), f32), pltpu.VMEM((8, 2 * KEYS), f32),
+        pltpu.VMEM((HALF, D), bf),
+        sem((4,)), sem((3,)), sem((3,)), sem((3, 4)), sem((3, 4)), sem((peers,)), sem((peers,)),
+        sem((len(FORWARD_OUT),)),
+    ]
+    outs = pl.pallas_call(
+        partial(forward_kernel, levels, groups, fast),
+        out_shape=[jax.ShapeDtypeStruct(s, t) for _, s, t in shapes],
+        in_specs=[vm, hbm, hbm, hbm] + [vm] * len(small),
+        out_specs=[hbm] * len(shapes),
+        scratch_shapes=scratch + Gather.semaphores(levels, groups),
+        compiler_params=pltpu.CompilerParams(
+            collective_id=0, has_side_effects=True, vmem_limit_bytes=63 * 2**20
+        ),
+        name="forward",
+    )(shard, tokens, frames, cotangent, *small)
+    return {n.removesuffix("_out") if n != "layer_out" else n: v for (n, _, _), v in zip(shapes, outs)}
 
 
 def scatter_kernel(levels, groups, part, out, even, odd, two, line, s1, r1, s2, r2, s3, r3):
@@ -596,21 +1041,26 @@
     own_unit = unit_bias.astype(f32)
     own_norm = norm_bias.astype(f32)
 
-    pack = jnp.concatenate([norm_bias.reshape(-1), unit_bias.reshape(-1)])
-    pack = jnp.pad(pack, (0, 2048 - pack.shape[0])).reshape(16, 128)
-    packs = small_exchange(pack, shards, False, False, 2).reshape(shards, 2, 2048)
-    norm_rows = (
-        packs[:, 0, : 9 * rows].reshape(shards, 9, rows).transpose(1, 0, 2).reshape(9, D).astype(f32)
-    )
-    unit_all = packs[:, :, 9 * rows : 9 * rows + 4 * unit_cols].reshape(shards, 2, 4, unit_cols)
-    bias_rows = (
-        unit_all.transpose(1, 2, 0, 3).reshape(8, 8, HD).transpose(1, 0, 2).reshape(8, 512).astype(f32)
-    )
+    if rows == 128:
+        pack = jnp.concatenate([norm_bias.astype(f32), unit_bias.astype(f32).reshape(2, 128)])
+        small = (jnp.pad(pack, ((0, 5), (0, 0))),)
+    else:
+        pack = jnp.concatenate([norm_bias.reshape(-1), unit_bias.reshape(-1)])
+        pack = jnp.pad(pack, (0, 2048 - pack.shape[0])).reshape(16, 128)
+        packs = small_exchange(pack, shards, False, False, 2).reshape(shards, 2, 2048)
+        norm_rows = packs[:, 0, : 9 * rows].reshape(shards, 9, rows).transpose(1, 0, 2).reshape(9, D).astype(f32)
+        unit_all = packs[:, :, 9 * rows : 9 * rows + 4 * unit_cols].reshape(shards, 2, 4, unit_cols)
+        bias_rows = (
+            unit_all.transpose(1, 2, 0, 3).reshape(2, 4, 8, HD).transpose(2, 0, 1, 3).reshape(16, COLS).astype(f32)
+        )
+        small = (jnp.pad(norm_rows, ((0, 7), (0, 0))), bias_rows)
 
     shard = jnp.concatenate(
         [attention_weights.reshape(8, rows, COLS), dense_weights.transpose(0, 2, 1, 3).reshape(8, rows, COLS)]
     )
-    wide = gather_weights(shard, shards)
+    kept = forward(shard, tokens, jnp.pad(frames, ((0, KEYS - HALF_FRAMES), (0, 0))), cotangent, small, shards)
+    wide = kept["wide"].reshape(MATS, 2, D, COLS)
+    norm_rows = kept["norm"]
 
     def project(left, mat):
         return jnp.einsum("rd,xde->rxe", left, wide[mat], preferred_element_type=f32).reshape(-1, 512)
@@ -630,41 +1080,33 @@
     def by_head(flat):
         return flat.reshape(-1, 8, HD)
 
-    row_data = pair_gather(tokens, 3).reshape(L, D).astype(f32)
-    out_grad_low = pair_gather(cotangent, 4).reshape(L, D)
-    frame_rows = pair_gather(frames, 5).reshape(FRAMES, D)
-
-    first_in, first_normed, first_scale = norm_forward(row_data, norm_rows[0], norm_rows[1])
-    first_in = first_in.astype(bf)
-    self_query = (project(first_in, 0) + bias_rows[0]).astype(bf)
-    self_keys = project(first_in, 1).astype(bf)
-    self_values = (project(first_in, 2) + bias_rows[1]).astype(bf)
-    self_context, self_total = clip_forward(
-        True, by_head(self_query), by_head(self_keys), by_head(self_values)
-    )
-    self_flat = self_context.reshape(L, 512)
-    hidden_one = row_data + norm_rows[6] + pair_sum(collect(self_flat, 3), 6)
-    second_in, second_normed, second_scale = norm_forward(hidden_one, norm_rows[2], norm_rows[3])
-    second_in = second_in.astype(bf)
-    cross_query = (project(second_in, 4) + bias_rows[2]).astype(bf)
-    cross_keys = project(frame_rows, 5).astype(bf)
-    cross_values = (project(frame_rows, 6) + bias_rows[3]).astype(bf)
-    cross_context, cross_total = clip_forward(
-        False, by_head(cross_query), by_head(cross_keys), by_head(cross_values)
-    )
-    cross_flat = cross_context.reshape(L, 512)
-    hidden_two = hidden_one + norm_rows[7] + pair_sum(collect(cross_flat, 7), 7)
-    third_in, third_normed, third_scale = norm_forward(hidden_two, norm_rows[4], norm_rows[5])
-    third_in = third_in.astype(bf)
-    before = project_hidden(third_in, 8) + bias_rows[4:8].reshape(2048)
-    activated = gelu_value(before).astype(bf)
-    result_rows = hidden_two + norm_rows[8] + pair_sum(collect_hidden(activated, 12), 8)
-    layer_out = lax.dynamic_slice_in_dim(result_rows, c * (L // 2), L // 2, 0).astype(bf)
+    def joined(panels):
+        return panels.transpose(1, 0, 2).reshape(panels.shape[1], -1)
+
+    def unpadded(halves):
+        return halves[:, :HALF_FRAMES].reshape(FRAMES, -1)
+
+    row_data = kept["x"].reshape(L, D).astype(f32)
+    out_grad_low = kept["dy"].reshape(L, D)
+    frame_rows = unpadded(kept["e"])
+    first_in, second_in, third_in = kept["a1"], kept["a2"], kept["a3"]
+    _, first_normed, first_scale = norm_forward(row_data, norm_rows[0], norm_rows[1])
+    _, second_normed, second_scale = norm_forward(kept["h1"], norm_rows[2], norm_rows[3])
+    _, third_normed, third_scale = norm_forward(kept["h2"], norm_rows[4], norm_rows[5])
+    self_query, self_keys, self_values = (joined(kept["qkv"][i, :, :L]) for i in range(3))
+    self_total, cross_total = kept["lse1"][..., 0], kept["lse2"][..., 0]
+    self_flat, cross_flat, cross_query = joined(kept["c1"]), joined(kept["c2"]), joined(kept["q2"])
+    cross_keys, cross_values = (
+        jnp.concatenate([unpadded(kept[n][side]) for side in range(2)], axis=1) for n in ("ek", "ev")
+    )
+    activated = joined(kept["z"])
+    slope = joined(kept["slope"]).astype(f32)
+    layer_out = kept["layer_out"]
 
     out_grad = out_grad_low.astype(f32)
     act_grad = project_hidden(out_grad_low, 12)
     down_grad = weight_grad(out_grad_low, activated)
-    before_grad = (act_grad * gelu_slope(before)).astype(bf)
+    before_grad = (act_grad * slope).astype(bf)
     hidden_bias_grad = jnp.sum(before_grad, axis=0, dtype=f32)
     up_grad = weight_grad(third_in, before_grad)
     third_back = pair_sum(collect_hidden(before_grad, 8), 9)

time: 801 us -> 765 us (0.955)
  matrix products: 153 us -> 119 us
  Pallas kernels: 431 us -> 465 us
  other arithmetic: 91.1 us -> 64.2 us
    pallas_call x1, Pallas kernels: 150 us -> 222 us  [forward(): pl.pallas_call(partial(forward_kernel, levels, groups, fast), out_shape=[...]
    pallas_call x10 -> x4, Pallas kernels: 53.8 us -> 25 us  [pair_gather(): pl.pallas_call(pair_kernel, out_shape=jax.ShapeDtypeStruct((2, *src.shape...]
    dot_general x9 -> x0, local copies, waits for them, and re-layouts: 27.2 us -> none  [the longest x7 16.2 us: project(): jnp.einsum('rd,xde->rxe', left, wide[mat], preferred_element_type=f32)]
    dot_general x8 -> x2, matrix products: 24 us -> 4.35 us  [project(): jnp.einsum('rd,xde->rxe', left, wide[mat], preferred_element_type=f32)]
    slice x2 -> x10, local copies, waits for them, and re-layouts: 0.03 us -> 16 us  [the longest x9 15 us: unpadded(): return halves[:, :HALF_FRAMES].reshape(FRAMES, -1)]
    dot_general x2, matrix products: 5.93 us -> 19.9 us  [clip_scores(): jnp.einsum('qhd,khd->hqk', queries, key_rows, preferred_element_type=jnp....]
    dot_general x2 -> x0, matrix products: 11.7 us -> none  [clip_forward(): jnp.einsum('hqk,khd->qhd', weights, values, preferred_element_type=jnp.fl...]
    dot_general x2 -> x1, matrix products: 12.2 us -> 2.12 us  [project_hidden(): jnp.einsum('rd,mxde->rmxe', left, wide[base:base + 4], preferred_element_...]
where the time goes in v2:
time: 765 us; the launch traced here: 757 us
  Pallas kernels  465 us (61%)
  matrix products  119 us (16%)
  local copies, waits for them, and re-layouts  107 us (14%)
  other arithmetic  64.2 us (8%)
    pallas_call x1, Pallas kernels, forward(): pl.pallas_call(partial(forward_kernel, levels, groups, fast), out_shape=[...  222 us
    pallas_call x1, Pallas kernels, scatter_grads(): pl.pallas_call(partial(kernel, levels, groups), out_shape=jax.ShapeDtypeS...  200 us
    dot_general x10, matrix products, weight_grad(): jnp.einsum('rd,rme->mde', left, right.reshape(right.shape[0], -1, COLS),...  28.7 us
    pallas_call x4, Pallas kernels, pair_gather(): pl.pallas_call(pair_kernel, out_shape=jax.ShapeDtypeStruct((2, *src.shape...  25 us
    concatenate x1, local copies, waits for them, and re-layouts, shards_fn(): jnp.concatenate([weight_grad(first_in, self_qflat), weight_grad(first_in,...  22.5 us
    dot_general x2, matrix products, clip_scores(): jnp.einsum('qhd,khd->hqk', queries, key_rows, preferred_element_type=jnp....  19.9 us
    pallas_call x2, Pallas kernels, small_exchange(): pl.pallas_call(partial(small_kernel, shards, every, scatter), out_shape=j...  18.7 us
    dot_general x2, matrix products, clip_backward(): jnp.einsum('qhd,khd->hqk', context_grad, values, preferred_element_type=j...  17.3 us

profile of v2, /device:TPU:0, one launch (start us, length us, event | category | flops | bytes accessed | tf_op | source)
XLA Modules:
  0.0 757.1 jit_solution(11089829494589783818)
XLA Ops:
  0.7 2.8 pad.16.refs_2_
  5.3 221.7 %forward.1 = (bf16[224,1024]{1,0:T(8,128)(2,1)}, f32[16,1024]{1,0:T(8,128)}, bf16[448,1024]{1,0:T(8,128)(2,1)}, bf16[2,224,1024]{2,1,0:T(8,128)(2,1)}, bf16[3,2,...) custom-call(bf16[16,128,256]{2,1,0:T(8,128)(2,1)} %pad_maximum_fusio, ...), custom_call_target="tpu_custom_call" | custom-call | tf_op jit(solution)/shard_map/forward/pallas_call | solution.py:643
  227.0 5.9 fusion.81
  232.9 6.4 copy.99
  244.2 2.3 reshape.327
  246.5 5.8 bitcast_convert_fusion.src
  252.3 5.0 pair_gather_9.1
  261.4 5.9 fusion.80
  270.8 2.5 slice_bitcast_fusion.1
  274.2 2.4 copy.107
  280.2 2.6 copy.108
  284.3 11.9 %fusion.22 = f32[8,448,1500]{2,1,0:T(8,128)} fusion(bf16[448,8,64]{0,2,1:T(8,128)(2,1)S(1)} %bitcast.294, bf16[1500,4,64]{0,2,1:T(8,128)(2,1)} %concatenate.52, bf16[1500,4,64]{0,2,1:T(8,128)(2,1)} %concatenate.51), kind=kOutput, calls=%fused_computation.61 | convolution fusion | flops 688896000 | bytes 23498752 | tf_op jit(solution)/shard_map/qhd,khd->hqk/dot_general | solution.py:989
  302.0 3.1 copy.103
  305.1 3.2 concatenate.49
  313.7 14.7 %multiply_reduce_fusion = (f32[8,448]{1,0:T(8,128)S(1)}, f32[8,448,1500]{2,1,0:T(8,128)}) fusion(f32[8,448,1500]{2,1,0:T(8,128)} %fusion.22, f32[8,448]{1,0:T(8,128)S(1)} %reduce.10, bf16[448,8,64]{0,2,1:T(8,128)(2,1)} %bitcast.298, bf16[1500,8,64]{0,2,1:T(8,128)(2,1)S(1)} %constant_dynamic-update-slice_fusion), kind=kOutput, calls=%fused_computation.1 | convolution fusion | flops 709628416 | bytes 45031424 | tf_op jit(solution)/shard_map/qhd,khd->hqk/dot_general | solution.py:963
  328.4 14.7 %multiply_convert_fusion = bf16[8,448,1500]{2,1,0:T(8,128)(2,1)S(1)} fusion(f32[8,448,1500]{2,1,0:T(8,128)} %get-tuple-element.129, f32[8,448,1500]{2,1,0:T(8,128)} %fusion.22, f32[8,448]{1,0:T(8,128)S(1)} %get-tuple-element.128), kind=kLoop, calls=%fused_computation | loop fusion | flops 16128000 | bytes 53774336 | tf_op jit(solution)/shard_map/convert_element_type | solution.py:990
  343.1 3.3 convert_reduce_fusion.4
  349.7 5.0 pair_gather_11.1
  359.0 4.4 fusion.15
  365.5 2.3 copy.112
  367.7 2.5 convolution_convert_fusion.8
  371.2 2.3 slice_bitcast_fusion.6
  375.7 5.1 fusion.85
  383.0 5.3 convert_reduce_fusion.5
  390.3 5.4 multiply_reduce_fusion.1
  395.9 2.4 multiply_convert_fusion.1
  404.9 4.9 pair_gather_12.1
  409.8 4.0 fusion.74
  417.2 10.5 %convert_reduce_fusion.2 = (f32[8,64]{1,0:T(8,128)S(1)}, bf16[8,64,1500]{2,1,0:T(8,128)(2,1)}) fusion(bf16[448,8,64]{0,2,1:T(8,128)(2,1)S(1)} %bitcast.295, f32[8,448,1500]{2,1,0:T(8,128)} %get-tuple-element.129), kind=kOutput, calls=%fused_computation.20 | convolution fusion | flops 695807488 | bytes 23500800 | tf_op jit(solution)/shard_map/hqk,qhd->khd/dot_general | solution.py:986
  428.6 9.2 %small_exchange_13.1 = f32[16,16,128]{2,1,0:T(8,128)} custom-call(f32[16,16,128]{2,1,0:T(8,128)} %reshape.335.src), custom_call_target="tpu_custom_call" | custom-call | tf_op jit(solution)/shard_map/small_exchange_13/pallas_call | solution.py:884
  440.4 3.0 fusion.35
  450.3 7.5 fusion.5
  459.7 4.1 reshape.353
  463.8 5.3 fusion.31
  469.1 2.9 fusion.33
  473.9 4.4 bitcast_dynamic-update-slice_fusion.1
  478.2 4.6 bitcast_dynamic-update-slice_fusion
  482.8 22.5 %copy.130 = bf16[32,1024,256]{2,1,0:T(8,128)(2,1)} copy(bf16[32,1024,256]{1,2,0:T(8,128)(2,1)} %bitcast_dynamic-update-slice_fusion) | data formatting | bytes 33554432 | tf_op jit(solution)/shard_map/concatenate | solution.py:1153
  505.3 200.1 %scatter_grads.1 = f32[16,128,256]{2,1,0:T(8,128)} custom-call(bf16[16,2,4,2,128,256]{5,4,3,2,1,0:T(8,128)(2,1)} %bitcast.290), custom_call_target="tpu_custom_call" | custom-call | tf_op jit(solution)/shard_map/scatter_grads/pallas_call | solution.py:810
  707.7 3.7 multiply_reduce_fusion.8
  711.4 2.5 multiply_reduce_fusion.9
  714.8 9.6 %small_exchange_14.1 = f32[32,8,128]{2,1,0:T(8,128)} custom-call(f32[8,128]{1,0:T(8,128)} %pad_bitcast_fusion.src), custom_call_target="tpu_custom_call" | custom-call | tf_op jit(solution)/shard_map/small_exchange_14/pallas_call | solution.py:884
  728.7 2.5 broadcast_multiply_fusion.1
  731.2 3.2 fusion.88
  734.4 3.6 fusion.2.src
  738.0 10.1 %pair_gather_10.1 = bf16[2,1500,1024]{2,1,0:T(8,128)(2,1)} custom-call(bf16[1500,1024]{1,0:T(8,128)(2,1)} %fusion.2.src), custom_call_target="tpu_custom_call" | custom-call | tf_op jit(solution)/shard_map/pair_gather_10/pallas_call | solution.py:916
  748.1 4.8 convert_reduce_fusion
  753.2 2.7 dynamic-slice_add_fusion
  (253 shorter events, 80.9 us)
Async XLA Ops:
  0.7 2.8 copy-start.30
  0.7 2.9 copy-start.32
  232.9 6.4 copy-start.40
  239.7 2.2 copy-start.20
  239.7 2.4 copy-start.23
  244.2 2.3 copy-start.38
  252.3 5.0 copy-start.4
  270.8 13.5 %copy-start.12 = (bf16[448,512]{0,1:T(8,128)(2,1)}, bf16[448,512]{0,1:T(8,128)(2,1)S(1)}, u32[]{:S(2)}) copy-start(bf16[448,512]{0,1:T(8,128)(2,1)S(1)} %copy.106) | copy-start | bytes 1376260
  284.3 11.9 %copy-start.41 = (bf16[2,2,768,256]{3,2,1,0:T(8,128)(2,1)S(1)}, bf16[2,2,768,256]{3,2,1,0:T(8,128)(2,1)}, u32[]{:S(2)}) copy-start(bf16[2,2,768,256]{3,2,1,0:T(8,128)(2,1)} %get-tuple-element.49) | copy-start | bytes 4718596
  343.1 4.1 copy-start
  343.1 4.8 copy-start.46
  349.7 5.0 copy-start.11
  359.0 4.4 copy-start.1
  359.0 4.4 copy-start.2
  390.3 5.4 slice-start
  390.3 5.6 slice-start.1
  395.8 2.4 copy-start.16
  399.1 2.4 copy-start.36
  409.8 4.1 copy-start.10
  413.9 2.0 copy-start.7
  417.2 21.7 %copy-start.58 = (f32[4,64]{1,0:T(4,128)S(1)}, f32[4,64]{1,0:T(4,128)}, u32[]{:S(2)}) copy-start(f32[4,64]{1,0:T(4,128)} %param.28) | copy-start | bytes 3076
  417.2 21.7 %copy-start.59 = (f32[4,64]{1,0:T(4,128)S(1)}, f32[4,64]{1,0:T(4,128)}, u32[]{:S(2)}) copy-start(f32[4,64]{1,0:T(4,128)} %param.24) | copy-start | bytes 3076
  417.2 22.4 %copy-start.54 = (f32[9,128]{1,0:T(8,128)S(1)}, f32[9,128]{1,0:T(8,128)}, u32[]{:S(2)}) copy-start(f32[9,128]{1,0:T(8,128)} %param.29) | copy-start | bytes 13828
  417.2 22.4 %copy-start.55 = (f32[9,128]{1,0:T(8,128)S(1)}, f32[9,128]{1,0:T(8,128)}, u32[]{:S(2)}) copy-start(f32[9,128]{1,0:T(8,128)} %param.25) | copy-start | bytes 13828
  417.2 23.2 %copy-start.37 = (bf16[8,64,448]{2,1,0:T(8,128)(2,1)S(1)}, bf16[8,64,448]{2,1,0:T(8,128)(2,1)}, u32[]{:S(2)}) copy-start(bf16[8,64,448]{2,1,0:T(8,128)(2,1)} %copy-done.36) | copy-start | bytes 1376260
  438.7 4.6 copy-start.35
  438.9 6.3 copy-start.56
  440.4 3.0 copy-start.63
  446.8 1.8 copy-start.48
  446.8 1.8 copy-start.62
  450.3 7.5 copy-start.28
  463.8 5.3 copy-start.14
  463.8 5.3 copy-start.27
  469.1 2.9 copy-start.50
  472.0 1.8 copy-start.61
  473.8 4.4 copy-start.25
  473.8 4.4 copy-start.60
  705.4 1.9 copy-start.31
  705.4 2.0 copy-start.42
  705.4 2.3 copy-start.43
  707.3 4.1 copy-start.22
  707.7 3.7 copy-start.33
  707.7 3.7 copy-start.44
  707.7 3.7 copy-start.45
  728.6 2.5 copy-start.29
  731.2 3.2 copy-start.17
  748.1 5.1 copy-start.9
  753.2 2.7 copy-start.52
  (18 other events, 25.0 us)

commit v3 on v2

--- a/solution.py
+++ b/solution.py
@@ -232,6 +232,11 @@
 
 def flat_panel(ref, mat, side):
     return ref[mat, side].reshape(D, COLS)
+
+
+def flat_rows(panel, j):
+    per = COLS // (2 * panel.shape[2])
+    return panel[pl.ds(j * per, per)].reshape(COLS, COLS)
 
 
 def rows_loop(count, body):
@@ -410,7 +415,7 @@
                     e = jnp.exp(s - top)
                     weight = jnp.sum(e, axis=-1, keepdims=True)
                     r["p"][rows, 0:total] = (e * (1.0 / weight)).astype(bf)
-                    lse[t * 2 + sub, rows, :] = top + jnp.log(weight)
+                    lse[rows, :] = jnp.where(lane == t * 2 + sub, top + jnp.log(weight), lse[rows, :])
 
                 rows_loop(L, rows_body)
                 acc = None
@@ -437,23 +442,12 @@
             rows = pl.ds(pl.multiple_of(j * COLS, COLS), COLS)
             acc = None
             for side in range(2):
-                w = r["wide"].at[mat, side]
-                per = COLS // w.shape[2] if w.shape[2] < COLS else 1
-                tile = flat_rows(w, j)
-                more = dot(ctx[side], tile, NT)
+                more = dot(ctx[side], flat_rows(r["wide"].at[mat, side], j), NT)
                 acc = more if acc is None else acc + more
             r["part"][n, j] = acc.astype(bf)
             trade(n, j).start()
 
         loop(4, body)
-
-    def flat_rows(w, j):
-        depth = w.shape[2]
-        if 2 * depth >= COLS:
-            per = COLS // (2 * depth)
-            return w[pl.ds(j * per, per)].reshape(COLS, COLS)
-        per = COLS // (2 * depth)
-        return w[pl.ds(j * per, per)].reshape(COLS, COLS)
 
     def trade(n, j):
         return remote(r["part"].at[n, j], r["got"].at[n, j], r["part_send"].at[n, j], r["part_recv"].at[n, j], mate)
@@ -604,11 +598,11 @@
 FORWARD_OUT = (
     ("layer_out", (HALF, D), jnp.bfloat16), ("norm_out", (16, D), jnp.float32),
     ("a1_out", (L, D), jnp.bfloat16), ("x_out", (2, HALF, D), jnp.bfloat16),
-    ("qkv_out", (3, 2, 512, COLS), jnp.bfloat16), ("lse1_out", (8, L, 1), jnp.float32),
+    ("qkv_out", (3, 2, 512, COLS), jnp.bfloat16), ("lse1_out", (L, 128), jnp.float32),
     ("c1_out", (2, L, COLS), jnp.bfloat16), ("h1_out", (L, D), jnp.float32), ("a2_out", (L, D), jnp.bfloat16),
     ("q2_out", (2, L, COLS), jnp.bfloat16), ("e_out", (2, KEYS, D), jnp.bfloat16),
     ("ek_out", (2, 2, KEYS, COLS), jnp.bfloat16), ("ev_out", (2, 2, KEYS, COLS), jnp.bfloat16),
-    ("lse2_out", (8, L, 1), jnp.float32), ("c2_out", (2, L, COLS), jnp.bfloat16),
+    ("lse2_out", (L, 128), jnp.float32), ("c2_out", (2, L, COLS), jnp.bfloat16),
     ("h2_out", (L, D), jnp.float32), ("a3_out", (L, D), jnp.bfloat16), ("dy_out", (2, HALF, D), jnp.bfloat16),
     ("z_out", (8, L, COLS), jnp.bfloat16), ("slope_out", (8, L, COLS), jnp.bfloat16), ("wide_out", None, jnp.bfloat16),
 )
@@ -631,7 +625,7 @@
         pltpu.VMEM((L, D), f32), pltpu.VMEM((L, D), f32),
         pltpu.VMEM((3, 2, 512, COLS), bf), pltpu.VMEM((2, L, COLS), bf), pltpu.VMEM((2, L, COLS), bf),
         pltpu.VMEM((2, L, COLS), bf), pltpu.VMEM((2, 2, KEYS, COLS), bf), pltpu.VMEM((2, 2, KEYS, COLS), bf),
-        pltpu.VMEM((8, L, 1), f32), pltpu.VMEM((8, L, 1), f32),
+        pltpu.VMEM((L, 128), f32), pltpu.VMEM((L, 128), f32),
         pltpu.VMEM((8, L, COLS), bf), pltpu.VMEM((8, L, COLS), bf),
         pltpu.VMEM((L, 2 * KEYS), f32), pltpu.VMEM((L, 2 * KEYS), bf), pltpu.VMEM((L, D), f32),
         pltpu.VMEM((3, 4, L, COLS), bf), pltpu.VMEM((3, 4, L, COLS), bf),
@@ -654,178 +648,579 @@
     return {n.removesuffix("_out") if n != "layer_out" else n: v for (n, _, _), v in zip(shapes, outs)}
 
 
-def scatter_kernel(levels, groups, part, out, even, odd, two, line, s1, r1, s2, r2, s3, r3):
+RING = 4
+
+
+class Scatter:
+    def __init__(self, levels, part, own, bufs, sems):
+        self.levels, self.part, self.own = levels, part, own
+        self.even, self.odd, self.two, self.line = bufs
+        self.s1, self.r1, self.s2, self.r2, self.s3, self.r3 = sems
+        self.at = place()
+        self.sent = self.steps = self.ready = 0
+
+    @staticmethod
+    def buffers(levels, rows):
+        bf = jnp.bfloat16
+        return [
+            pltpu.VMEM((2, 2, levels, rows, COLS), bf), pltpu.VMEM((2, levels, 2, rows, COLS), bf),
+            pltpu.VMEM((RING, levels, rows, COLS), bf), pltpu.VMEM((RING, levels, rows, COLS), bf),
+        ]
+
+    @staticmethod
+    def semaphores(levels):
+        sem = pltpu.SemaphoreType.DMA
+        one = sem((MATS,))
+        many = sem((MATS, levels))
+        return [one, one, one, one, many, many]
+
+    def first(self, g, even):
+        z, y, x, c = self.at
+        m = MATS - 1 - g
+        if even:
+            src, dst, dev = self.part.at[m, :, :, 1 - y], self.even.at[lax.rem(g // 2, 2)], device(z, 1 - y, x, c)
+        else:
+            src, dst, dev = self.part.at[m, 1 - x], self.odd.at[lax.rem(g // 2, 2)], device(z, y, 1 - x, c)
+        return pltpu.make_async_remote_copy(
+            src, dst, self.s1.at[g], self.r1.at[g], device_id=dev, device_id_type=DT
+        )
+
+    def second(self, g, even):
+        z, y, x, c = self.at
+        m = MATS - 1 - g
+        if even:
+            src, dev = self.part.at[m, 1 - x, :, y], device(z, y, 1 - x, c)
+        else:
+            src, dev = self.part.at[m, x, :, 1 - y], device(z, 1 - y, x, c)
+        return pltpu.make_async_remote_copy(
+            src, self.two.at[lax.rem(g, RING)], self.s2.at[g], self.r2.at[g], device_id=dev, device_id_type=DT
+        )
+
+    def third(self, g, zz, k):
+        z, y, x, c = self.at
+        return pltpu.make_async_remote_copy(
+            self.part.at[MATS - 1 - g, x, zz, y], self.line.at[lax.rem(g, RING), k], self.s3.at[g, zz],
+            self.r3.at[g, k], device_id=device(zz, y, x, c), device_id_type=DT,
+        )
+
+    def both(self, g, body):
+        even = lax.rem(g, 2) == 0
+
+        @pl.when(even)
+        def _():
+            body(True)
+
+        @pl.when(jnp.logical_not(even))
+        def _():
+            body(False)
+
+    def send(self, count):
+        def body(i):
+            self.both(i, lambda even: self.first(i, even).start())
+
+        start = self.sent
+        self.sent += count
+        loop(count, lambda i: body(start + i))
+
+    def add(self, at, got):
+        self.part[at] = (self.part[at].astype(jnp.float32) + got.astype(jnp.float32)).astype(jnp.bfloat16)
+
+    def step_a(self, g):
+        z, y, x, c = self.at
+        m = MATS - 1 - g
+
+        def run(even):
+            self.first(g, even).wait_recv()
+            for k in range(2):
+                def body(zz):
+                    if even:
+                        self.add((m, k, zz, y), self.even[lax.rem(g // 2, 2), k, zz])
+                    else:
+                        self.add((m, x, zz, k), self.odd[lax.rem(g // 2, 2), zz, k])
+
+                loop(self.levels, body)
+            self.second(g, even).start()
+
+        self.both(g, run)
+
+    def step_b(self, g):
+        z, y, x, c = self.at
+        m = MATS - 1 - g
+
+        def run(even):
+            self.second(g, even).wait_recv()
+            loop(self.levels, lambda zz: self.add((m, x, zz, y), self.two[lax.rem(g, RING), zz]))
+
+        self.both(g, run)
+        loop(self.levels - 1, lambda k: self.third(g, lax.rem(z + k + 1, self.levels), z).start())
+
+    def step_c(self, g):
+        z, y, x, c = self.at
+        m = MATS - 1 - g
+        loop(self.levels - 1, lambda k: self.third(g, z, lax.rem(z + k + 1, self.levels)).wait_recv())
+        self.own[m] = self.part[m, x, z, y].astype(jnp.float32)
+
+        def body(k):
+            @pl.when(k != z)
+            def _():
+                self.own[m] += self.line[lax.rem(g, RING), k].astype(jnp.float32)
+
+        loop(self.levels, body)
+
+    def step(self, t):
+        @pl.when(t < MATS)
+        def _():
+            self.step_a(t)
+
+        @pl.when((t >= 1) & (t <= MATS))
+        def _():
+            self.step_b(t - 1)
+
+        @pl.when(t >= 2)
+        def _():
+            self.step_c(t - 2)
+
+    def turn(self, count):
+        start, first = self.steps, self.sent
+        self.steps += count
+        self.sent = max(first, min(MATS, self.steps + RING - 2))
+        assert self.sent <= self.ready
+
+        def body(i):
+            t = start + i
+            self.step(t)
+            g = t + RING - 2
+
+            @pl.when((g >= first) & (g < MATS))
+            def _():
+                self.both(g, lambda even: self.first(g, even).start())
+
+        return body
+
+    def run(self, count):
+        loop(count, self.turn(count))
+
+    def drain(self):
+        z, y, x, c = self.at
+
+        def body(g):
+            def run(even):
+                self.first(g, even).wait_send()
+                self.second(g, even).wait_send()
+
+            self.both(g, run)
+            loop(self.levels - 1, lambda k: self.third(g, lax.rem(z + k + 1, self.levels), z).wait_send())
+
+        loop(MATS, body)
+
+
+BACKWARD_IN = (
+    "dy", "wide", "slope", "z", "a3", "h2", "norm", "c2", "q2", "lse2", "ek", "ev", "e", "a2", "h1",
+    "c1", "qkv", "lse1", "a1", "x",
+)
+
+
+def backward_kernel(levels, fast, *refs):
+    f32, bf = jnp.float32, jnp.bfloat16
+    given = dict(zip(BACKWARD_IN, refs))
+    outs = ("owned_out", "input_out", "frame_out") + (("small_out",) if fast else ("cols_out", "bcols_out"))
+    names = outs + (
+        "part", "own", "dy", "slope", "z", "left", "h", "norm", "c2", "q2", "lse2", "ek", "ev", "e", "a2",
+        "c1", "qkv", "lse1", "x", "dh", "dhb", "dc", "stat", "s", "dp", "p", "ds", "mine", "got", "fsend", "frecv",
+        "fout", "cols", "bcols", "small", "smallgot", "smallsum", "in_sem", "trade_send", "trade_recv", "frame_send",
+        "frame_recv", "frame_out_sem", "small_send", "small_recv", "out_sem",
+    )
+    rest = refs[len(BACKWARD_IN):]
+    r = dict(zip(names, rest))
+    rest = rest[len(names):]
+    scatter = Scatter(levels, r["part"], r["own"], rest[:4], rest[4:])
     z, y, x, c = place()
-    size = MATS // groups
-    greet_neighbours(levels)
-
-    def span(g):
-        return pl.ds(g * size, size)
-
-    def first(g):
-        if g % 2 == 0:
-            src, dev = part.at[span(g), :, :, 1 - y], device(z, 1 - y, x, c)
-        else:
-            src, dev = part.at[span(g), 1 - x, :, :], device(z, y, 1 - x, c)
-        return pltpu.make_async_remote_copy(
-            src, (odd if g % 2 else even).at[g // 2], s1.at[g], r1.at[g], device_id=dev, device_id_type=DT
-        )
-
-    def second(g):
-        if g % 2 == 0:
-            dev = device(z, y, 1 - x, c)
-            src = part.at[span(g), 1 - x, :, y]
-        else:
-            dev = device(z, 1 - y, x, c)
-            src = part.at[span(g), x, :, 1 - y]
-        return pltpu.make_async_remote_copy(
-            src, two.at[g], s2.at[g], r2.at[g], device_id=dev, device_id_type=DT
-        )
-
-    def add_first(g):
-        for m in range(size):
-            for k in range(2):
-                def body(zz, carry):
-                    if g % 2 == 0:
-                        at = (g * size + m, k, zz, y)
-                    else:
-                        at = (g * size + m, x, zz, k)
-                    got = even[g // 2, m, k, zz] if g % 2 == 0 else odd[g // 2, m, zz, k]
-                    part[at] = (part[at].astype(jnp.float32) + got.astype(jnp.float32)).astype(jnp.bfloat16)
-                    return carry
-
-                lax.fori_loop(0, levels, body, 0)
-
-    def add_second(g):
-        for m in range(size):
-            def body(zz, carry):
-                at = (g * size + m, x, zz, y)
-                part[at] = (part[at].astype(jnp.float32) + two[g, m, zz].astype(jnp.float32)).astype(jnp.bfloat16)
-                return carry
-
-            lax.fori_loop(0, levels, body, 0)
-
-    def z_copy(g, zz, up):
-        return pltpu.make_async_remote_copy(
-            part.at[span(g), x, zz, y], line.at[g, up, zz], s3.at[g, zz], r3.at[g, up, zz],
-            device_id=device(z + 1 if up else z - 1, y, x, c), device_id_type=DT,
-        )
-
-    def add_line(g, zz, up):
-        for m in range(size):
-            at = (g * size + m, x, zz, y)
-            part[at] = (part[at].astype(jnp.float32) + line[g, up, zz, m].astype(jnp.float32)).astype(jnp.bfloat16)
-
-    def third(g):
-        def run(k, carry):
-            top = levels - 1 - k
-
-            @pl.when(top > z)
-            def _():
-                @pl.when(z > 0)
-                def _():
-                    z_copy(g, top, 1).wait_recv()
-                    add_line(g, top, 1)
-
-                z_copy(g, top, 1).start()
-
-            @pl.when(k < z)
-            def _():
-                @pl.when(z < levels - 1)
-                def _():
-                    z_copy(g, k, 0).wait_recv()
-                    add_line(g, k, 0)
-
-                z_copy(g, k, 0).start()
-
-            return carry
-
-        lax.fori_loop(0, levels, run, 0)
-
-    def last(g):
-        @pl.when(z > 0)
+    dp = z * 2 + y
+    mate = (dp, x, 1 - c)
+    count = levels * 4
+    me = dp * 2 + x
+    rows_of = D // (levels * 2)
+    per = COLS // (2 * rows_of)
+
+    def peer(i):
+        return (i // 2, lax.rem(i, 2), c)
+
+    loads = {}
+
+    def load(name, src, dst):
+        loads[name] = pltpu.make_async_copy(src, dst, r["in_sem"].at[len(loads)])
+        loads[name].start()
+
+    def loaded(*which):
+        for name in which:
+            loads[name].wait()
+
+    load("dy", given["dy"], r["dy"])
+    load("w2", given["wide"].at[12:16], r["part"].at[12:16])
+    load("slope", given["slope"], r["slope"])
+    load("z", given["z"], r["z"])
+    load("w1", given["wide"].at[8:12], r["part"].at[8:12])
+    load("a3", given["a3"], r["left"])
+    load("h2", given["h2"], r["h"])
+    load("w0", given["wide"].at[0:8], r["part"].at[0:8])
+    for name in ("norm", "c2", "q2", "lse2", "ek", "ev", "e", "a2", "c1", "qkv", "lse1", "x"):
+        load(name, given[name], r[name])
+
+    bar = pltpu.get_barrier_semaphore()
+    loop(count - 1, lambda k: pl.semaphore_signal(
+        bar, inc=1, device_id=peer(lax.rem(me + k + 1, count)), device_id_type=DT))
+    pl.semaphore_signal(bar, inc=1, device_id=mate, device_id_type=DT)
+    pl.semaphore_wait(bar, count)
+
+    def remote(src, dst, send, recv, dev):
+        return pltpu.make_async_remote_copy(src, dst, send, recv, device_id=dev, device_id_type=DT)
+
+    def trade(n, j):
+        return remote(r["mine"].at[n % 2, j], r["got"].at[n % 2, j], r["trade_send"].at[n, j],
+                      r["trade_recv"].at[n, j], mate)
+
+    def panel(mat, side):
+        return r["part"][mat, side].reshape(D, COLS)
+
+    def grads(lefts, items):
+        def body(j):
+            cols = pl.ds(pl.multiple_of(j * COLS, COLS), COLS)
+            turned = [v.T for v in lefts(cols)]
+            for mat, side, rights in items:
+                acc = None
+                for t, right in zip(turned, rights()):
+                    more = dot(t, right, NN)
+                    acc = more if acc is None else acc + more
+                r["part"][mat, side, pl.ds(j * per, per)] = acc.astype(bf).reshape(per, 2, rows_of, COLS)
+
+        loop(4, body)
+
+    def send_back(n, items):
+        if n >= 2:
+            loop(4, lambda j: trade(n - 2, j).wait_send())
+
+        def body(j):
+            acc = None
+            for value, mat, side in items:
+                more = dot(value(), flat_rows(r["part"].at[mat, side], j), NT)
+                acc = more if acc is None else acc + more
+            r["mine"][n % 2, j] = acc.astype(bf)
+            trade(n, j).start()
+
+        loop(4, body)
+
+    def fold(v):
+        return jnp.sum(v.reshape(BLOCK // 8, 8, D), axis=0)
+
+    def norm_row(k):
+        return r["norm"][k : k + 1, :]
+
+    def grow(k, v):
+        r["cols"][k * 8 : (k + 1) * 8, :] += fold(v)
+
+    def half_rows(ref, i):
+        half = i // (HALF // BLOCK)
+        inner = pl.ds(pl.multiple_of((i - half * (HALF // BLOCK)) * BLOCK, BLOCK), BLOCK)
+        return ref[half, inner, :].astype(f32)
+
+    def norm_back(n, k, base, incoming, sum_k):
+        loop(4, lambda j: trade(n, j).wait_recv())
+
+        def body(rows, i):
+            normed, scaled = normed_block(base(rows, i))
+            dn = panels_row(r["mine"].at[n % 2], rows) + panels_row(r["got"].at[n % 2], rows)
+            inner = dn * norm_row(k)
+            back = scaled * (
+                inner - jnp.mean(inner, axis=-1, keepdims=True)
+                - normed * jnp.mean(inner * normed, axis=-1, keepdims=True)
+            )
+            came = incoming(rows, i)
+            out = came + back
+            r["dh"][rows, :] = out
+            grow(k, dn * normed)
+            grow(k + 1, dn)
+            if sum_k is not None:
+                r["dhb"][rows, :] = out.astype(bf)
+                grow(sum_k, out)
+            if n == 0:
+                grow(8, came)
+
+        rows_loop(L, body)
+
+    r["cols"][...] = jnp.zeros((72, D), f32)
+    loaded("dy", "w2", "slope")
+
+    def hidden_back(t):
+        m, side = t // 2, lax.rem(t, 2)
+        du = (dot(r["dy"][...].reshape(L, D), panel(12 + m, side), NN) * r["slope"][t].astype(f32)).astype(bf)
+        r["slope"][t] = du
+        r["bcols"][pl.ds(8 + t, 1), :] = jnp.sum(du.astype(f32), axis=0, keepdims=True)
+
+    loop(8, hidden_back)
+    loaded("z")
+    grads(
+        lambda cols: [r["dy"][:, :, cols].reshape(L, COLS)],
+        [(12 + t // 2, t % 2, lambda t=t: [r["z"][t]]) for t in range(8)],
+    )
+    scatter.send(4)
+    loaded("w1")
+    send_back(0, [(lambda t=t: r["slope"][t], 8 + t // 2, t % 2) for t in range(8)])
+    loaded("a3", "h2", "norm")
+    grads(
+        lambda cols: [r["left"][:, cols]],
+        [(8 + t // 2, t % 2, lambda t=t: [r["slope"][t]]) for t in range(8)],
+    )
+    scatter.ready = 8
+    load("a1", given["a1"], r["left"])
+    norm_back(0, 4, lambda rows, i: r["h"][rows, :], lambda rows, i: half_rows(r["dy"], i), 7)
+    load("h1", given["h1"], r["h"])
+    scatter.run(1)
+    loaded("w0")
+
+    def context_back(mat):
+        def body(side):
+            r["dc"][side] = dot(r["dhb"][...], panel(mat, side), NN).astype(bf)
+
+        loop(2, body)
+
+    def statistics(lse, ctx):
+        r["stat"][0:8, :] = lse[...].T[0:8, :]
+        for side in range(2):
+            both = (r["dc"][side].astype(f32) * ctx[side].astype(f32)).T
+            r["stat"][8 + side * 4 : 12 + side * 4, :] = jnp.sum(both.reshape(4, HD, L), axis=1)
+
+    lane = lax.broadcasted_iota(jnp.int32, (1, 128), 1)
+    low = lane < HD
+    low_row = lax.broadcasted_iota(jnp.int32, (128, 1), 0) < HD
+
+    def attend_back(query, keys, values, parts, width, causal, turn):
+        def body(t):
+            side, half = t // 2, lax.rem(t, 2)
+            lanes = pl.ds(pl.multiple_of(half * 128, 128), 128)
+            q = query[(side, slice(0, L), lanes)].astype(f32) * 0.125
+            dc = r["dc"][side, :, lanes].astype(f32)
+            back = None
+            for n in range(parts):
+                at = (side, n, slice(None), lanes) if parts > 1 else (side, slice(0, L), lanes)
+                k, v = keys[at], values[at]
+                flat = k.T
+                dk = dv = None
+                for sub in range(2):
+                    mine = low if sub == 0 else jnp.logical_not(low)
+                    mine_row = low_row if sub == 0 else jnp.logical_not(low_row)
+                    qh = jnp.where(mine, q, 0.0).astype(bf)
+                    dm = jnp.where(mine, dc, 0.0).astype(bf)
+                    kt = jnp.where(mine_row, flat.astype(f32), 0.0).astype(bf)
+                    r["s"][0:width, :] = dot(k, qh, NT)
+                    r["dp"][0:width, :] = dot(v, dm, NT)
+                    lse = r["stat"][pl.ds(t * 2 + sub, 1), :]
+                    delta = r["stat"][pl.ds(8 + t * 2 + sub, 1), :]
+
+                    def rows_body(rows, i):
+                        key = i * BLOCK + lax.broadcasted_iota(jnp.int32, (BLOCK, L), 0)
+                        if causal:
+                            keep = lax.broadcasted_iota(jnp.int32, (BLOCK, L), 1) >= key
+                        else:
+                            keep = key < HALF_FRAMES
+                        p = jnp.where(keep, jnp.exp(jnp.where(keep, r["s"][rows, :], -1e30) - lse), 0.0)
+                        r["p"][rows, :] = p.astype(bf)
+                        r["ds"][rows, :] = (p * (r["dp"][rows, :] - delta)).astype(bf)
+
+                    rows_loop(width, rows_body)
+                    p, ds = r["p"][0:width, :], r["ds"][0:width, :]
+                    dv = dot(p, dm, NN) if dv is None else dv + dot(p, dm, NN)
+                    dk = dot(ds, qh, NN) if dk is None else dk + dot(ds, qh, NN)
+                    more = dot(kt, ds, NN)
+                    back = more if back is None else back + more
+                keys[at] = dk.astype(bf)
+                values[at] = dv.astype(bf)
+            query[(side, slice(0, L), lanes)] = (back.T * 0.125).astype(bf)
+            turn(t)
+
+        loop(4, body)
+
+    def column(k, ref, at):
+        def body(side):
+            r["bcols"][pl.ds(k * 2 + side, 1), :] = jnp.sum(ref[at(side)].astype(f32), axis=0, keepdims=True)
+
+        loop(2, body)
+
+    context_back(7)
+    loaded("c2", "lse2")
+    statistics(r["lse2"], r["c2"])
+    grads(
+        lambda cols: [r["dhb"][:, cols]], [(7, side, lambda side=side: [r["c2"][side]]) for side in range(2)]
+    )
+    scatter.ready = 9
+    scatter.run(1)
+    loaded("q2", "ek", "ev")
+    attend_back(r["q2"], r["ek"], r["ev"], 2, KEYS, False, scatter.turn(4))
+
+    loaded("e", "a2")
+
+    def frame_share(half, j):
+        acc = None
+        for mat, ref in ((5, r["ek"]), (6, r["ev"])):
+            for side in range(2):
+                more = dot(ref[side, half], flat_rows(r["part"].at[mat, side], j), NT)
+                acc = more if acc is None else acc + more
+        return acc
+
+    def frame_trade(j):
+        return remote(r["fsend"].at[j], r["frecv"].at[j], r["frame_send"].at[j], r["frame_recv"].at[j], mate)
+
+    def frame_store(j):
+        cols = pl.ds(pl.multiple_of(j * COLS, COLS), COLS)
+        return pltpu.make_async_copy(r["fout"].at[lax.rem(j, 2)], r["frame_out"].at[:, cols], r["frame_out_sem"].at[j])
+
+    def frame_far(j):
+        r["fsend"][j] = frame_share(1 - c, j).astype(bf)
+        frame_trade(j).start()
+
+    def frame_near(j):
+        @pl.when(j >= 2)
         def _():
-            z_copy(g, z, 1).wait_recv()
-
-        @pl.when(z < levels - 1)
-        def _():
-            z_copy(g, z, 0).wait_recv()
-
-        for m in range(size):
-            i = g * size + m
-            own = part[i, x, z, y].astype(jnp.float32)
-            below = jnp.where(z > 0, line[g, 1, z, m].astype(jnp.float32), 0.0)
-            above = jnp.where(z < levels - 1, line[g, 0, z, m].astype(jnp.float32), 0.0)
-            out[i] = own + below + above
-
-    def drain(g):
-        first(g).wait_send()
-        second(g).wait_send()
-
-        def run(zz, carry):
-            @pl.when(zz > z)
-            def _():
-                z_copy(g, zz, 1).wait_send()
-
-            @pl.when(zz < z)
-            def _():
-                z_copy(g, zz, 0).wait_send()
-
-            return carry
-
-        lax.fori_loop(0, levels, run, 0)
-
-    for g in range(groups):
-        first(g).start()
-    for step in range(groups + 2):
-        if step < groups:
-            first(step).wait_recv()
-            add_first(step)
-            second(step).start()
-        if 1 <= step <= groups:
-            second(step - 1).wait_recv()
-            add_second(step - 1)
-            third(step - 1)
-        if step >= 2:
-            last(step - 2)
-    for g in range(groups):
-        drain(g)
-
-
-def scatter_grads(part, shards):
-    levels = shards // 2
-    rows = D // shards
-    groups = 8
-    size = MATS // groups
+            frame_store(j - 2).wait()
+
+        frame_trade(j).wait_recv()
+        r["fout"][lax.rem(j, 2)] = frame_share(c, j) + r["frecv"][j].astype(f32)
+        frame_store(j).start()
+
+    loop(4, frame_far)
+    send_back(1, [(lambda side=side: r["q2"][side], 4, side) for side in range(2)])
+    loop(4, frame_near)
+    scatter.run(1)
+    grads(
+        lambda cols: [r["e"][n, :, cols] for n in range(2)],
+        [(5 + i, side, lambda ref=ref, side=side: [ref[side, n] for n in range(2)])
+         for i, ref in ((1, r["ev"]), (0, r["ek"])) for side in range(2)],
+    )
+    scatter.ready = 11
+    scatter.run(1)
+    column(2, r["q2"], lambda side: (side,))
+
+    def value_column(side):
+        total = sum(jnp.sum(r["ev"][side, n].astype(f32), axis=0, keepdims=True) for n in range(2))
+        r["bcols"][pl.ds(6 + side, 1), :] = total
+
+    loop(2, value_column)
+    grads(lambda cols: [r["a2"][:, cols]], [(4, side, lambda side=side: [r["q2"][side]]) for side in range(2)])
+    scatter.ready = 12
+    loaded("h1")
+    norm_back(1, 2, lambda rows, i: r["h"][rows, :], lambda rows, i: r["dh"][rows, :], 6)
+    scatter.run(1)
+    context_back(3)
+    loaded("c1", "lse1")
+    statistics(r["lse1"], r["c1"])
+    grads(
+        lambda cols: [r["dhb"][:, cols]], [(3, side, lambda side=side: [r["c1"][side]]) for side in range(2)]
+    )
+    scatter.ready = 13
+    scatter.run(1)
+    loaded("qkv")
+    q_ref, k_ref, v_ref = (r["qkv"].at[i] for i in range(3))
+    attend_back(q_ref, k_ref, v_ref, 1, L, True, lambda t: None)
+    send_back(2, [(lambda i=i, side=side: r["qkv"][i, side, 0:L, :], i, side) for i in range(3) for side in range(2)])
+    loaded("a1")
+    grads(
+        lambda cols: [r["left"][:, cols]],
+        [(i, side, lambda i=i, side=side: [r["qkv"][i, side, 0:L, :]]) for i in (2, 1, 0) for side in range(2)],
+    )
+    scatter.ready = 16
+    scatter.run(1)
+    column(0, q_ref, lambda side: (side, slice(0, L)))
+    column(1, v_ref, lambda side: (side, slice(0, L)))
+    loaded("x")
+    norm_back(2, 0, lambda rows, i: half_rows(r["x"], i), lambda rows, i: r["dh"][rows, :], None)
+    own_rows = pl.ds(pl.multiple_of(c * HALF, HALF), HALF)
+    input_copy = pltpu.make_async_copy(r["dh"].at[own_rows], r["input_out"], r["out_sem"].at[0])
+    input_copy.start()
+
+    sums = jnp.concatenate([jnp.sum(r["cols"][k * 8 : k * 8 + 8, :], axis=0, keepdims=True) for k in range(9)], axis=0)
+    if fast:
+        r["small"][...] = jnp.zeros(r["small"].shape, f32)
+        for i in range(2 * levels):
+            for xx in range(2):
+                k = i * 2 + xx
+                r["small"][k, 0:9, :] = sums[:, i * 128 : (i + 1) * 128]
+                r["small"][k, 9:10, :] = r["bcols"][k : k + 1, 0:128]
+                r["small"][k, 10:11, :] = r["bcols"][k : k + 1, 128:256]
+
+        def small_copy(k, slot):
+            i = lax.rem(me + k + 1, count)
+            return remote(r["small"].at[i], r["smallgot"].at[slot], r["small_send"].at[k], r["small_recv"].at[slot],
+                          peer(i))
+
+        loop(count - 1, lambda k: small_copy(k, me).start())
+        r["smallgot"][me] = r["small"][me]
+    else:
+        r["smallsum"][0:9, :] = sums
+    while scatter.steps < MATS + 2:
+        scatter.run(min(4, MATS + 2 - scatter.steps))
+    owned_copy = pltpu.make_async_copy(r["own"], r["owned_out"], r["out_sem"].at[1])
+    owned_copy.start()
+    if fast:
+        loop(count - 1, lambda k: small_copy(k, lax.rem(me + k + 1, count)).wait_recv())
+        total = r["smallgot"][0]
+        for k in range(1, 4 * levels):
+            total = total + r["smallgot"][k]
+        r["smallsum"][...] = total
+        small_store = pltpu.make_async_copy(r["smallsum"], r["small_out"], r["out_sem"].at[2])
+        small_store.start()
+        loop(count - 1, lambda k: small_copy(k, me).wait_send())
+        small_store.wait()
+    else:
+        first_store = pltpu.make_async_copy(r["smallsum"], r["cols_out"], r["out_sem"].at[2])
+        second_store = pltpu.make_async_copy(r["bcols"], r["bcols_out"], r["out_sem"].at[3])
+        first_store.start()
+        second_store.start()
+        first_store.wait()
+        second_store.wait()
+    for n in (1, 2):
+        loop(4, lambda j: trade(n, j).wait_send())
+    loop(4, lambda j: frame_trade(j).wait_send())
+    for j in (2, 3):
+        frame_store(j).wait()
+    scatter.drain()
+    input_copy.wait()
+    owned_copy.wait()
+
+
+def backward(kept, shards):
+    levels, rows = shards // 2, D // shards
+    fast = rows == 128
+    f32, bf = jnp.float32, jnp.bfloat16
     sem = pltpu.SemaphoreType.DMA
-    bf = jnp.bfloat16
-    vm = pl.BlockSpec(memory_space=pltpu.VMEM)
-
-    def kernel(levels, groups, given, out, part, *rest):
-        load = pltpu.make_async_copy(given, part, rest[-1])
-        load.start()
-        load.wait()
-        scatter_kernel(levels, groups, part, out, *rest[:-1])
-
+    hbm = pl.BlockSpec(memory_space=pl.ANY)
+    peers = shards * 2
+    shapes = [((MATS, rows, COLS), f32), ((HALF, D), f32), ((KEYS, D), f32)]
+    shapes += [((16, 128), f32)] if fast else [((16, D), f32), ((16, COLS), f32)]
+    small = (peers, 16, 128) if fast else (1, 16, 128)
+    vm = pltpu.VMEM
+    scratch = [
+        vm((MATS, 2, levels, 2, rows, COLS), bf), vm((MATS, rows, COLS), f32), vm((2, HALF, D), bf),
+        vm((8, L, COLS), bf), vm((8, L, COLS), bf), vm((L, D), bf), vm((L, D), f32), vm((16, D), f32),
+        vm((2, L, COLS), bf), vm((2, L, COLS), bf), vm((L, 128), f32), vm((2, 2, KEYS, COLS), bf),
+        vm((2, 2, KEYS, COLS), bf), vm((2, KEYS, D), bf), vm((L, D), bf),
+        vm((2, L, COLS), bf), vm((3, 2, 512, COLS), bf), vm((L, 128), f32), vm((2, HALF, D), bf),
+        vm((L, D), f32), vm((L, D), bf), vm((2, L, COLS), bf), vm((16, L), f32),
+        vm((KEYS, L), f32), vm((KEYS, L), f32), vm((KEYS, L), bf), vm((KEYS, L), bf),
+        vm((2, 4, L, COLS), bf), vm((2, 4, L, COLS), bf), vm((4, KEYS, COLS), bf), vm((4, KEYS, COLS), bf),
+        vm((2, KEYS, COLS), f32), vm((72, D), f32), vm((16, COLS), f32), vm(small, f32), vm(small, f32),
+        vm((16, 128) if fast else (16, D), f32),
+        sem((24,)), sem((3, 4)), sem((3, 4)), sem((4,)), sem((4,)), sem((4,)), sem((peers,)), sem((peers,)), sem((4,)),
+    ]
     return pl.pallas_call(
-        partial(kernel, levels, groups),
-        out_shape=jax.ShapeDtypeStruct((MATS, rows, COLS), jnp.float32),
-        in_specs=[pl.BlockSpec(memory_space=pl.ANY)],
-        out_specs=vm,
-        scratch_shapes=[
-            pltpu.VMEM((MATS, 2, levels, 2, rows, COLS), bf),
-            pltpu.VMEM((groups // 2, size, 2, levels, rows, COLS), bf),
-            pltpu.VMEM((groups // 2, size, levels, 2, rows, COLS), bf),
-            pltpu.VMEM((groups, size, levels, rows, COLS), bf),
-            pltpu.VMEM((groups, 2, levels, size, rows, COLS), bf),
-            sem((groups,)), sem((groups,)), sem((groups,)), sem((groups,)),
-            sem((groups, levels)), sem((groups, 2, levels)), sem,
-        ],
+        partial(backward_kernel, levels, fast),
+        out_shape=[jax.ShapeDtypeStruct(s, t) for s, t in shapes],
+        in_specs=[hbm] * len(BACKWARD_IN),
+        out_specs=[hbm] * len(shapes),
+        scratch_shapes=scratch + Scatter.buffers(levels, rows) + Scatter.semaphores(levels),
         compiler_params=pltpu.CompilerParams(
-            collective_id=1, has_side_effects=True, vmem_limit_bytes=62 * 2**20
+            collective_id=1, has_side_effects=True, vmem_limit_bytes=63 * 2**20
         ),
-        name="scatter_grads",
-    )(part.reshape(MATS, 2, levels, 2, rows, COLS))
+        name="backward",
+    )(*[kept[n] for n in BACKWARD_IN])
 
 
 def small_kernel(shards, every, scatter, src, out, own_sem, send_sem, recv_sem):
@@ -892,117 +1287,6 @@
     )(src)
 
 
-def pair_kernel(src, out, own_sem, send_sem, recv_sem):
-    dp, x, c = (lax.axis_index(a) for a in AXES)
-    bar = pltpu.get_barrier_semaphore()
-    pl.semaphore_signal(bar, inc=1, device_id=(dp, x, 1 - c), device_id_type=DT)
-    pl.semaphore_wait(bar, 1)
-    copy = pltpu.make_async_remote_copy(
-        src, out.at[c], send_sem, recv_sem, device_id=(dp, x, 1 - c), device_id_type=DT
-    )
-    copy.start()
-    own = pltpu.make_async_copy(src, out.at[c], own_sem)
-    own.start()
-    own.wait()
-    copy.wait_send()
-    pltpu.make_async_remote_copy(
-        src, out.at[1 - c], send_sem, recv_sem, device_id=(dp, x, 1 - c), device_id_type=DT
-    ).wait_recv()
-
-
-def pair_gather(src, call_id):
-    sem = pltpu.SemaphoreType.DMA
-    vm = pl.BlockSpec(memory_space=pltpu.VMEM)
-    return pl.pallas_call(
-        pair_kernel,
-        out_shape=jax.ShapeDtypeStruct((2, *src.shape), src.dtype),
-        in_specs=[vm],
-        out_specs=vm,
-        scratch_shapes=[sem, sem, sem],
-        compiler_params=pltpu.CompilerParams(collective_id=call_id, has_side_effects=True),
-        name=f"pair_gather_{call_id}",
-    )(src)
-
-
-def pair_sum(part, call_id):
-    both = pair_gather(part.astype(jnp.bfloat16), call_id)
-    return both[0].astype(jnp.float32) + both[1].astype(jnp.float32)
-
-
-def norm_forward(values, gain_row, offset):
-    centre = values - jnp.mean(values, axis=-1, keepdims=True)
-    spread = jnp.mean(centre * centre, axis=-1, keepdims=True)
-    scaled = lax.rsqrt(spread + 1e-05)
-    normed = centre * scaled
-    return (normed * gain_row + offset, normed, scaled)
-
-
-def norm_backward(gradient, normed, scaled, gain_row):
-    inner_grad = gradient * gain_row
-    result = scaled * (
-        inner_grad
-        - jnp.mean(inner_grad, axis=-1, keepdims=True)
-        - normed * jnp.mean(inner_grad * normed, axis=-1, keepdims=True)
-    )
-    return (result, jnp.sum(gradient * normed, axis=0), jnp.sum(gradient, axis=0))
-
-
-def gelu_value(values):
-    return 0.5 * values * (1.0 + jax.scipy.special.erf(values * 0.7071067811865476))
-
-
-def gelu_slope(values):
-    return (
-        0.5 * (1.0 + jax.scipy.special.erf(values * 0.7071067811865476))
-        + values * jnp.exp(-0.5 * values * values) * 0.3989422804014327
-    )
-
-
-def clip_scores(queries, key_rows, causal):
-    scores = (
-        jnp.einsum("qhd,khd->hqk", queries, key_rows, preferred_element_type=jnp.float32) * 0.125
-    )
-    if causal:
-        allowed = lax.broadcasted_iota(jnp.int32, scores.shape, 1) >= lax.broadcasted_iota(
-            jnp.int32, scores.shape, 2
-        )
-        scores = jnp.where(allowed, scores, -1e30)
-    return scores
-
-
-def clip_forward(causal, queries, key_rows, values):
-    scores = clip_scores(queries, key_rows, causal)
-    row_max = jnp.max(scores, axis=-1, keepdims=True)
-    shifted = jnp.exp(scores - row_max)
-    row_sum = jnp.sum(shifted, axis=-1, keepdims=True)
-    weights = (shifted / row_sum).astype(jnp.bfloat16)
-    context = jnp.einsum("hqk,khd->qhd", weights, values, preferred_element_type=jnp.float32)
-    return (context.astype(jnp.bfloat16), (row_max + jnp.log(row_sum))[..., 0])
-
-
-def clip_backward(causal, queries, key_rows, values, log_total, context_grad):
-    scores = clip_scores(queries, key_rows, causal)
-    probs = jnp.exp(scores - log_total[..., None])
-    value_grad = jnp.einsum(
-        "hqk,qhd->khd", probs.astype(jnp.bfloat16), context_grad, preferred_element_type=jnp.float32
-    )
-    prob_grad = jnp.einsum("qhd,khd->hqk", context_grad, values, preferred_element_type=jnp.float32)
-    score_grad = (probs * (prob_grad - jnp.sum(probs * prob_grad, axis=-1, keepdims=True))).astype(
-        jnp.bfloat16
-    )
-    query_grad = (
-        jnp.einsum("hqk,khd->qhd", score_grad, key_rows, preferred_element_type=jnp.float32) * 0.125
-    )
-    key_grad = (
-        jnp.einsum("hqk,qhd->khd", score_grad, queries, preferred_element_type=jnp.float32) * 0.125
-    )
-    return (
-        query_grad.astype(jnp.bfloat16),
-        key_grad.astype(jnp.bfloat16),
-        value_grad.astype(jnp.bfloat16),
-    )
-
-
 def adapt(weight, gradient, moment, second, token_total):
     scaled_grad = gradient / token_total
     new_moment = 0.5 * moment + 0.5 * scaled_grad
@@ -1059,134 +1343,24 @@
         [attention_weights.reshape(8, rows, COLS), dense_weights.transpose(0, 2, 1, 3).reshape(8, rows, COLS)]
     )
     kept = forward(shard, tokens, jnp.pad(frames, ((0, KEYS - HALF_FRAMES), (0, 0))), cotangent, small, shards)
-    wide = kept["wide"].reshape(MATS, 2, D, COLS)
-    norm_rows = kept["norm"]
-
-    def project(left, mat):
-        return jnp.einsum("rd,xde->rxe", left, wide[mat], preferred_element_type=f32).reshape(-1, 512)
-
-    def project_hidden(left, base):
-        return jnp.einsum("rd,mxde->rmxe", left, wide[base : base + 4], preferred_element_type=f32).reshape(-1, 2048)
-
-    def collect(left, mat):
-        return jnp.einsum("rxe,xde->rd", left.reshape(-1, 2, COLS), wide[mat], preferred_element_type=f32)
-
-    def collect_hidden(left, base):
-        return jnp.einsum("rmxe,mxde->rd", left.reshape(-1, 4, 2, COLS), wide[base : base + 4], preferred_element_type=f32)
-
-    def weight_grad(left, right):
-        return jnp.einsum("rd,rme->mde", left, right.reshape(right.shape[0], -1, COLS), preferred_element_type=f32).astype(bf)
-
-    def by_head(flat):
-        return flat.reshape(-1, 8, HD)
-
-    def joined(panels):
-        return panels.transpose(1, 0, 2).reshape(panels.shape[1], -1)
-
-    def unpadded(halves):
-        return halves[:, :HALF_FRAMES].reshape(FRAMES, -1)
-
-    row_data = kept["x"].reshape(L, D).astype(f32)
-    out_grad_low = kept["dy"].reshape(L, D)
-    frame_rows = unpadded(kept["e"])
-    first_in, second_in, third_in = kept["a1"], kept["a2"], kept["a3"]
-    _, first_normed, first_scale = norm_forward(row_data, norm_rows[0], norm_rows[1])
-    _, second_normed, second_scale = norm_forward(kept["h1"], norm_rows[2], norm_rows[3])
-    _, third_normed, third_scale = norm_forward(kept["h2"], norm_rows[4], norm_rows[5])
-    self_query, self_keys, self_values = (joined(kept["qkv"][i, :, :L]) for i in range(3))
-    self_total, cross_total = kept["lse1"][..., 0], kept["lse2"][..., 0]
-    self_flat, cross_flat, cross_query = joined(kept["c1"]), joined(kept["c2"]), joined(kept["q2"])
-    cross_keys, cross_values = (
-        jnp.concatenate([unpadded(kept[n][side]) for side in range(2)], axis=1) for n in ("ek", "ev")
-    )
-    activated = joined(kept["z"])
-    slope = joined(kept["slope"]).astype(f32)
     layer_out = kept["layer_out"]
-
-    out_grad = out_grad_low.astype(f32)
-    act_grad = project_hidden(out_grad_low, 12)
-    down_grad = weight_grad(out_grad_low, activated)
-    before_grad = (act_grad * slope).astype(bf)
-    hidden_bias_grad = jnp.sum(before_grad, axis=0, dtype=f32)
-    up_grad = weight_grad(third_in, before_grad)
-    third_back = pair_sum(collect_hidden(before_grad, 8), 9)
-    third_input_grad, third_gain_grad, third_offset_grad = norm_backward(
-        third_back, third_normed, third_scale, norm_rows[4]
-    )
-    two_grad = out_grad + third_input_grad
-    two_low = two_grad.astype(bf)
-    cross_ctx_grad = project(two_low, 7).astype(bf)
-    cross_out_grad = weight_grad(two_low, cross_flat)
-    cross_qgrad, cross_kgrad, cross_vgrad = clip_backward(
-        False, by_head(cross_query), by_head(cross_keys), by_head(cross_values), cross_total,
-        by_head(cross_ctx_grad),
-    )
-    cross_qflat = cross_qgrad.reshape(L, 512)
-    cross_kflat = cross_kgrad.reshape(FRAMES, 512)
-    cross_vflat = cross_vgrad.reshape(FRAMES, 512)
-    frame_part = collect(cross_kflat, 5) + collect(cross_vflat, 6)
-    frame_both = pair_gather(frame_part.astype(bf), 10)
-    frame_gradient = jnp.sum(
-        lax.dynamic_slice_in_dim(frame_both, c * (FRAMES // 2), FRAMES // 2, 1).astype(f32), axis=0
-    )
-    second_back = pair_sum(collect(cross_qflat, 4), 11)
-    second_input_grad, second_gain_grad, second_offset_grad = norm_backward(
-        second_back, second_normed, second_scale, norm_rows[2]
-    )
-    one_grad = two_grad + second_input_grad
-    one_low = one_grad.astype(bf)
-    self_ctx_grad = project(one_low, 3).astype(bf)
-    self_out_grad = weight_grad(one_low, self_flat)
-    self_qgrad, self_kgrad, self_vgrad = clip_backward(
-        True, by_head(self_query), by_head(self_keys), by_head(self_values), self_total,
-        by_head(self_ctx_grad),
-    )
-    self_qflat, self_kflat, self_vflat = (v.reshape(L, 512) for v in (self_qgrad, self_kgrad, self_vgrad))
-    first_back = pair_sum(
-        collect(self_qflat, 0) + collect(self_kflat, 1) + collect(self_vflat, 2), 12
-    )
-    first_input_grad, first_gain_grad, first_offset_grad = norm_backward(
-        first_back, first_normed, first_scale, norm_rows[0]
-    )
-    input_gradient = lax.dynamic_slice_in_dim(one_grad + first_input_grad, c * (L // 2), L // 2, 0)
-
-    parts = jnp.concatenate(
-        [
-            weight_grad(first_in, self_qflat), weight_grad(first_in, self_kflat),
-            weight_grad(first_in, self_vflat), self_out_grad,
-            weight_grad(second_in, cross_qflat), weight_grad(frame_rows, cross_kflat),
-            weight_grad(frame_rows, cross_vflat), cross_out_grad, up_grad, down_grad,
-        ]
-    )
-    owned = scatter_grads(parts, shards)
+    owned, input_gradient, frame_gradient, *small_grads = backward(kept, shards)
+    frame_gradient = frame_gradient[:HALF_FRAMES]
     attention_owned = owned[:8].reshape(2, 4, rows, COLS)
     dense_owned = owned[8:].reshape(2, 4, rows, COLS).transpose(0, 2, 1, 3)
 
-    def column(v):
-        return jnp.sum(v, axis=0, dtype=f32)
-
-    unit_rows_grad = jnp.concatenate(
-        [
-            jnp.stack([column(self_qflat), column(self_vflat), column(cross_qflat), column(cross_vflat)]),
-            hidden_bias_grad.reshape(4, 512),
-        ]
-    )
-    unit_grads = (
-        unit_rows_grad.reshape(8, 2, 4, HD).transpose(1, 2, 0, 3).reshape(2, 4, shards, unit_cols)
-        .transpose(2, 0, 1, 3).reshape(shards, 2, 4 * unit_cols)
-    )
-    norm_grads = jnp.stack(
-        [
-            first_gain_grad, first_offset_grad, second_gain_grad, second_offset_grad,
-            third_gain_grad, third_offset_grad, column(one_grad), column(two_grad), column(out_grad),
-        ]
-    )
-    norm_parts = norm_grads.reshape(9, shards, rows).transpose(1, 0, 2).reshape(shards, 1, 9 * rows)
-    small = jnp.concatenate([jnp.broadcast_to(norm_parts, (shards, 2, 9 * rows)), unit_grads], axis=2)
-    small = jnp.pad(small, ((0, 0), (0, 0), (0, 2048 - small.shape[2]))).reshape(shards * 2, 16, 128)
-    small = jnp.sum(small_exchange(small, shards, False, True, 13), axis=0).reshape(2048)
-    norm_owned = small[: 9 * rows].reshape(9, rows)
-    unit_owned = small[9 * rows : 9 * rows + 4 * unit_cols].reshape(4, unit_cols)
+    if rows == 128:
+        norm_owned = small_grads[0][:9]
+        unit_owned = small_grads[0][9:11].reshape(4, unit_cols)
+    else:
+        norm_parts = small_grads[0][:9].reshape(9, shards, rows).transpose(1, 0, 2).reshape(shards, 1, 9 * rows)
+        unit_parts = small_grads[1].reshape(8, 2, 4, HD).transpose(1, 2, 0, 3).reshape(2, 4, shards, unit_cols)
+        unit_parts = unit_parts.transpose(2, 0, 1, 3).reshape(shards, 2, 4 * unit_cols)
+        small = jnp.concatenate([jnp.broadcast_to(norm_parts, (shards, 2, 9 * rows)), unit_parts], axis=2)
+        small = jnp.pad(small, ((0, 0), (0, 0), (0, 2048 - small.shape[2]))).reshape(shards * 2, 16, 128)
+        small = jnp.sum(small_exchange(small, shards, False, True, 13), axis=0).reshape(2048)
+        norm_owned = small[: 9 * rows].reshape(9, rows)
+        unit_owned = small[9 * rows : 9 * rows + 4 * unit_cols].reshape(4, unit_cols)
 
     token_total = float(tokens.shape[0] * shards * 4)
     attn_moment, attn_second, attn_dir = adapt(

time: 765 us -> 436 us (0.57)
  matrix products: 119 us -> 0 us
  local copies, waits for them, and re-layouts: 107 us -> 11.5 us
  Pallas kernels: 465 us -> 406 us
  other arithmetic: 64.2 us -> 17.1 us
    dot_general x30 -> x0, matrix products: 119 us -> none  [the longest x10 28.7 us: weight_grad(): jnp.einsum('rd,rme->mde', left, right.reshape(right.shape[0], -1, COLS),...]
    pallas_call x5 -> x1, Pallas kernels: 225 us -> 173 us  [backward(): pl.pallas_call(partial(backward_kernel, levels, fast), out_shape=[jax.Sha...]
    concatenate x12 -> x0, local copies, waits for them, and re-layouts: 31.6 us -> none  [the longest x1 22.5 us: shards_fn(): jnp.concatenate([weight_grad(first_in, self_qflat), weight_grad(first_in,...]
    slice x14 -> x2, local copies, waits for them, and re-layouts: 34.3 us -> 4.07 us  [the longest x1 4.07 us: shards_fn(): frame_gradient = frame_gradient[:HALF_FRAMES]]
    reduce_sum x17 -> x0, other arithmetic: 23.7 us -> none  [the longest x2 5.31 us: norm_backward(): jnp.sum(gradient * normed, axis=0)]
    convert_element_type x2 -> x0, other arithmetic: 17.1 us -> none  [clip_backward(): (probs * (prob_grad - jnp.sum(probs * prob_grad, axis=-1, keepdims=True))...]
    transpose x5 -> x0, local copies, waits for them, and re-layouts: 8.56 us -> none  [joined(): return panels.transpose(1, 0, 2).reshape(panels.shape[1], -1)]
    pallas_call x2 -> x1, Pallas kernels: 18.7 us -> 11.9 us  [small_exchange(): pl.pallas_call(partial(small_kernel, shards, every, scatter), out_shape=j...]
where the time goes in v3:
time: 436 us
  Pallas kernels  406 us (93%)
  other arithmetic  17.1 us (4%)
  local copies, waits for them, and re-layouts  11.5 us (3%)
    pallas_call x1, Pallas kernels, forward(): pl.pallas_call(partial(forward_kernel, levels, groups, fast), out_shape=[...  221 us
    pallas_call x1, Pallas kernels, backward(): pl.pallas_call(partial(backward_kernel, levels, fast), out_shape=[jax.Sha...  173 us
    pallas_call x1, Pallas kernels, small_exchange(): pl.pallas_call(partial(small_kernel, shards, every, scatter), out_shape=j...  11.9 us

profile of v3, /device:TPU:0, one launch (start us, length us, event | category | flops | bytes accessed | tf_op | source)
XLA Modules:
  0.0 435.6 jit_solution(3060170951879839144)
XLA Ops:
  0.7 0.0 copy-start.3
  0.7 1.2 copy.38
  1.9 2.1 pad_maximum_fusion.refs_0_
  4.0 0.0 copy-done.3
  4.0 1.3 pad.12.refs_2_
  5.3 0.0 copy-done.13
  5.3 0.1 reshape.115
  5.4 0.0 copy-done.8
  5.4 0.6 select_maximum_fusion.refs_4_
  6.0 221.5 %forward.1 = (bf16[224,1024]{1,0:T(8,128)(2,1)}, f32[16,1024]{1,0:T(8,128)}, bf16[448,1024]{1,0:T(8,128)(2,1)}, bf16[2,224,1024]{2,1,0:T(8,128)(2,1)}, bf16[3,2,...) custom-call(bf16[16,128,256]{2,1,0:T(8,128)(2,1)} %pad_maximum_fusio, ...), custom_call_target="tpu_custom_call" | custom-call | tf_op jit(solution)/shard_map/forward/pallas_call | solution.py:637
  227.5 172.8 %backward.1 = (f32[16,128,256]{2,1,0:T(8,128)}, f32[224,1024]{1,0:T(8,128)}, f32[768,1024]{1,0:T(8,128)}, f32[16,128]{1,0:T(8,128)}) custom-call(bf16[2,224,1024]{2,1,0:T(8,128)(2,1)} %get-tuple-element.47.refs_0_, bf16[16,2,4,2,128,256]{5,4,3,2,1,0:T(8,128)(2,1)} %get-tuple-element.48.refs_1_, bf16[8,448,256]{2,1,0:T(8,128)(2,1)} %get-tuple-element.49.refs_2_, ...), custom_call_target="tpu_custom_call" | custom-call | tf_op jit(solution)/shard_map/backward/pallas_call | solution.py:1213
  400.3 0.0 copy-start.2
  400.3 4.1 slice.33
  404.4 0.0 copy-done.2
  404.4 0.2 fusion.7
  404.6 0.0 copy-start
  404.6 0.8 copy-done.1
  405.4 0.7 copy-done.4
  406.2 0.3 copy-done.5
  406.5 3.7 multiply_reduce_fusion
  410.2 0.0 copy-done.9
  410.2 0.1 reshape.118
  410.3 0.7 multiply_reduce_fusion.2
  411.0 0.0 copy-done
  411.0 0.0 copy-start.14
  411.0 0.0 copy-start.15
  411.0 3.8 multiply_reduce_fusion.1
  414.8 0.6 multiply_reduce_fusion.4
  415.4 0.1 reshape.119
  415.5 0.1 select_reduce_fusion.1
  415.7 0.1 reshape.120
  415.8 0.1 concatenate.11
  415.9 0.6 pad_bitcast_fusion.src
  416.5 11.9 %small_exchange_14.1 = f32[32,8,128]{2,1,0:T(8,128)} custom-call(f32[8,128]{1,0:T(8,128)} %pad_bitcast_fusion.src), custom_call_target="tpu_custom_call" | custom-call | tf_op jit(solution)/shard_map/small_exchange_14/pallas_call | solution.py:1279
  428.4 0.9 reduce_sum.118
  429.3 0.6 fusion.4
  429.9 0.1 fusion.8
  430.0 0.1 mul.252
  430.1 1.1 broadcast_multiply_fusion.1
  431.2 0.1 slice_multiply_fusion.1
  431.3 1.2 broadcast_multiply_fusion
  432.5 0.1 select_reduce_fusion
  432.6 0.6 broadcast_multiply_fusion.3
  433.2 0.1 slice_multiply_fusion
  433.3 0.7 broadcast_multiply_fusion.2
  433.9 0.0 copy-done.7
  433.9 0.8 copy.44
  434.7 0.9 copy.45
  (22 shorter events, 0.1 us)
Async XLA Ops:
  0.7 3.4 copy-start.3
  4.0 1.3 copy-start.13
  4.0 1.4 copy-start.8
  400.3 4.1 copy-start.2
  404.4 1.0 copy-start.1
  404.4 1.8 copy-start.4
  404.4 2.1 copy-start.5
  404.6 6.4 %copy-start = (f32[8,128,256]{2,1,0:T(8,128)}, f32[8,128,256]{2,1,0:T(8,128)S(1)}, u32[]{:S(2)}) copy-start(f32[8,128,256]{2,1,0:T(8,128)S(1)} %get-tuple-element.95) | copy-start | bytes 3145732
  406.5 3.7 copy-start.9
  406.5 3.8 copy-start.10
  406.5 3.8 copy-start.11
  410.3 4.6 %copy-start.12 = (f32[4,64]{1,0:T(4,128)}, f32[4,64]{1,0:T(4,128)S(1)}, u32[]{:S(2)}) copy-start(f32[4,64]{1,0:T(4,128)S(1)} %reshape.118) | copy-start | bytes 3076
  411.0 3.8 copy-start.14
  411.0 3.8 copy-start.15
  430.1 3.9 copy-start.7
  431.2 3.5 copy-start.6

commit v4 on v3

v4 whole, which is shorter than its diff:
```python
from functools import partial
from typing import NamedTuple

import jax
import jax.numpy as jnp
from jax import lax
from jax.experimental import pallas as pl
from jax.experimental.pallas import tpu as pltpu
from jax.sharding import Mesh, PartitionSpec as P

D = 1024
HEADS = 16
HD = 64
L = 448
FRAMES = 1500
MATS = 16
COLS = 256

learning_rate = 0.3
DT = pl.DeviceIdType.MESH
AXES = ("dp", "side", "core")


def place():
    dp = lax.axis_index("dp")
    return dp // 2, lax.rem(dp, 2), lax.axis_index("side"), lax.axis_index("core")


def device(z, y, x, c):
    return (z * 2 + y, x, c)


def greet_neighbours(levels):
    z, y, x, c = place()
    bar = pltpu.get_barrier_semaphore()
    pl.semaphore_signal(bar, inc=1, device_id=device(z, y, 1 - x, c), device_id_type=DT)
    pl.semaphore_signal(bar, inc=1, device_id=device(z, 1 - y, x, c), device_id_type=DT)

    @pl.when(z > 0)
    def _():
        pl.semaphore_signal(bar, inc=1, device_id=device(z - 1, y, x, c), device_id_type=DT)

    @pl.when(z < levels - 1)
    def _():
        pl.semaphore_signal(bar, inc=1, device_id=device(z + 1, y, x, c), device_id_type=DT)

    pl.semaphore_wait(
        bar, 2 + jnp.where(z > 0, 1, 0) + jnp.where(z < levels - 1, 1, 0)
    )


class Gather:
    def __init__(self, levels, groups, shard, wide, sems):
        self.levels, self.groups, self.size = levels, groups, MATS // groups
        self.shard, self.wide = shard, wide
        self.own, self.zs, self.zr, self.xs, self.xr, self.ys, self.yr = sems
        self.at = place()
        self.done = 0
        self.total = (groups + LAG) * levels

    @staticmethod
    def semaphores(levels, groups):
        sem = pltpu.SemaphoreType.DMA
        one, pair = sem((groups, levels)), sem((groups, levels, 2))
        return [sem, pair, one, pair, pair, pair, pair]

    def block(self, g, xx, zz, yy):
        return self.wide.at[pl.ds(g * self.size, self.size), xx, zz, yy]

    def mine(self, g):
        return self.shard.at[pl.ds(g * self.size, self.size)]

    def z_copy(self, g, zz, up, own=False):
        z, y, x, c = self.at
        return pltpu.make_async_remote_copy(
            self.mine(g) if own else self.block(g, x, zz, y), self.block(g, x, zz, y), self.zs.at[g, zz, up],
            self.zr.at[g, zz], device_id=device(z + 1 if up else z - 1, y, x, c), device_id_type=DT,
        )

    def x_copy(self, g, zz, yy, own=False):
        z, y, x, c = self.at
        return pltpu.make_async_remote_copy(
            self.mine(g) if own else self.block(g, x, zz, yy), self.block(g, x, zz, yy), self.xs.at[g, zz, yy],
            self.xr.at[g, zz, yy], device_id=device(z, y, 1 - x, c), device_id_type=DT,
        )

    def y_copy(self, g, zz, xx, own=False):
        z, y, x, c = self.at
        return pltpu.make_async_remote_copy(
            self.mine(g) if own else self.block(g, xx, zz, y), self.block(g, xx, zz, y), self.ys.at[g, zz, xx],
            self.yr.at[g, zz, xx], device_id=device(z, 1 - y, x, c), device_id_type=DT,
        )

    def z_send(self, g):
        z = self.at[0]
        for up in (1, 0):
            @pl.when(z < self.levels - 1 if up else z > 0)
            def _():
                self.z_copy(g, z, up, True).start()

    def begin(self):
        z, y, x, c = self.at
        for g in range(min(Z_AHEAD, self.groups)):
            self.z_send(g)
        self.local = pltpu.make_async_copy(self.shard, self.wide.at[:, x, z, y], self.own)
        self.local.start()

    def first(self, g, d):
        z, y, x, c = self.at

        @pl.when(d == 0)
        def _():
            @pl.when(g + Z_AHEAD < self.groups)
            def _():
                self.z_send(g + Z_AHEAD)

            self.x_copy(g, z, y, True).start()
            self.y_copy(g, z, x, True).start()

        for up in (1, 0):
            zz = z - d if up else z + d

            @pl.when((d > 0) & (zz >= 0 if up else zz < self.levels))
            def _():
                self.z_copy(g, zz, up).wait_recv()

                @pl.when(z < self.levels - 1 if up else z > 0)
                def _():
                    self.z_copy(g, zz, up).start()

                self.x_copy(g, zz, y).start()
                self.y_copy(g, zz, x).start()

    def second(self, g, d):
        z, y, x, c = self.at
        for up in (1, 0):
            zz = z - d if up else z + d
            here = zz >= 0 if up else (zz < self.levels) & (d > 0)
            even = lax.rem(zz + self.levels, 2) == 0

            @pl.when(here & even)
            def _():
                self.x_copy(g, zz, y).wait_recv()
                self.y_copy(g, zz, 1 - x).start()

            @pl.when(here & jnp.logical_not(even))
            def _():
                self.y_copy(g, zz, x).wait_recv()
                self.x_copy(g, zz, 1 - y).start()

    def tick(self, t):
        g, d = t // self.levels, lax.rem(t, self.levels)

        @pl.when((g >= LAG) & (g < self.groups + LAG))
        def _():
            self.second(g - LAG, d)

        @pl.when(g < self.groups)
        def _():
            self.first(g, d)

    def run(self, count):
        count = max(0, min(count, self.total - self.done))
        start = self.done
        self.done += count
        if count:
            loop(count, lambda i: self.tick(start + i))

    def turn(self, count):
        start = self.done
        self.done = min(self.total, self.done + count)
        return lambda i: self.tick(start + i)

    def need(self, mat):
        g = mat // self.size
        self.run((g + 1 + LAG) * self.levels - self.done)
        z, y, x, c = self.at

        def body(zz):
            @pl.when(lax.rem(zz, 2) == 0)
            def _():
                self.y_copy(g, zz, x).wait_recv()
                self.y_copy(g, zz, 1 - x).wait_recv()

            @pl.when(lax.rem(zz, 2) == 1)
            def _():
                self.x_copy(g, zz, y).wait_recv()
                self.x_copy(g, zz, 1 - y).wait_recv()

        if mat % self.size == 0:
            loop(self.levels, body)
        if mat == 0:
            self.local.wait()

    def drain(self):
        z, y, x, c = self.at

        def group(g):
            def sent(zz):
                self.x_copy(g, zz, y).wait_send()
                self.y_copy(g, zz, x).wait_send()

                @pl.when(lax.rem(zz, 2) == 0)
                def _():
                    self.y_copy(g, zz, 1 - x).wait_send()

                @pl.when(lax.rem(zz, 2) == 1)
                def _():
                    self.x_copy(g, zz, 1 - y).wait_send()

            loop(self.levels, sent)

            def relayed(zz):
                @pl.when((z < self.levels - 1) & (zz <= z))
                def _():
                    self.z_copy(g, zz, 1).wait_send()

                @pl.when((z > 0) & (zz >= z))
                def _():
                    self.z_copy(g, zz, 0).wait_send()

            loop(self.levels, relayed)

        loop(self.groups, group)


LAG = 2
Z_AHEAD = 1
GROUPS = 8
HALF = L // 2
KEYS = 768
HALF_FRAMES = FRAMES // 2
BLOCK = 32
SOFT_TURNS = 14
NORM_TURNS = 7
BACK_TURNS = 12


def dot(a, b, dims):
    return lax.dot_general(a, b, (dims, ((), ())), preferred_element_type=jnp.float32)


NN, NT, TN = ((1,), (0,)), ((1,), (1,)), ((0,), (0,))


def flat_panel(ref, mat, side):
    return ref[mat, side].reshape(D, COLS)


def flat_rows(panel, j):
    per = COLS // (2 * panel.shape[2])
    return panel[pl.ds(j * per, per)].reshape(COLS, COLS)


def rows_loop(count, body, turns=1):
    def run(k, carry):
        for u in range(turns):
            i = k * turns + u
            body(pl.ds(pl.multiple_of(i * BLOCK, BLOCK), BLOCK), i)
        return carry

    lax.fori_loop(0, count // (BLOCK * turns), run, 0)


def loop(count, body):
    def run(i, carry):
        body(i)
        return carry

    lax.fori_loop(0, count, run, 0)


def normed_block(values):
    centre = values - jnp.mean(values, axis=-1, keepdims=True)
    spread = jnp.mean(centre * centre, axis=-1, keepdims=True)
    scaled = lax.rsqrt(spread + 1e-05)
    return centre * scaled, scaled


def panels_row(ref, rows):
    return jnp.concatenate([ref[j, rows, :].astype(jnp.float32) for j in range(4)], axis=1)


def forward_kernel(levels, groups, fast, *refs):
    f32, bf = jnp.float32, jnp.bfloat16
    width = len(ForwardRefs._fields)
    r = ForwardRefs(*refs[:width])
    gather = Gather(levels, groups, r.shard, r.wide, refs[width:])
    z, y, x, c = place()
    dp = z * 2 + y
    mate = (dp, x, 1 - c)
    count = levels * 4
    me = dp * 2 + x

    def peer(i):
        return (i // 2, lax.rem(i, 2), c)

    bar = pltpu.get_barrier_semaphore()
    loop(count - 1, lambda k: pl.semaphore_signal(
        bar, inc=1, device_id=peer(lax.rem(me + k + 1, count)), device_id_type=DT))
    pl.semaphore_signal(bar, inc=1, device_id=mate, device_id_type=DT)
    pl.semaphore_wait(bar, count)

    def remote(src, dst, send, recv, dev):
        return pltpu.make_async_remote_copy(src, dst, send, recv, device_id=dev, device_id_type=DT)

    inputs = ((r.tokens, r.x), (r.frames, r.e), (r.cotangent, r.dy))

    def swap(k, slot):
        src, dst = inputs[k]
        return remote(src, dst.at[slot], r.swap_send.at[k], r.swap_recv.at[k], mate)

    def local(k):
        src, dst = inputs[k]
        return pltpu.make_async_copy(src, dst.at[c], r.in_sem.at[k])

    if fast:
        def pack_copy(k, slot):
            return remote(r.pack, r.packs.at[slot], r.pack_send.at[k], r.pack_recv.at[slot],
                          peer(lax.rem(me + k + 1, count)))

        loop(count - 1, lambda k: pack_copy(k, me).start())
        own_pack = pltpu.make_async_copy(r.pack, r.packs.at[me], r.in_sem.at[3])
        own_pack.start()
    swap(0, c).start()
    local(0).start()
    gather.begin()
    gather.run(1)
    for k in (1, 2):
        swap(k, c).start()
        local(k).start()

    def arrived(k):
        local(k).wait()
        swap(k, 1 - c).wait_recv()

    outs = []

    def emit(out, scratch):
        outs.append(pltpu.make_async_copy(scratch, out, r.out_sem.at[len(outs)]))
        outs[-1].start()

    if fast:
        own_pack.wait()
        loop(count - 1, lambda k: pack_copy(k, lax.rem(me + k + 1, count)).wait_recv())
        for i in range(2 * levels):
            for xx in range(2):
                block = r.packs[i * 2 + xx]
                if xx == 0:
                    r.norm[:, i * 128 : (i + 1) * 128] = block
                r.bias[i * 2 + xx : i * 2 + xx + 1, 0:128] = block[9:10]
                r.bias[i * 2 + xx : i * 2 + xx + 1, 128:256] = block[10:11]
    else:
        r.norm[...] = r.norm_in[...]
        r.bias[...] = r.bias_in[...]
    emit(r.norm_out, r.norm)

    def norm_row(k):
        return r.norm[k : k + 1, :]

    def bias_row(k, side):
        return r.bias[pl.ds(k * 2 + side, 1), :]

    key = lax.broadcasted_iota(jnp.int32, (1, 2 * KEYS), 1)
    real = lax.rem(key, KEYS) < HALF_FRAMES
    r.padrow[0:1, :] = jnp.where(real, 0.0, -1e30).astype(f32)
    for i in range(3):
        for side in range(2):
            r.qkv[i, side, L:512, :] = jnp.zeros((512 - L, COLS), bf)

    arrived(0)

    def ln1(half):
        def body(rows, i):
            normed, _ = normed_block(r.x[half, rows, :].astype(f32))
            out = (normed * norm_row(0) + norm_row(1)).astype(bf)
            r.a1[pl.ds(pl.multiple_of(half * HALF + i * BLOCK, BLOCK), BLOCK), :] = out

        rows_loop(HALF, body, NORM_TURNS if NORM_TURNS in (1, 7) else 1)

    ln1(0)
    ln1(1)
    emit(r.a1_out, r.a1)
    emit(r.x_out, r.x)

    def project_one(i, side):
        bias = bias_row(0, side) if i == 0 else bias_row(1, side)
        acc = dot(r.a1[...], flat_panel(r.wide, i, side), NN)
        if i != 1:
            acc = acc + bias
        r.qkv[i, side, 0:L, :] = acc.astype(bf)

    for i in range(3):
        gather.need(i)
        loop(2, lambda side: project_one(i, side))
    emit(r.qkv_out, r.qkv)

    lane = lax.broadcasted_iota(jnp.int32, (1, 128), 1)
    low = lane < HD

    def attend(query, key_parts, values, width, causal, lse, ctx, per_head, tick):
        def body(t):
            side, half = t // 2, lax.rem(t, 2)
            lanes = pl.ds(pl.multiple_of(half * 128, 128), 128)
            q = query(side, lanes)
            found = []
            for sub in range(2):
                mine = low if sub == 0 else jnp.logical_not(low)
                qh = jnp.where(mine, q.astype(f32) * 0.125, 0.0).astype(bf)
                for n, part in enumerate(key_parts(side, lanes)):
                    r.s[:, n * width : (n + 1) * width] = dot(qh, part, NT)
                total = width * len(key_parts(side, lanes))

                def rows_body(rows, i):
                    s = r.s[rows, 0:total]
                    if causal:
                        row = i * BLOCK + lax.broadcasted_iota(jnp.int32, (BLOCK, total), 0)
                        col = lax.broadcasted_iota(jnp.int32, (BLOCK, total), 1)
                        s = jnp.where(col <= row, s, -1e30)
                    else:
                        s = s + r.padrow[0:1, 0:total]
                    top = jnp.max(s, axis=-1, keepdims=True)
                    e = jnp.exp(s - top)
                    weight = jnp.sum(e, axis=-1, keepdims=True)
                    r.p[rows, 0:total] = (e * (1.0 / weight)).astype(bf)
                    lse[rows, :] = jnp.where(lane == t * 2 + sub, top + jnp.log(weight), lse[rows, :])

                rows_loop(L, rows_body, SOFT_TURNS)
                for i in range(per_head):
                    tick((t * 2 + sub) * per_head + i)
                acc = None
                for n, part in enumerate(values(side, lanes)):
                    more = dot(r.p[:, n * width : (n + 1) * width], part, NN)
                    acc = more if acc is None else acc + more
                found.append(acc)
            ctx[side, :, lanes] = jnp.where(low, found[0], found[1]).astype(bf)

        loop(4, body)

    attend(
        lambda side, lanes: r.qkv[0, side, 0:L, lanes],
        lambda side, lanes: [r.qkv[1, side, :, lanes]],
        lambda side, lanes: [r.qkv[2, side, :, lanes]],
        512, True, r.lse1, r.c1, 1, gather.turn(8),
    )
    emit(r.lse1_out, r.lse1)
    emit(r.c1_out, r.c1)

    def collect(n, ctx, mat):
        def body(j):
            rows = pl.ds(pl.multiple_of(j * COLS, COLS), COLS)
            acc = None
            for side in range(2):
                more = dot(ctx[side], flat_rows(r.wide.at[mat, side], j), NT)
                acc = more if acc is None else acc + more
            r.part[n, j] = acc.astype(bf)
            trade(n, j).start()

        loop(4, body)

    def trade(n, j):
        return remote(r.part.at[n, j], r.got.at[n, j], r.part_send.at[n, j], r.part_recv.at[n, j], mate)

    def traded(n):
        loop(4, lambda j: trade(n, j).wait_recv())

    def residual(n, base, bias_k, out, gain_k, normed_out):
        def body(rows, i):
            v = base(rows, i) + norm_row(bias_k) + (panels_row(r.part.at[n], rows) + panels_row(r.got.at[n], rows))
            out[rows, :] = v
            normed, _ = normed_block(v)
            normed_out[rows, :] = (normed * norm_row(gain_k) + norm_row(gain_k + 1)).astype(bf)

        rows_loop(L, body, NORM_TURNS)

    def x_rows(rows, i):
        half = i // (HALF // BLOCK)
        inner = pl.ds(pl.multiple_of((i - half * (HALF // BLOCK)) * BLOCK, BLOCK), BLOCK)
        return r.x[half, inner, :].astype(f32)

    gather.need(3)
    collect(0, r.c1, 3)
    gather.run(1)
    traded(0)
    residual(0, x_rows, 6, r.h1, 2, r.a2)
    emit(r.h1_out, r.h1)
    emit(r.a2_out, r.a2)

    gather.need(4)

    def query_two(side):
        acc = dot(r.a2[...], flat_panel(r.wide, 4, side), NN) + bias_row(2, side)
        r.q2[side] = acc.astype(bf)

    loop(2, query_two)
    emit(r.q2_out, r.q2)
    arrived(1)
    emit(r.e_out, r.e)

    gather.need(5)

    def frame_keys(t):
        side, half = t // 2, lax.rem(t, 2)
        r.ek[side, half] = dot(r.e[half], flat_panel(r.wide, 5, side), NN).astype(bf)

    loop(4, frame_keys)
    emit(r.ek_out, r.ek)
    gather.need(6)

    def frame_values(t):
        side, half = t // 2, lax.rem(t, 2)
        acc = dot(r.e[half], flat_panel(r.wide, 6, side), NN) + bias_row(3, side)
        r.ev[side, half] = acc.astype(bf)

    loop(4, frame_values)
    emit(r.ev_out, r.ev)
    attend(
        lambda side, lanes: r.q2[side, :, lanes],
        lambda side, lanes: [r.ek[side, half, :, lanes] for half in range(2)],
        lambda side, lanes: [r.ev[side, half, :, lanes] for half in range(2)],
        KEYS, False, r.lse2, r.c2, 2, gather.turn(16),
    )
    emit(r.lse2_out, r.lse2)
    emit(r.c2_out, r.c2)
    gather.need(7)
    collect(1, r.c2, 7)
    gather.run(1)
    traded(1)
    residual(1, lambda rows, i: r.h1[rows, :], 7, r.h2, 4, r.a3)
    emit(r.h2_out, r.h2)
    emit(r.a3_out, r.a3)
    arrived(2)
    emit(r.dy_out, r.dy)

    def hidden(t):
        m, side = t // 2, lax.rem(t, 2)
        u = dot(r.a3[...], flat_panel(r.wide, 8 + m, side), NN) + bias_row(4 + m, side)
        half = 0.5 * (1.0 + lax.erf(u * 0.7071067811865476))
        r.z[t] = (u * half).astype(bf)
        r.slope[t] = (half + u * jnp.exp(-0.5 * u * u) * 0.3989422804014327).astype(bf)

    def result(k):
        def tile(j):
            cols = pl.ds(pl.multiple_of(j * COLS, COLS), COLS)
            acc = None
            for t in range(4 * k, 4 * k + 4):
                more = dot(r.z[t], flat_rows(r.wide.at[12 + t // 2, t % 2], j), NT)
                acc = more if acc is None else acc + more
            if k == 0:
                r.acc[:, cols] = acc
            else:
                r.acc[:, cols] += acc

        loop(4, tile)

    for m in range(4):
        gather.need(8 + m)
        loop(2, lambda side: hidden(2 * m + side))
    emit(r.z_out, r.z)
    emit(r.slope_out, r.slope)
    for k in range(2):
        gather.need(12 + 2 * k)
        gather.need(13 + 2 * k)
        result(k)

    emit(r.wide_out, r.wide)

    for half in range(2):
        @pl.when(c == half)
        def _():
            far = (1 - half) * HALF

            def body(j):
                cols = pl.ds(pl.multiple_of(j * COLS, COLS), COLS)
                r.part[2, j, 0:HALF, :] = r.acc[far : far + HALF, cols].astype(bf)

            loop(4, body)

    last = remote(
        r.part.at[2, :, 0:HALF], r.got.at[2, :, 0:HALF], r.part_send.at[2, 0], r.part_recv.at[2, 0], mate
    )
    last.start()
    last.wait_recv()

    def finish(rows, i):
        here = pl.ds(pl.multiple_of(c * HALF + i * BLOCK, BLOCK), BLOCK)
        own = r.acc[here, :].astype(bf).astype(f32)
        v = r.h2[here, :] + norm_row(8) + (own + panels_row(r.got.at[2], rows))
        r.outrows[rows, :] = v.astype(bf)

    rows_loop(HALF, finish)
    emit(r.layer_out, r.outrows)

    for k in range(3):
        swap(k, c).wait_send()
    if fast:
        loop(count - 1, lambda k: pack_copy(k, me).wait_send())
    for n in range(2):
        loop(4, lambda j: trade(n, j).wait_send())
    last.wait_send()
    gather.drain()
    for copy in outs:
        copy.wait()


class ForwardRefs(NamedTuple):
    shard: object
    tokens: object
    frames: object
    cotangent: object
    pack: object
    norm_in: object
    bias_in: object
    layer_out: object
    norm_out: object
    a1_out: object
    x_out: object
    qkv_out: object
    lse1_out: object
    c1_out: object
    h1_out: object
    a2_out: object
    q2_out: object
    e_out: object
    ek_out: object
    ev_out: object
    lse2_out: object
    c2_out: object
    h2_out: object
    a3_out: object
    dy_out: object
    z_out: object
    slope_out: object
    wide_out: object
    wide: object
    x: object
    dy: object
    e: object
    norm: object
    bias: object
    a1: object
    a2: object
    a3: object
    h1: object
    h2: object
    qkv: object
    c1: object
    q2: object
    c2: object
    ek: object
    ev: object
    lse1: object
    lse2: object
    z: object
    slope: object
    s: object
    p: object
    acc: object
    part: object
    got: object
    packs: object
    padrow: object
    outrows: object
    in_sem: object
    swap_send: object
    swap_recv: object
    part_send: object
    part_recv: object
    pack_send: object
    pack_recv: object
    out_sem: object


class Kept(NamedTuple):
    layer_out: object
    norm: object
    a1: object
    x: object
    qkv: object
    lse1: object
    c1: object
    h1: object
    a2: object
    q2: object
    e: object
    ek: object
    ev: object
    lse2: object
    c2: object
    h2: object
    a3: object
    dy: object
    z: object
    slope: object
    wide: object


def forward(shard, tokens, frames, cotangent, small, shards):
    levels, rows = shards // 2, D // shards
    groups = GROUPS if levels <= 4 else 4
    fast = rows == 128
    f32, bf = jnp.float32, jnp.bfloat16
    sem = pltpu.SemaphoreType.DMA
    vm, hbm = pl.BlockSpec(memory_space=pltpu.VMEM), pl.BlockSpec(memory_space=pl.ANY)
    wide = (MATS, 2, levels, 2, rows, COLS)
    shapes = [
        ((HALF, D), bf),
        ((16, D), f32),
        ((L, D), bf),
        ((2, HALF, D), bf),
        ((3, 2, 512, COLS), bf),
        ((L, 128), f32),
        ((2, L, COLS), bf),
        ((L, D), f32),
        ((L, D), bf),
        ((2, L, COLS), bf),
        ((2, KEYS, D), bf),
        ((2, 2, KEYS, COLS), bf),
        ((2, 2, KEYS, COLS), bf),
        ((L, 128), f32),
        ((2, L, COLS), bf),
        ((L, D), f32),
        ((L, D), bf),
        ((2, HALF, D), bf),
        ((8, L, COLS), bf),
        ((8, L, COLS), bf),
        (wide, bf),
    ]
    peers = shards * 2
    scratch = [
        pltpu.VMEM(wide, bf), pltpu.VMEM((2, HALF, D), bf), pltpu.VMEM((2, HALF, D), bf), pltpu.VMEM((2, KEYS, D), bf),
        pltpu.VMEM((16, D), f32), pltpu.VMEM((16, COLS), f32),
        pltpu.VMEM((L, D), bf), pltpu.VMEM((L, D), bf), pltpu.VMEM((L, D), bf),
        pltpu.VMEM((L, D), f32), pltpu.VMEM((L, D), f32),
        pltpu.VMEM((3, 2, 512, COLS), bf), pltpu.VMEM((2, L, COLS), bf), pltpu.VMEM((2, L, COLS), bf),
        pltpu.VMEM((2, L, COLS), bf), pltpu.VMEM((2, 2, KEYS, COLS), bf), pltpu.VMEM((2, 2, KEYS, COLS), bf),
        pltpu.VMEM((L, 128), f32), pltpu.VMEM((L, 128), f32),
        pltpu.VMEM((8, L, COLS), bf), pltpu.VMEM((8, L, COLS), bf),
        pltpu.VMEM((L, 2 * KEYS), f32), pltpu.VMEM((L, 2 * KEYS), bf), pltpu.VMEM((L, D), f32),
        pltpu.VMEM((3, 4, L, COLS), bf), pltpu.VMEM((3, 4, L, COLS), bf),
        pltpu.VMEM((peers, 16, 128) if fast else (1, 16, 128), f32), pltpu.VMEM((8, 2 * KEYS), f32),
        pltpu.VMEM((HALF, D), bf),
        sem((4,)), sem((3,)), sem((3,)), sem((3, 4)), sem((3, 4)), sem((peers,)), sem((peers,)),
        sem((len(shapes),)),
    ]
    outs = pl.pallas_call(
        partial(forward_kernel, levels, groups, fast),
        out_shape=[jax.ShapeDtypeStruct(s, t) for s, t in shapes],
        in_specs=[vm, hbm, hbm, hbm, vm, vm, vm],
        out_specs=[hbm] * len(shapes),
        scratch_shapes=scratch + Gather.semaphores(levels, groups),
        compiler_params=pltpu.CompilerParams(
            collective_id=0, has_side_effects=True, vmem_limit_bytes=63 * 2**20
        ),
        name="forward",
    )(shard, tokens, frames, cotangent, *small)
    return Kept(*outs)


RING = 4


class Scatter:
    def __init__(self, levels, part, own, bufs, sems):
        self.levels, self.part, self.own = levels, part, own
        self.one_y, self.one_x, self.two_x, self.two_y, self.line = bufs
        self.s1, self.r1, self.s2, self.r2, self.s3, self.r3 = sems
        self.at = place()
        self.sent = self.steps = self.ready = 0

    @staticmethod
    def buffers(levels, rows):
        bf, half = jnp.bfloat16, levels // 2
        return [
            pltpu.VMEM((RING, 2, half, rows, COLS), bf), pltpu.VMEM((RING, half, 2, rows, COLS), bf),
            pltpu.VMEM((RING, half, rows, COLS), bf), pltpu.VMEM((RING, half, rows, COLS), bf),
            pltpu.VMEM((RING, levels, rows, COLS), bf),
        ]

    @staticmethod
    def semaphores(levels):
        sem = pltpu.SemaphoreType.DMA
        two = sem((MATS, 2))
        many = sem((MATS, levels))
        return [two, two, two, two, many, many]

    def to_x(self, src, dst, send, recv):
        z, y, x, c = self.at
        return pltpu.make_async_remote_copy(src, dst, send, recv, device_id=device(z, y, 1 - x, c), device_id_type=DT)

    def to_y(self, src, dst, send, recv):
        z, y, x, c = self.at
        return pltpu.make_async_remote_copy(src, dst, send, recv, device_id=device(z, 1 - y, x, c), device_id_type=DT)

    def first(self, g):
        z, y, x, c = self.at
        m, slot = MATS - 1 - g, lax.rem(g, RING)
        return (
            self.to_y(self.part.at[m, :, :, 0, 1 - y], self.one_y.at[slot], self.s1.at[g, 0], self.r1.at[g, 0]),
            self.to_x(self.part.at[m, 1 - x, :, 1], self.one_x.at[slot], self.s1.at[g, 1], self.r1.at[g, 1]),
        )

    def second(self, g):
        z, y, x, c = self.at
        m, slot = MATS - 1 - g, lax.rem(g, RING)
        return (
            self.to_x(self.part.at[m, 1 - x, :, 0, y], self.two_x.at[slot], self.s2.at[g, 0], self.r2.at[g, 0]),
            self.to_y(self.part.at[m, x, :, 1, 1 - y], self.two_y.at[slot], self.s2.at[g, 1], self.r2.at[g, 1]),
        )

    def third(self, g, zz, k):
        z, y, x, c = self.at
        return pltpu.make_async_remote_copy(
            self.part.at[MATS - 1 - g, x, zz // 2, lax.rem(zz, 2), y], self.line.at[lax.rem(g, RING), k],
            self.s3.at[g, zz], self.r3.at[g, k], device_id=device(zz, y, x, c), device_id_type=DT,
        )

    def send(self, count):
        def body(i):
            for copy in self.first(i):
                copy.start()

        start = self.sent
        self.sent += count
        loop(count, lambda i: body(start + i))

    def add(self, at, got):
        self.part[at] = (self.part[at].astype(jnp.float32) + got.astype(jnp.float32)).astype(jnp.bfloat16)

    def step_a(self, g):
        z, y, x, c = self.at
        m, slot = MATS - 1 - g, lax.rem(g, RING)
        along_y, along_x = self.first(g)
        then_x, then_y = self.second(g)
        along_y.wait_recv()
        for k in range(2):
            loop(self.levels // 2, lambda h: self.add((m, k, h, 0, y), self.one_y[slot, k, h]))
        then_x.start()
        along_x.wait_recv()
        for k in range(2):
            loop(self.levels // 2, lambda h: self.add((m, x, h, 1, k), self.one_x[slot, h, k]))
        then_y.start()

    def step_b(self, g):
        z, y, x, c = self.at
        m, slot = MATS - 1 - g, lax.rem(g, RING)
        then_x, then_y = self.second(g)
        then_x.wait_recv()
        loop(self.levels // 2, lambda h: self.add((m, x, h, 0, y), self.two_x[slot, h]))
        then_y.wait_recv()
        loop(self.levels // 2, lambda h: self.add((m, x, h, 1, y), self.two_y[slot, h]))
        loop(self.levels - 1, lambda k: self.third(g, lax.rem(z + k + 1, self.levels), z).start())

    def step_c(self, g):
        z, y, x, c = self.at
        m = MATS - 1 - g
        loop(self.levels - 1, lambda k: self.third(g, z, lax.rem(z + k + 1, self.levels)).wait_recv())
        self.own[m] = self.part[m, x, z // 2, lax.rem(z, 2), y].astype(jnp.float32)

        def body(k):
            @pl.when(k != z)
            def _():
                self.own[m] += self.line[lax.rem(g, RING), k].astype(jnp.float32)

        loop(self.levels, body)

    def step(self, t):
        @pl.when(t < MATS)
        def _():
            self.step_a(t)

        @pl.when((t >= 1) & (t <= MATS))
        def _():
            self.step_b(t - 1)

        @pl.when(t >= 2)
        def _():
            self.step_c(t - 2)

    def turn(self, count):
        start, first = self.steps, self.sent
        self.steps += count
        self.sent = max(first, min(MATS, self.steps + RING - 2))
        assert self.sent <= self.ready

        def body(i):
            t = start + i
            self.step(t)
            g = t + RING - 2

            @pl.when((g >= first) & (g < MATS))
            def _():
                for copy in self.first(g):
                    copy.start()

        return body

    def run(self, count):
        loop(count, self.turn(count))

    def drain(self):
        z, y, x, c = self.at

        def body(g):
            for copy in (*self.first(g), *self.second(g)):
                copy.wait_send()
            loop(self.levels - 1, lambda k: self.third(g, lax.rem(z + k + 1, self.levels), z).wait_send())

        loop(MATS, body)


class BackwardIn(NamedTuple):
    dy: object
    wide: object
    slope: object
    z: object
    a3: object
    h2: object
    norm: object
    c2: object
    q2: object
    lse2: object
    ek: object
    ev: object
    e: object
    a2: object
    h1: object
    c1: object
    qkv: object
    lse1: object
    a1: object
    x: object


class BackwardRefs(NamedTuple):
    owned_out: object
    input_out: object
    frame_out: object
    small_out: object
    bcols_out: object
    part: object
    own: object
    dy: object
    slope: object
    z: object
    left: object
    h: object
    norm: object
    c2: object
    q2: object
    lse2: object
    ek: object
    ev: object
    e: object
    a2: object
    c1: object
    qkv: object
    lse1: object
    x: object
    dh: object
    dhb: object
    dc: object
    stat: object
    s: object
    dp: object
    p: object
    ds: object
    mine: object
    got: object
    fsend: object
    frecv: object
    fout: object
    cols: object
    bcols: object
    small: object
    smallgot: object
    smallsum: object
    in_sem: object
    trade_send: object
    trade_recv: object
    frame_send: object
    frame_recv: object
    frame_out_sem: object
    small_send: object
    small_recv: object
    out_sem: object


def backward_kernel(levels, fast, *refs):
    f32, bf = jnp.float32, jnp.bfloat16
    at, width = len(BackwardIn._fields), len(BackwardRefs._fields)
    given = BackwardIn(*refs[:at])
    r = BackwardRefs(*refs[at : at + width])
    rest = refs[at + width :]
    scatter = Scatter(levels, r.part, r.own, rest[:5], rest[5:])
    z, y, x, c = place()
    dp = z * 2 + y
    mate = (dp, x, 1 - c)
    count = levels * 4
    me = dp * 2 + x
    rows_of = D // (levels * 2)
    per = COLS // (2 * rows_of)

    def peer(i):
        return (i // 2, lax.rem(i, 2), c)

    loads = []

    def load(src, dst):
        loads.append(pltpu.make_async_copy(src, dst, r.in_sem.at[len(loads)]))
        loads[-1].start()
        return loads[-1]

    def loaded(*which):
        for copy in which:
            copy.wait()

    get_dy = load(given.dy, r.dy)
    get_w2 = load(given.wide.at[12:16], r.part.at[12:16])
    get_slope = load(given.slope, r.slope)
    get_z = load(given.z, r.z)
    get_w1 = load(given.wide.at[8:12], r.part.at[8:12])
    get_a3 = load(given.a3, r.left)
    get_h2 = load(given.h2, r.h)
    get_w0 = load(given.wide.at[0:8], r.part.at[0:8])
    get_norm = load(given.norm, r.norm)
    get_c2 = load(given.c2, r.c2)
    get_q2 = load(given.q2, r.q2)
    get_lse2 = load(given.lse2, r.lse2)
    get_ek = load(given.ek, r.ek)
    get_ev = load(given.ev, r.ev)
    get_e = load(given.e, r.e)
    get_a2 = load(given.a2, r.a2)
    get_c1 = load(given.c1, r.c1)
    get_qkv = load(given.qkv, r.qkv)
    get_lse1 = load(given.lse1, r.lse1)
    get_x = load(given.x, r.x)

    bar = pltpu.get_barrier_semaphore()
    loop(count - 1, lambda k: pl.semaphore_signal(
        bar, inc=1, device_id=peer(lax.rem(me + k + 1, count)), device_id_type=DT))
    pl.semaphore_signal(bar, inc=1, device_id=mate, device_id_type=DT)
    pl.semaphore_wait(bar, count)

    def remote(src, dst, send, recv, dev):
        return pltpu.make_async_remote_copy(src, dst, send, recv, device_id=dev, device_id_type=DT)

    def trade(n, j):
        return remote(r.mine.at[n % 2, j], r.got.at[n % 2, j], r.trade_send.at[n, j],
                      r.trade_recv.at[n, j], mate)

    def panel(mat, side):
        return r.part[mat, side].reshape(D, COLS)

    def part_rows(mat, side, j):
        if per == 1:
            return r.part[mat, side, j // 2, lax.rem(j, 2)].reshape(COLS, COLS)
        return r.part[mat, side, pl.ds(j * (per // 2), per // 2)].reshape(COLS, COLS)

    def grads(lefts, items):
        def body(j):
            cols = pl.ds(pl.multiple_of(j * COLS, COLS), COLS)
            turned = [v.T for v in lefts(cols)]
            for mat, side, rights in items:
                acc = None
                for t, right in zip(turned, rights()):
                    more = dot(t, right, NN)
                    acc = more if acc is None else acc + more
                if per == 1:
                    r.part[mat, side, j // 2, lax.rem(j, 2)] = acc.astype(bf).reshape(2, rows_of, COLS)
                else:
                    blocks = pl.ds(j * (per // 2), per // 2)
                    r.part[mat, side, blocks] = acc.astype(bf).reshape(per // 2, 2, 2, rows_of, COLS)

        loop(4, body)

    def send_back(n, items):
        if n >= 2:
            loop(4, lambda j: trade(n - 2, j).wait_send())

        def body(j):
            acc = None
            for value, mat, side in items:
                more = dot(value(), part_rows(mat, side, j), NT)
                acc = more if acc is None else acc + more
            r.mine[n % 2, j] = acc.astype(bf)
            trade(n, j).start()

        loop(4, body)

    def fold(v):
        return jnp.sum(v.reshape(BLOCK // 8, 8, D), axis=0)

    def norm_row(k):
        return r.norm[k : k + 1, :]

    def grow(k, v):
        r.cols[k * 8 : (k + 1) * 8, :] += fold(v)

    def half_rows(ref, i):
        half = i // (HALF // BLOCK)
        inner = pl.ds(pl.multiple_of((i - half * (HALF // BLOCK)) * BLOCK, BLOCK), BLOCK)
        return ref[half, inner, :].astype(f32)

    def norm_back(n, k, base, incoming, sum_k):
        loop(4, lambda j: trade(n, j).wait_recv())

        def body(rows, i):
            normed, scaled = normed_block(base(rows, i))
            dn = panels_row(r.mine.at[n % 2], rows) + panels_row(r.got.at[n % 2], rows)
            inner = dn * norm_row(k)
            back = scaled * (
                inner - jnp.mean(inner, axis=-1, keepdims=True)
                - normed * jnp.mean(inner * normed, axis=-1, keepdims=True)
            )
            came = incoming(rows, i)
            out = came + back
            r.dh[rows, :] = out
            grow(k, dn * normed)
            grow(k + 1, dn)
            if sum_k is not None:
                r.dhb[rows, :] = out.astype(bf)
                grow(sum_k, out)
            if n == 0:
                grow(8, came)

        rows_loop(L, body, NORM_TURNS)

    r.cols[...] = jnp.zeros((72, D), f32)
    loaded(get_dy, get_w2, get_slope)

    def hidden_back(t):
        m, side = t // 2, lax.rem(t, 2)
        du = (dot(r.dy[...].reshape(L, D), panel(12 + m, side), NN) * r.slope[t].astype(f32)).astype(bf)
        r.slope[t] = du
        r.bcols[pl.ds(8 + t, 1), :] = jnp.sum(du.astype(f32), axis=0, keepdims=True)

    loop(8, hidden_back)
    loaded(get_z)
    grads(
        lambda cols: [r.dy[:, :, cols].reshape(L, COLS)],
        [(12 + t // 2, t % 2, lambda t=t: [r.z[t]]) for t in range(8)],
    )
    scatter.send(4)
    loaded(get_w1)
    send_back(0, [(lambda t=t: r.slope[t], 8 + t // 2, t % 2) for t in range(8)])
    loaded(get_a3, get_h2, get_norm)
    grads(
        lambda cols: [r.left[:, cols]],
        [(8 + t // 2, t % 2, lambda t=t: [r.slope[t]]) for t in range(8)],
    )
    scatter.ready = 8
    get_a1 = load(given.a1, r.left)
    norm_back(0, 4, lambda rows, i: r.h[rows, :], lambda rows, i: half_rows(r.dy, i), 7)
    get_h1 = load(given.h1, r.h)
    scatter.run(1)
    loaded(get_w0)

    def context_back(mat):
        def body(side):
            r.dc[side] = dot(r.dhb[...], panel(mat, side), NN).astype(bf)

        loop(2, body)

    def statistics(lse, ctx):
        r.stat[0:8, :] = lse[...].T[0:8, :]
        for side in range(2):
            both = (r.dc[side].astype(f32) * ctx[side].astype(f32)).T
            r.stat[8 + side * 4 : 12 + side * 4, :] = jnp.sum(both.reshape(4, HD, L), axis=1)

    lane = lax.broadcasted_iota(jnp.int32, (1, 128), 1)
    low = lane < HD
    low_row = lax.broadcasted_iota(jnp.int32, (128, 1), 0) < HD

    def attend_back(query, keys, values, parts, width, causal, turn):
        def body(t):
            side, half = t // 2, lax.rem(t, 2)
            lanes = pl.ds(pl.multiple_of(half * 128, 128), 128)
            q = query[(side, slice(0, L), lanes)].astype(f32) * 0.125
            dc = r.dc[side, :, lanes].astype(f32)
            back = None
            for n in range(parts):
                at = (side, n, slice(None), lanes) if parts > 1 else (side, slice(0, L), lanes)
                k, v = keys[at], values[at]
                flat = k.T
                dk = dv = None
                for sub in range(2):
                    mine = low if sub == 0 else jnp.logical_not(low)
                    mine_row = low_row if sub == 0 else jnp.logical_not(low_row)
                    qh = jnp.where(mine, q, 0.0).astype(bf)
                    dm = jnp.where(mine, dc, 0.0).astype(bf)
                    kt = jnp.where(mine_row, flat.astype(f32), 0.0).astype(bf)
                    r.s[0:width, :] = dot(k, qh, NT)
                    r.dp[0:width, :] = dot(v, dm, NT)
                    lse = r.stat[pl.ds(t * 2 + sub, 1), :]
                    delta = r.stat[pl.ds(8 + t * 2 + sub, 1), :]

                    def rows_body(rows, i):
                        key = i * BLOCK + lax.broadcasted_iota(jnp.int32, (BLOCK, L), 0)
                        if causal:
                            keep = lax.broadcasted_iota(jnp.int32, (BLOCK, L), 1) >= key
                        else:
                            keep = key < HALF_FRAMES
                        p = jnp.where(keep, jnp.exp(jnp.where(keep, r.s[rows, :], -1e30) - lse), 0.0)
                        r.p[rows, :] = p.astype(bf)
                        r.ds[rows, :] = (p * (r.dp[rows, :] - delta)).astype(bf)

                    rows_loop(width, rows_body, 14 if causal else BACK_TURNS)
                    p, ds = r.p[0:width, :], r.ds[0:width, :]
                    dv = dot(p, dm, NN) if dv is None else dv + dot(p, dm, NN)
                    dk = dot(ds, qh, NN) if dk is None else dk + dot(ds, qh, NN)
                    more = dot(kt, ds, NN)
                    back = more if back is None else back + more
                keys[at] = dk.astype(bf)
                values[at] = dv.astype(bf)
            query[(side, slice(0, L), lanes)] = (back.T * 0.125).astype(bf)
            turn(t)

        loop(4, body)

    def column(k, ref, at):
        def body(side):
            r.bcols[pl.ds(k * 2 + side, 1), :] = jnp.sum(ref[at(side)].astype(f32), axis=0, keepdims=True)

        loop(2, body)

    context_back(7)
    loaded(get_c2, get_lse2)
    statistics(r.lse2, r.c2)
    grads(
        lambda cols: [r.dhb[:, cols]], [(7, side, lambda side=side: [r.c2[side]]) for side in range(2)]
    )
    scatter.ready = 9
    scatter.run(1)
    loaded(get_q2, get_ek, get_ev)
    attend_back(r.q2, r.ek, r.ev, 2, KEYS, False, scatter.turn(4))

    loaded(get_e, get_a2)

    def frame_share(half, j):
        acc = None
        for mat, ref in ((5, r.ek), (6, r.ev)):
            for side in range(2):
                more = dot(ref[side, half], part_rows(mat, side, j), NT)
                acc = more if acc is None else acc + more
        return acc

    def frame_trade(j):
        return remote(r.fsend.at[j], r.frecv.at[j], r.frame_send.at[j], r.frame_recv.at[j], mate)

    def frame_store(j):
        cols = pl.ds(pl.multiple_of(j * COLS, COLS), COLS)
        return pltpu.make_async_copy(r.fout.at[lax.rem(j, 2)], r.frame_out.at[:, cols], r.frame_out_sem.at[j])

    def frame_far(j):
        r.fsend[j] = frame_share(1 - c, j).astype(bf)
        frame_trade(j).start()

    def frame_near(j):
        @pl.when(j >= 2)
        def _():
            frame_store(j - 2).wait()

        frame_trade(j).wait_recv()
        r.fout[lax.rem(j, 2)] = frame_share(c, j) + r.frecv[j].astype(f32)
        frame_store(j).start()

    loop(4, frame_far)
    send_back(1, [(lambda side=side: r.q2[side], 4, side) for side in range(2)])
    loop(4, frame_near)
    scatter.run(1)
    grads(
        lambda cols: [r.e[n, :, cols] for n in range(2)],
        [(5 + i, side, lambda ref=ref, side=side: [ref[side, n] for n in range(2)])
         for i, ref in ((1, r.ev), (0, r.ek)) for side in range(2)],
    )
    scatter.ready = 11
    scatter.run(1)
    column(2, r.q2, lambda side: (side,))

    def value_column(side):
        total = sum(jnp.sum(r.ev[side, n].astype(f32), axis=0, keepdims=True) for n in range(2))
        r.bcols[pl.ds(6 + side, 1), :] = total

    loop(2, value_column)
    grads(lambda cols: [r.a2[:, cols]], [(4, side, lambda side=side: [r.q2[side]]) for side in range(2)])
    scatter.ready = 12
    loaded(get_h1)
    norm_back(1, 2, lambda rows, i: r.h[rows, :], lambda rows, i: r.dh[rows, :], 6)
    scatter.run(1)
    context_back(3)
    loaded(get_c1, get_lse1)
    statistics(r.lse1, r.c1)
    grads(
        lambda cols: [r.dhb[:, cols]], [(3, side, lambda side=side: [r.c1[side]]) for side in range(2)]
    )
    scatter.ready = 13
    scatter.run(1)
    loaded(get_qkv)
    q_ref, k_ref, v_ref = (r.qkv.at[i] for i in range(3))
    attend_back(q_ref, k_ref, v_ref, 1, L, True, lambda t: None)
    send_back(2, [(lambda i=i, side=side: r.qkv[i, side, 0:L, :], i, side) for i in range(3) for side in range(2)])
    loaded(get_a1)
    grads(
        lambda cols: [r.left[:, cols]],
        [(i, side, lambda i=i, side=side: [r.qkv[i, side, 0:L, :]]) for i in (2, 1, 0) for side in range(2)],
    )
    scatter.ready = 16
    scatter.run(1)
    column(0, q_ref, lambda side: (side, slice(0, L)))
    column(1, v_ref, lambda side: (side, slice(0, L)))
    loaded(get_x)
    norm_back(2, 0, lambda rows, i: half_rows(r.x, i), lambda rows, i: r.dh[rows, :], None)
    own_rows = pl.ds(pl.multiple_of(c * HALF, HALF), HALF)
    input_copy = pltpu.make_async_copy(r.dh.at[own_rows], r.input_out, r.out_sem.at[0])
    input_copy.start()

    sums = jnp.concatenate([jnp.sum(r.cols[k * 8 : k * 8 + 8, :], axis=0, keepdims=True) for k in range(9)], axis=0)
    if fast:
        r.small[...] = jnp.zeros(r.small.shape, f32)
        for i in range(2 * levels):
            for xx in range(2):
                k = i * 2 + xx
                r.small[k, 0:9, :] = sums[:, i * 128 : (i + 1) * 128]
                r.small[k, 9:10, :] = r.bcols[k : k + 1, 0:128]
                r.small[k, 10:11, :] = r.bcols[k : k + 1, 128:256]

        def small_copy(k, slot):
            i = lax.rem(me + k + 1, count)
            return remote(r.small.at[i], r.smallgot.at[slot], r.small_send.at[k], r.small_recv.at[slot],
                          peer(i))

        loop(count - 1, lambda k: small_copy(k, me).start())
        r.smallgot[me] = r.small[me]
    else:
        r.smallsum[0:9, :] = sums
    while scatter.steps < MATS + 2:
        scatter.run(min(4, MATS + 2 - scatter.steps))
    owned_copy = pltpu.make_async_copy(r.own, r.owned_out, r.out_sem.at[1])
    owned_copy.start()
    if fast:
        loop(count - 1, lambda k: small_copy(k, lax.rem(me + k + 1, count)).wait_recv())
        total = r.smallgot[0]
        for k in range(1, 4 * levels):
            total = total + r.smallgot[k]
        r.smallsum[...] = total
        loop(count - 1, lambda k: small_copy(k, me).wait_send())
    small_store = pltpu.make_async_copy(r.smallsum, r.small_out, r.out_sem.at[2])
    bcols_store = pltpu.make_async_copy(r.bcols, r.bcols_out, r.out_sem.at[3])
    small_store.start()
    bcols_store.start()
    small_store.wait()
    bcols_store.wait()
    for n in (1, 2):
        loop(4, lambda j: trade(n, j).wait_send())
    loop(4, lambda j: frame_trade(j).wait_send())
    for j in (2, 3):
        frame_store(j).wait()
    scatter.drain()
    input_copy.wait()
    owned_copy.wait()


def backward(kept, shards):
    levels, rows = shards // 2, D // shards
    fast = rows == 128
    f32, bf = jnp.float32, jnp.bfloat16
    sem = pltpu.SemaphoreType.DMA
    hbm = pl.BlockSpec(memory_space=pl.ANY)
    peers = shards * 2
    shapes = [((MATS, rows, COLS), f32), ((HALF, D), f32), ((KEYS, D), f32)]
    shapes += [((16, 128) if fast else (16, D), f32), ((16, COLS), f32)]
    small = (peers, 16, 128) if fast else (1, 16, 128)
    vm = pltpu.VMEM
    scratch = [
        vm((MATS, 2, levels // 2, 2, 2, rows, COLS), bf), vm((MATS, rows, COLS), f32), vm((2, HALF, D), bf),
        vm((8, L, COLS), bf), vm((8, L, COLS), bf), vm((L, D), bf), vm((L, D), f32), vm((16, D), f32),
        vm((2, L, COLS), bf), vm((2, L, COLS), bf), vm((L, 128), f32), vm((2, 2, KEYS, COLS), bf),
        vm((2, 2, KEYS, COLS), bf), vm((2, KEYS, D), bf), vm((L, D), bf),
        vm((2, L, COLS), bf), vm((3, 2, 512, COLS), bf), vm((L, 128), f32), vm((2, HALF, D), bf),
        vm((L, D), f32), vm((L, D), bf), vm((2, L, COLS), bf), vm((16, L), f32),
        vm((KEYS, L), f32), vm((KEYS, L), f32), vm((KEYS, L), bf), vm((KEYS, L), bf),
        vm((2, 4, L, COLS), bf), vm((2, 4, L, COLS), bf), vm((4, KEYS, COLS), bf), vm((4, KEYS, COLS), bf),
        vm((2, KEYS, COLS), f32), vm((72, D), f32), vm((16, COLS), f32), vm(small, f32), vm(small, f32),
        vm((16, 128) if fast else (16, D), f32),
        sem((24,)), sem((3, 4)), sem((3, 4)), sem((4,)), sem((4,)), sem((4,)), sem((peers,)), sem((peers,)), sem((4,)),
    ]
    return pl.pallas_call(
        partial(backward_kernel, levels, fast),
        out_shape=[jax.ShapeDtypeStruct(s, t) for s, t in shapes],
        in_specs=[hbm] * len(BackwardIn._fields),
        out_specs=[hbm] * len(shapes),
        scratch_shapes=scratch + Scatter.buffers(levels, rows) + Scatter.semaphores(levels),
        compiler_params=pltpu.CompilerParams(
            collective_id=1, has_side_effects=True, vmem_limit_bytes=63 * 2**20
        ),
        name="backward",
    )(
        kept.dy, kept.wide.reshape(MATS, 2, levels // 2, 2, 2, rows, COLS), kept.slope, kept.z, kept.a3, kept.h2, kept.norm, kept.c2, kept.q2, kept.lse2,
        kept.ek, kept.ev, kept.e, kept.a2, kept.h1, kept.c1, kept.qkv, kept.lse1, kept.a1, kept.x,
    )


def small_kernel(shards, every, scatter, src, out, own_sem, send_sem, recv_sem):
    dp, x, c = (lax.axis_index(a) for a in AXES)
    cores = 2 if every else 1
    count = shards * 2 * cores
    me = (dp * 2 + x) * cores + (c if every else 0)

    def peer(i):
        if every:
            return (i // 4, lax.rem(i // 2, 2), lax.rem(i, 2))
        return (i // 2, lax.rem(i, 2), c)

    bar = pltpu.get_barrier_semaphore()

    def greet(k, carry):
        pl.semaphore_signal(bar, inc=1, device_id=peer(lax.rem(me + k, count)), device_id_type=DT)
        return carry

    lax.fori_loop(1, count, greet, 0)
    pl.semaphore_wait(bar, count - 1)

    def copy(k):
        i = lax.rem(me + k, count)
        return pltpu.make_async_remote_copy(
            src.at[i] if scatter else src, out.at[me], send_sem.at[k], recv_sem.at[me],
            device_id=peer(i), device_id_type=DT,
        )

    def send(k, carry):
        copy(k).start()
        return carry

    own = pltpu.make_async_copy(src.at[me] if scatter else src, out.at[me], own_sem)
    own.start()
    lax.fori_loop(1, count, send, 0)
    own.wait()

    def finish(k, carry):
        i = lax.rem(me + k, count)
        pltpu.make_async_remote_copy(
            src.at[i] if scatter else src, out.at[i], send_sem.at[k], recv_sem.at[i],
            device_id=peer(i), device_id_type=DT,
        ).wait_recv()
        copy(k).wait_send()
        return carry

    lax.fori_loop(1, count, finish, 0)


def small_exchange(src, shards, every, scatter, call_id):
    count = shards * 2 * (2 if every else 1)
    shape = src.shape[1:] if scatter else src.shape
    sem = pltpu.SemaphoreType.DMA
    vm = pl.BlockSpec(memory_space=pltpu.VMEM)
    return pl.pallas_call(
        partial(small_kernel, shards, every, scatter),
        out_shape=jax.ShapeDtypeStruct((count, *shape), src.dtype),
        in_specs=[vm],
        out_specs=vm,
        scratch_shapes=[sem, sem((count,)), sem((count,))],
        compiler_params=pltpu.CompilerParams(collective_id=call_id, has_side_effects=True),
        name=f"small_exchange_{call_id}",
    )(src)


def adapt(weight, gradient, moment, second, token_total):
    scaled_grad = gradient / token_total
    new_moment = 0.5 * moment + 0.5 * scaled_grad
    new_second = 0.5 * second + 0.5 * scaled_grad * scaled_grad
    direction = new_moment / (jnp.sqrt(new_second) + 1e-06) + 0.01 * weight
    return (new_moment, new_second, direction)


def shards_fn(
    tokens, frames, cotangent, attention_weights, dense_weights, unit_bias, norm_bias,
    attention_mean, dense_mean, unit_mean, norm_mean,
    attention_square, dense_square, unit_square, norm_square,
):
    f32, bf = jnp.float32, jnp.bfloat16
    shards = lax.axis_size("dp")
    rows = D // shards
    c = lax.axis_index("core")
    unit_cols = unit_bias.shape[1]
    column_rows = (lax.axis_index("dp") * unit_cols + jnp.arange(unit_cols, dtype=jnp.int32)) // HD
    row_pick = (column_rows[:, None] == jnp.arange(8, dtype=jnp.int32)[None, :]).astype(f32)
    leader = ((lax.axis_index("side") == 0) & (c == 0)).astype(f32)

    def square_rows(attn_part, dense_part, unit_part, norm_part):
        unit_sums = jnp.sum(jnp.sum(unit_part * unit_part, axis=0)[:, None] * row_pick, axis=0)
        return jnp.concatenate(
            [
                jnp.sum(attn_part * attn_part, axis=(2, 3)).reshape(8),
                jnp.sum(dense_part * dense_part, axis=(1, 2, 3)),
                unit_sums,
                jnp.sum(norm_part * norm_part, axis=1) * leader,
            ]
        )

    own_attn = attention_weights.astype(f32)
    own_dense = dense_weights.astype(f32)
    own_unit = unit_bias.astype(f32)
    own_norm = norm_bias.astype(f32)

    if rows == 128:
        pack = jnp.concatenate([norm_bias.astype(f32), unit_bias.astype(f32).reshape(2, 128)])
        small = (jnp.pad(pack, ((0, 5), (0, 0))), jnp.zeros((8, 128), f32), jnp.zeros((8, 128), f32))
    else:
        pack = jnp.concatenate([norm_bias.reshape(-1), unit_bias.reshape(-1)])
        pack = jnp.pad(pack, (0, 2048 - pack.shape[0])).reshape(16, 128)
        packs = small_exchange(pack, shards, False, False, 2).reshape(shards, 2, 2048)
        norm_rows = packs[:, 0, : 9 * rows].reshape(shards, 9, rows).transpose(1, 0, 2).reshape(9, D).astype(f32)
        unit_all = packs[:, :, 9 * rows : 9 * rows + 4 * unit_cols].reshape(shards, 2, 4, unit_cols)
        bias_rows = (
            unit_all.transpose(1, 2, 0, 3).reshape(2, 4, 8, HD).transpose(2, 0, 1, 3).reshape(16, COLS).astype(f32)
        )
        small = (jnp.zeros((16, 128), f32), jnp.pad(norm_rows, ((0, 7), (0, 0))), bias_rows)

    shard = jnp.concatenate(
        [attention_weights.reshape(8, rows, COLS), dense_weights.transpose(0, 2, 1, 3).reshape(8, rows, COLS)]
    )
    kept = forward(shard, tokens, jnp.pad(frames, ((0, KEYS - HALF_FRAMES), (0, 0))), cotangent, small, shards)
    layer_out = kept.layer_out
    owned, input_gradient, frame_gradient, *small_grads = backward(kept, shards)
    frame_gradient = frame_gradient[:HALF_FRAMES]
    attention_owned = owned[:8].reshape(2, 4, rows, COLS)
    dense_owned = owned[8:].reshape(2, 4, rows, COLS).transpose(0, 2, 1, 3)

    if rows == 128:
        norm_owned = small_grads[0][:9]
        unit_owned = small_grads[0][9:11].reshape(4, unit_cols)
    else:
        norm_parts = small_grads[0][:9].reshape(9, shards, rows).transpose(1, 0, 2).reshape(shards, 1, 9 * rows)
        unit_parts = small_grads[1].reshape(8, 2, 4, HD).transpose(1, 2, 0, 3).reshape(2, 4, shards, unit_cols)
        unit_parts = unit_parts.transpose(2, 0, 1, 3).reshape(shards, 2, 4 * unit_cols)
        small = jnp.concatenate([jnp.broadcast_to(norm_parts, (shards, 2, 9 * rows)), unit_parts], axis=2)
        small = jnp.pad(small, ((0, 0), (0, 0), (0, 2048 - small.shape[2]))).reshape(shards * 2, 16, 128)
        small = jnp.sum(small_exchange(small, shards, False, True, 13), axis=0).reshape(2048)
        norm_owned = small[: 9 * rows].reshape(9, rows)
        unit_owned = small[9 * rows : 9 * rows + 4 * unit_cols].reshape(4, unit_cols)

    token_total = float(tokens.shape[0] * shards * 4)
    attn_moment, attn_second, attn_dir = adapt(
        own_attn, attention_owned, attention_mean, attention_square, token_total
    )
    dense_moment, dense_second, dense_dir = adapt(
        own_dense, dense_owned, dense_mean, dense_square, token_total
    )
    unit_moment, unit_second, unit_dir = adapt(
        own_unit, unit_owned, unit_mean, unit_square, token_total
    )
    norm_moment, norm_second, norm_dir = adapt(
        own_norm, norm_owned, norm_mean, norm_square, token_total
    )
    sums = jnp.concatenate(
        [
            square_rows(own_attn, own_dense, own_unit, own_norm),
            square_rows(attn_dir, dense_dir, unit_dir, norm_dir),
        ]
    )
    sums = jnp.pad(sums, (0, 1024 - 54)).reshape(8, 128)
    sums = jnp.sum(small_exchange(sums, shards, True, False, 14), axis=0).reshape(1024)
    weight_norms = jnp.sqrt(sums[:27])
    step_norms = jnp.sqrt(sums[27:54])
    trust = weight_norms / step_norms
    attention_step = -learning_rate * trust[0:8].reshape(2, 4, 1, 1) * attn_dir
    dense_step = -learning_rate * trust[8:10].reshape(2, 1, 1, 1) * dense_dir
    unit_factor = jnp.sum(row_pick * trust[10:18][None, :], axis=1)
    unit_step = -learning_rate * unit_factor[None, :] * unit_dir
    norm_step = -learning_rate * trust[18:27][:, None] * norm_dir
    return (
        layer_out, input_gradient, frame_gradient,
        attention_owned, dense_owned, unit_owned, norm_owned,
        attn_moment, dense_moment, unit_moment, norm_moment,
        attn_second, dense_second, unit_second, norm_second,
        attention_step, dense_step, unit_step, norm_step,
        weight_norms, step_norms,
    )


def solution(mesh):
    shards = mesh.shape["dp"]
    inner = Mesh(mesh.devices.reshape(shards, 2, 2), AXES)
    tensor = ("side", "core")
    rows = P(("dp", *tensor), None)
    state = (P(None, None, "dp", tensor), P(None, "dp", None, tensor), P(tensor, "dp"), P(None, "dp"))
    return jax.shard_map(
        shards_fn,
        mesh=inner,
        in_specs=(rows, rows, rows) + state * 3,
        out_specs=(rows, rows, rows) + state * 4 + (P(), P()),
        check_vma=False,
    )
```

time: 436 us -> 383 us (0.88); the launches traced: 436 us -> 376 us
  Pallas kernels: 406 us -> 345 us
    pallas_call x1, Pallas kernels: 221 us -> 169 us  [forward(): pl.pallas_call(partial(forward_kernel, levels, groups, fast), out_shape=[...]
    pallas_call x1, Pallas kernels: 173 us -> 166 us  [backward(): pl.pallas_call(partial(backward_kernel, levels, fast), out_shape=[jax.Sha...]
where the time goes in v4:
time: 383 us; the launch traced here: 376 us
  Pallas kernels  345 us (90%)
  other arithmetic  17.1 us (4%)
  local copies, waits for them, and re-layouts  12.1 us (3%)
    pallas_call x1, Pallas kernels, forward(): pl.pallas_call(partial(forward_kernel, levels, groups, fast), out_shape=[...  169 us
    pallas_call x1, Pallas kernels, backward(): pl.pallas_call(partial(backward_kernel, levels, fast), out_shape=[jax.Sha...  166 us
    pallas_call x1, Pallas kernels, small_exchange(): pl.pallas_call(partial(small_kernel, shards, every, scatter), out_shape=j...  10.1 us

profile of v4, /device:TPU:0, one launch (start us, length us, event | category | flops | bytes accessed | tf_op | source)
XLA Modules:
  0.0 375.6 jit_solution(14755906134887117696)
XLA Ops:
  0.7 0.0 copy-start.3
  0.7 1.2 copy.38
  1.9 2.1 pad_maximum_fusion.refs_0_
  4.0 0.0 copy-done.3
  4.0 1.3 pad.12.refs_2_
  5.3 0.0 copy-done.13
  5.3 0.1 reshape.118
  5.4 0.0 copy-done.8
  5.4 0.6 select_maximum_fusion.refs_4_
  6.0 0.6 broadcast_15_refs_5__refs_6_.2.refs_5_.refs_6_
  6.6 169.4 %forward.1 = (bf16[224,1024]{1,0:T(8,128)(2,1)}, f32[16,1024]{1,0:T(8,128)}, bf16[448,1024]{1,0:T(8,128)(2,1)}, bf16[2,224,1024]{2,1,0:T(8,128)(2,1)}, bf16[3,2,...) custom-call(bf16[16,128,256]{2,1,0:T(8,128)(2,1)} %pad_maximum_fusio, ...), custom_call_target="tpu_custom_call" | custom-call | tf_op jit(solution)/shard_map/forward/pallas_call | solution.py:746
  176.0 165.7 %backward.1 = (f32[16,128,256]{2,1,0:T(8,128)}, f32[224,1024]{1,0:T(8,128)}, f32[768,1024]{1,0:T(8,128)}, f32[16,128]{1,0:T(8,128)}, f32[16,256]{1,0:T(8,128)}) custom-call(bf16[2,224,1024]{2,1,0:T(8,128)(2,1)} %get-tuple-element.47.refs_0_, bf16[16,2,2,2,2,128,256]{6,5,4,3,2,1,0:T(8,128)(2,1)} %bitcast.12, bf16[8,448,256]{2,1,0:T(8,128)(2,1)} %get-tuple-element.49.refs_2_, ...), custom_call_target="tpu_custom_call" | custom-call | tf_op jit(solution)/shard_map/backward/pallas_call | solution.py:1388
  341.8 0.0 copy-start.2
  341.8 4.1 %slice.33 = f32[750,1024]{1,0:T(8,128)} slice(f32[768,1024]{1,0:T(8,128)} %get-tuple-element.68), slice={[0:750], [0:1024]} | slice | bytes 6144000 | tf_op jit(solution)/shard_map/slice | solution.py:1526
  345.9 0.0 copy-done.2
  345.9 0.2 fusion.7
  346.1 0.0 copy-start
  346.1 0.8 copy-done.1
  346.9 0.7 copy-done.4
  347.6 0.3 copy-done.5
  347.9 3.7 multiply_reduce_fusion
  351.6 0.1 reshape.122
  351.7 0.7 multiply_reduce_fusion.2
  352.5 0.0 copy-start.14
  352.5 0.0 copy-start.15
  352.5 3.8 %multiply_reduce_fusion.1 = (f32[2,4]{1,0:T(2,128)S(1)}, f32[2,4,128,256]{3,2,1,0:T(8,128)S(1)}, f32[2,4,128,256]{3,2,1,0:T(8,128)}, f32[2,4,128,256]{3,2,1,0:T(8,128)}, f32[2,4]{1,0:T(2,128)S(1)}) fusion(bf16[2,4,128,256]{3,2,1,0:T(8,128)(2,1)} %param.18, f32[2,4,128,256]{3,2,1,0:T(8,128)S(1)} %bitcast.13, f32[2,4,128,256]{3,2,1,0:T(8,128)} %param.26, ...), kind=kLoop, calls=%fused_computation.11 | loop fusion | flops 4194288 | bytes 6815808 | tf_op jit(solution)/shard_map/reduce_sum | solution.py:1494
  356.3 0.0 copy-done.12
  356.3 0.6 multiply_reduce_fusion.4
  356.9 0.1 reshape.123
  357.0 0.1 select_reduce_fusion.1
  357.2 0.1 reshape.124
  357.2 0.1 concatenate.11
  357.3 0.6 pad_bitcast_fusion.src
  357.9 10.1 %small_exchange_14.1 = f32[32,8,128]{2,1,0:T(8,128)} custom-call(f32[8,128]{1,0:T(8,128)} %pad_bitcast_fusion.src), custom_call_target="tpu_custom_call" | custom-call | tf_op jit(solution)/shard_map/small_exchange_14/pallas_call | solution.py:1457
  368.0 0.9 reduce_sum.118
  369.0 0.6 fusion.4
  369.6 0.1 fusion.8
  369.6 0.1 mul.252
  369.7 1.1 broadcast_multiply_fusion.1
  370.9 0.1 slice_multiply_fusion.1
  370.9 1.2 broadcast_multiply_fusion
  372.1 0.1 select_reduce_fusion
  372.2 0.6 broadcast_multiply_fusion.3
  372.8 0.1 slice_multiply_fusion
  372.9 0.7 broadcast_multiply_fusion.2
  373.6 0.0 copy-done.7
  373.6 0.8 copy.44
  374.3 0.9 copy.45
  (23 shorter events, 0.1 us)
Async XLA Ops:
  0.7 3.4 copy-start.3
  4.0 1.3 copy-start.13
  4.0 1.4 copy-start.8
  341.8 4.1 %copy-start.2 = (f32[16,128,256]{2,1,0:T(8,128)S(1)}, f32[16,128,256]{2,1,0:T(8,128)}, u32[]{:S(2)}) copy-start(f32[16,128,256]{2,1,0:T(8,128)} %get-tuple-element.69) | copy-start | bytes 6291460
  345.9 1.0 copy-start.1
  345.9 1.8 copy-start.4
  345.9 2.1 copy-start.5
  346.1 6.4 %copy-start = (f32[8,128,256]{2,1,0:T(8,128)}, f32[8,128,256]{2,1,0:T(8,128)S(1)}, u32[]{:S(2)}) copy-start(f32[8,128,256]{2,1,0:T(8,128)S(1)} %get-tuple-element.95) | copy-start | bytes 3145732
  347.9 3.7 copy-start.9
  347.9 3.8 %copy-start.10 = (f32[9,128]{1,0:T(8,128)S(1)}, f32[9,128]{1,0:T(8,128)}, u32[]{:S(2)}) copy-start(f32[9,128]{1,0:T(8,128)} %param.29) | copy-start | bytes 13828
  347.9 3.8 %copy-start.11 = (f32[9,128]{1,0:T(8,128)S(1)}, f32[9,128]{1,0:T(8,128)}, u32[]{:S(2)}) copy-start(f32[9,128]{1,0:T(8,128)} %param.25) | copy-start | bytes 13828
  351.7 4.6 %copy-start.12 = (f32[4,64]{1,0:T(4,128)}, f32[4,64]{1,0:T(4,128)S(1)}, u32[]{:S(2)}) copy-start(f32[4,64]{1,0:T(4,128)S(1)} %reshape.122) | copy-start | bytes 3076
  352.5 3.8 %copy-start.14 = (f32[4,64]{1,0:T(4,128)S(1)}, f32[4,64]{1,0:T(4,128)}, u32[]{:S(2)}) copy-start(f32[4,64]{1,0:T(4,128)} %param.28) | copy-start | bytes 3076
  352.5 3.8 %copy-start.15 = (f32[4,64]{1,0:T(4,128)S(1)}, f32[4,64]{1,0:T(4,128)}, u32[]{:S(2)}) copy-start(f32[4,64]{1,0:T(4,128)} %param.24) | copy-start | bytes 3076
  369.7 3.9 %copy-start.7 = (bf16[224,1024]{1,0:T(8,128)(2,1)S(1)}, bf16[224,1024]{1,0:T(8,128)(2,1)}, u32[]{:S(2)}) copy-start(bf16[224,1024]{1,0:T(8,128)(2,1)} %get-tuple-element.125) | copy-start | bytes 1376260
  370.9 3.5 copy-start.6

commit v5 on v4

--- a/solution.py
+++ b/solution.py
@@ -930,14 +930,52 @@
     lse1: object
     a1: object
     x: object
-
-
-class BackwardRefs(NamedTuple):
-    owned_out: object
+    mean_attn: object
+    mean_dense: object
+    square_attn: object
+    square_dense: object
+    shard: object
+    pack: object
+    pack_mean: object
+    pack_square: object
+
+
+class BackwardOut(NamedTuple):
+    owned_attn: object
+    owned_dense: object
     input_out: object
     frame_out: object
     small_out: object
     bcols_out: object
+    mean_attn: object
+    mean_dense: object
+    square_attn: object
+    square_dense: object
+    step_attn: object
+    step_dense: object
+    small_mean: object
+    small_square: object
+    small_step: object
+    norms: object
+
+
+class BackwardRefs(NamedTuple):
+    owned_attn: object
+    owned_dense: object
+    input_out: object
+    frame_out: object
+    small_out: object
+    bcols_out: object
+    mean_attn: object
+    mean_dense: object
+    square_attn: object
+    square_dense: object
+    step_attn: object
+    step_dense: object
+    small_mean: object
+    small_square: object
+    small_step: object
+    norms: object
     part: object
     own: object
     dy: object
@@ -984,9 +1022,21 @@
     small_send: object
     small_recv: object
     out_sem: object
-
-
-def backward_kernel(levels, fast, *refs):
+    moments: object
+    held: object
+    squares: object
+    sums: object
+    sumsgot: object
+    sumspair: object
+    load_sem: object
+    store_sem: object
+    step_sem: object
+    pair_sem: object
+    sums_send: object
+    sums_recv: object
+
+
+def backward_kernel(levels, fast, token_total, *refs):
     f32, bf = jnp.float32, jnp.bfloat16
     at, width = len(BackwardIn._fields), len(BackwardRefs._fields)
     given = BackwardIn(*refs[:at])
@@ -1262,7 +1312,7 @@
             frame_store(j - 2).wait()
 
         frame_trade(j).wait_recv()
-        r.fout[lax.rem(j, 2)] = frame_share(c, j) + r.frecv[j].astype(f32)
+        r.fout[lax.rem(j, 2)] = (frame_share(c, j) + r.frecv[j].astype(f32))[0:HALF_FRAMES]
         frame_store(j).start()
 
     loop(4, frame_far)
@@ -1334,17 +1384,160 @@
         r.smallgot[me] = r.small[me]
     else:
         r.smallsum[0:9, :] = sums
-    while scatter.steps < MATS + 2:
-        scatter.run(min(4, MATS + 2 - scatter.steps))
-    owned_copy = pltpu.make_async_copy(r.own, r.owned_out, r.out_sem.at[1])
-    owned_copy.start()
+
+    def either(m, attn, dense, action):
+        @pl.when(m < 8)
+        def _():
+            action(attn())
+
+        @pl.when(m >= 8)
+        def _():
+            action(dense())
+
+    def moment_loads(g, action):
+        m, slot = MATS - 1 - g, lax.rem(g, 2)
+        for k, (attn, dense) in enumerate(
+            ((given.mean_attn, given.mean_dense), (given.square_attn, given.square_dense))
+        ):
+            def copy(src, at):
+                return pltpu.make_async_copy(src.at[at], r.moments.at[slot, k], r.load_sem.at[slot, k])
+
+            either(m, lambda: copy(attn, m), lambda: copy(dense, m - 8), action)
+        action(pltpu.make_async_copy(given.shard.at[m], r.held.at[slot], r.load_sem.at[slot, 2]))
+
+    def moment_stores(g, action):
+        m, slot = MATS - 1 - g, lax.rem(g, 2)
+        for k, (attn, dense) in enumerate(((r.mean_attn, r.mean_dense), (r.square_attn, r.square_dense))):
+            def copy(dst, at):
+                return pltpu.make_async_copy(r.moments.at[slot, k], dst.at[at], r.store_sem.at[slot, k])
+
+            either(m, lambda: copy(attn, m), lambda: copy(dense, m - 8), action)
+
+    def begin(copy):
+        copy.start()
+
+    def end(copy):
+        copy.wait()
+
+    def whole_store(m, attn, dense, action):
+        def copy(dst, at):
+            return pltpu.make_async_copy(r.own.at[m], dst.at[at], r.step_sem.at[m])
+
+        either(m, lambda: copy(attn, m), lambda: copy(dense, m - 8), action)
+
+    def adapted(gradient, moment, second, weight):
+        scaled = gradient / token_total
+        moment = 0.5 * moment + 0.5 * scaled
+        second = 0.5 * second + 0.5 * scaled * scaled
+        return moment, second, moment / (jnp.sqrt(second) + 1e-06) + 0.01 * weight
+
+    def update(g):
+        m, slot = MATS - 1 - g, lax.rem(g, 2)
+        whole_store(m, r.owned_attn, r.owned_dense, begin)
+        moment_loads(g, end)
+
+        @pl.when(g >= 1)
+        def _():
+            moment_stores(g - 1, end)
+
+        @pl.when(g + 1 < MATS)
+        def _():
+            moment_loads(g + 1, begin)
+
+        whole_store(m, r.owned_attn, r.owned_dense, end)
+        r.squares[pl.ds(m, 1), :] = jnp.zeros((1, COLS), f32)
+        r.squares[pl.ds(MATS + m, 1), :] = jnp.zeros((1, COLS), f32)
+
+        def block(rows, i):
+            weight = r.held[slot, rows, :].astype(f32)
+            moment, second, direction = adapted(
+                r.own[m, rows, :], r.moments[slot, 0, rows, :], r.moments[slot, 1, rows, :], weight
+            )
+            r.moments[slot, 0, rows, :] = moment
+            r.moments[slot, 1, rows, :] = second
+            r.own[m, rows, :] = direction
+            r.squares[pl.ds(m, 1), :] += jnp.sum(direction * direction, axis=0, keepdims=True)
+            r.squares[pl.ds(MATS + m, 1), :] += jnp.sum(weight * weight, axis=0, keepdims=True)
+
+        rows_loop(rows_of, block, 2)
+        moment_stores(g, begin)
+
+    if fast:
+        moment_loads(0, begin)
+        updated = scatter.steps - 2
+        loop(updated, update)
+        left = MATS + 2 - scatter.steps
+        final = scatter.turn(left)
+
+        def last_turn(i):
+            final(i)
+            update(updated + i)
+
+        loop(left, last_turn)
+    else:
+        scatter.run(MATS + 2 - scatter.steps)
+        for k, dst in enumerate((r.owned_attn, r.owned_dense)):
+            copy = pltpu.make_async_copy(r.own.at[8 * k : 8 * k + 8], dst, r.step_sem.at[k])
+            copy.start()
+            copy.wait()
     if fast:
         loop(count - 1, lambda k: small_copy(k, lax.rem(me + k + 1, count)).wait_recv())
         total = r.smallgot[0]
         for k in range(1, 4 * levels):
             total = total + r.smallgot[k]
         r.smallsum[...] = total
+        moment, second, direction = adapted(total, given.pack_mean[...], given.pack_square[...], given.pack[...])
+        r.small_mean[...] = moment
+        r.small_square[...] = second
+        lanes = lax.broadcasted_iota(jnp.int32, (1, 128), 1)
+        wide_lane = lax.broadcasted_iota(jnp.int32, (16, 128), 1)
+        row = lax.broadcasted_iota(jnp.int32, (16, 128), 0)
+        place_of = jnp.where(row < 9, 18 + row, jnp.where(row < 11, 10 + dp, 127))
+        counted = jnp.where(row < 9, jnp.where((x == 0) & (c == 0), 1.0, 0.0), 1.0)
+
+        def spread(first_row, small):
+            line = jnp.zeros((1, 128), f32)
+            for m in range(MATS):
+                k = first_row + m
+                one = jnp.sum(r.squares[k : k + 1, :], axis=1, keepdims=True)
+                line = line + jnp.where(lanes == (m if m < 8 else 8 + (m - 8) // 4), one, 0.0)
+            per_row = jnp.sum(small * small * counted, axis=1, keepdims=True)
+            return line + jnp.sum(jnp.where(wide_lane == place_of, per_row, 0.0), axis=0, keepdims=True)
+
+        r.sums[0, 0:1, :] = spread(MATS, given.pack[...])
+        r.sums[0, 1:2, :] = spread(0, direction)
+        pair = remote(r.sums.at[0], r.sumspair, r.pair_sem.at[0], r.pair_sem.at[1], mate)
+        pair.start()
+        pair.wait_recv()
+        r.sums[1] = r.sums[0] + r.sumspair[...]
+
+        def sums_copy(k, slot):
+            return remote(r.sums.at[1], r.sumsgot.at[slot], r.sums_send.at[k], r.sums_recv.at[slot],
+                          peer(lax.rem(me + k + 1, count)))
+
+        loop(count - 1, lambda k: sums_copy(k, me).start())
+        r.sumsgot[me] = r.sums[1]
+        loop(count - 1, lambda k: sums_copy(k, lax.rem(me + k + 1, count)).wait_recv())
+        all_sums = r.sumsgot[0]
+        for k in range(1, 4 * levels):
+            all_sums = all_sums + r.sumsgot[k]
+        norms = jnp.sqrt(all_sums)
+        r.norms[...] = norms
+        trust = norms[0:1] / norms[1:2]
+
+        def scale(m):
+            at = jnp.where(m < 8, m, 8 + (m - 8) // 4)
+            factor = -learning_rate * jnp.sum(jnp.where(lanes == at, trust, 0.0), axis=1, keepdims=True)
+            r.own[m] = r.own[m] * factor
+            whole_store(m, r.step_attn, r.step_dense, begin)
+
+        loop(MATS, scale)
+        small_factor = jnp.sum(jnp.where(wide_lane == place_of, trust, 0.0), axis=1, keepdims=True)
+        r.small_step[...] = jnp.where(row < 11, -learning_rate * small_factor * direction, 0.0)
+        pair.wait_send()
         loop(count - 1, lambda k: small_copy(k, me).wait_send())
+        loop(count - 1, lambda k: sums_copy(k, me).wait_send())
+        moment_stores(MATS - 1, end)
     small_store = pltpu.make_async_copy(r.smallsum, r.small_out, r.out_sem.at[2])
     bcols_store = pltpu.make_async_copy(r.bcols, r.bcols_out, r.out_sem.at[3])
     small_store.start()
@@ -1358,20 +1551,24 @@
         frame_store(j).wait()
     scatter.drain()
     input_copy.wait()
-    owned_copy.wait()
-
-
-def backward(kept, shards):
+    if fast:
+        loop(MATS, lambda m: whole_store(m, r.step_attn, r.step_dense, end))
+
+
+def backward(kept, state, token_total, shards):
     levels, rows = shards // 2, D // shards
     fast = rows == 128
     f32, bf = jnp.float32, jnp.bfloat16
     sem = pltpu.SemaphoreType.DMA
     hbm = pl.BlockSpec(memory_space=pl.ANY)
     peers = shards * 2
-    shapes = [((MATS, rows, COLS), f32), ((HALF, D), f32), ((KEYS, D), f32)]
+    half = ((8, rows, COLS), f32)
+    shapes = [half, half, ((HALF, D), f32), ((HALF_FRAMES, D), f32)]
     shapes += [((16, 128) if fast else (16, D), f32), ((16, COLS), f32)]
+    shapes += [half] * 6 + [((16, 128), f32)] * 3 + [((8, 128), f32)]
     small = (peers, 16, 128) if fast else (1, 16, 128)
     vm = pltpu.VMEM
+    inside = pl.BlockSpec(memory_space=pltpu.VMEM)
     scratch = [
         vm((MATS, 2, levels // 2, 2, 2, rows, COLS), bf), vm((MATS, rows, COLS), f32), vm((2, HALF, D), bf),
         vm((8, L, COLS), bf), vm((8, L, COLS), bf), vm((L, D), bf), vm((L, D), f32), vm((16, D), f32),
@@ -1381,15 +1578,18 @@
         vm((L, D), f32), vm((L, D), bf), vm((2, L, COLS), bf), vm((16, L), f32),
         vm((KEYS, L), f32), vm((KEYS, L), f32), vm((KEYS, L), bf), vm((KEYS, L), bf),
         vm((2, 4, L, COLS), bf), vm((2, 4, L, COLS), bf), vm((4, KEYS, COLS), bf), vm((4, KEYS, COLS), bf),
-        vm((2, KEYS, COLS), f32), vm((72, D), f32), vm((16, COLS), f32), vm(small, f32), vm(small, f32),
+        vm((2, HALF_FRAMES, COLS), f32), vm((72, D), f32), vm((16, COLS), f32), vm(small, f32), vm(small, f32),
         vm((16, 128) if fast else (16, D), f32),
         sem((24,)), sem((3, 4)), sem((3, 4)), sem((4,)), sem((4,)), sem((4,)), sem((peers,)), sem((peers,)), sem((4,)),
+        vm((2, 2, rows, COLS), f32), vm((2, rows, COLS), bf), vm((2 * MATS, COLS), f32), vm((2, 8, 128), f32),
+        vm((peers if fast else 1, 8, 128), f32), vm((8, 128), f32), sem((2, 3)), sem((2, 2)), sem((MATS,)), sem((2,)),
+        sem((peers,)), sem((peers,)),
     ]
     return pl.pallas_call(
-        partial(backward_kernel, levels, fast),
+        partial(backward_kernel, levels, fast, token_total),
         out_shape=[jax.ShapeDtypeStruct(s, t) for s, t in shapes],
-        in_specs=[hbm] * len(BackwardIn._fields),
-        out_specs=[hbm] * len(shapes),
+        in_specs=[hbm] * (len(BackwardIn._fields) - 3) + [inside] * 3,
+        out_specs=[hbm] * (len(shapes) - 4) + [inside] * 4,
         scratch_shapes=scratch + Scatter.buffers(levels, rows) + Scatter.semaphores(levels),
         compiler_params=pltpu.CompilerParams(
             collective_id=1, has_side_effects=True, vmem_limit_bytes=63 * 2**20
@@ -1397,7 +1597,7 @@
         name="backward",
     )(
         kept.dy, kept.wide.reshape(MATS, 2, levels // 2, 2, 2, rows, COLS), kept.slope, kept.z, kept.a3, kept.h2, kept.norm, kept.c2, kept.q2, kept.lse2,
-        kept.ek, kept.ev, kept.e, kept.a2, kept.h1, kept.c1, kept.qkv, kept.lse1, kept.a1, kept.x,
+        kept.ek, kept.ev, kept.e, kept.a2, kept.h1, kept.c1, kept.qkv, kept.lse1, kept.a1, kept.x, *state,
     )
 
 
@@ -1522,14 +1722,39 @@
     )
     kept = forward(shard, tokens, jnp.pad(frames, ((0, KEYS - HALF_FRAMES), (0, 0))), cotangent, small, shards)
     layer_out = kept.layer_out
-    owned, input_gradient, frame_gradient, *small_grads = backward(kept, shards)
-    frame_gradient = frame_gradient[:HALF_FRAMES]
-    attention_owned = owned[:8].reshape(2, 4, rows, COLS)
-    dense_owned = owned[8:].reshape(2, 4, rows, COLS).transpose(0, 2, 1, 3)
+    def by_matrix(attn, dense):
+        return attn.reshape(8, rows, COLS), dense.transpose(0, 2, 1, 3).reshape(8, rows, COLS)
+
+    def from_matrix(attn, dense):
+        return attn.reshape(2, 4, rows, COLS), dense.reshape(2, 4, rows, COLS).transpose(0, 2, 1, 3)
+
+    def small_pack(norm, unit):
+        if rows != 128:
+            return jnp.zeros((16, 128), f32)
+        return jnp.pad(jnp.concatenate([norm, unit.reshape(2, 128)]), ((0, 5), (0, 0)))
+
+    def from_pack(pack):
+        return pack[9:11].reshape(4, unit_cols), pack[:9]
+
+    token_total = float(tokens.shape[0] * shards * 4)
+    state = (
+        *by_matrix(attention_mean, dense_mean), *by_matrix(attention_square, dense_square), shard, small[0],
+        small_pack(norm_mean, unit_mean), small_pack(norm_square, unit_square),
+    )
+    done = BackwardOut(*backward(kept, state, token_total, shards))
+    input_gradient, frame_gradient = done.input_out, done.frame_out
+    attention_owned, dense_owned = from_matrix(done.owned_attn, done.owned_dense)
+    small_grads = (done.small_out, done.bcols_out)
 
     if rows == 128:
-        norm_owned = small_grads[0][:9]
-        unit_owned = small_grads[0][9:11].reshape(4, unit_cols)
+        unit_owned, norm_owned = from_pack(done.small_out)
+        means = (*from_matrix(done.mean_attn, done.mean_dense), *from_pack(done.small_mean))
+        seconds = (*from_matrix(done.square_attn, done.square_dense), *from_pack(done.small_square))
+        steps = (*from_matrix(done.step_attn, done.step_dense), *from_pack(done.small_step))
+        return (
+            layer_out, input_gradient, frame_gradient, attention_owned, dense_owned, unit_owned, norm_owned,
+            *means, *seconds, *steps, done.norms[0, :27], done.norms[1, :27],
+        )
     else:
         norm_parts = small_grads[0][:9].reshape(9, shards, rows).transpose(1, 0, 2).reshape(shards, 1, 9 * rows)
         unit_parts = small_grads[1].reshape(8, 2, 4, HD).transpose(1, 2, 0, 3).reshape(2, 4, shards, unit_cols)
@@ -1540,7 +1765,6 @@
         norm_owned = small[: 9 * rows].reshape(9, rows)
         unit_owned = small[9 * rows : 9 * rows + 4 * unit_cols].reshape(4, unit_cols)
 
-    token_total = float(tokens.shape[0] * shards * 4)
     attn_moment, attn_second, attn_dir = adapt(
         own_attn, attention_owned, attention_mean, attention_square, token_total
     )

time: 383 us -> 384 us (level); the launches traced: 376 us -> 383 us
  local copies, waits for them, and re-layouts: 12.1 us -> 32.3 us
  other arithmetic: 17.1 us -> 4.81 us
    reshape x4 -> x10, local copies, waits for them, and re-layouts: 0.85 us -> 12.1 us  [the longest x4 7.9 us: from_matrix(): dense.reshape(2, 4, rows, COLS).transpose(0, 2, 1, 3)]
    reduce_sum x7 -> x0, other arithmetic: 9.98 us -> none  [the longest x1 3.82 us: square_rows(): jnp.sum(attn_part * attn_part, axis=(2, 3)).reshape(8)]
    pallas_call x1, Pallas kernels: 169 us -> 162 us  [forward(): pl.pallas_call(partial(forward_kernel, levels, groups, fast), out_shape=[...]
    pallas_call x2 -> x1, Pallas kernels: 176 us -> 183 us  [backward(): pl.pallas_call(partial(backward_kernel, levels, fast, token_total), out_s...]
    unnamed x34 -> x45, local copies, waits for them, and re-layouts: 3.6 us -> 10 us
where the time goes in v5:
time: 384 us; the launch traced here: 383 us
  Pallas kernels  345 us (90%)
  local copies, waits for them, and re-layouts  32.3 us (8%)
  other arithmetic  4.81 us (1%)
    pallas_call x1, Pallas kernels, backward(): pl.pallas_call(partial(backward_kernel, levels, fast, token_total), out_s...  183 us
    pallas_call x1, Pallas kernels, forward(): pl.pallas_call(partial(forward_kernel, levels, groups, fast), out_shape=[...  162 us
    unnamed x45, local copies, waits for them, and re-layouts  10 us
    reshape x4, local copies, waits for them, and re-layouts, from_matrix(): dense.reshape(2, 4, rows, COLS).transpose(0, 2, 1, 3)  7.9 us

profile of v5, /device:TPU:0, one launch (start us, length us, event | category | flops | bytes accessed | tf_op | source)
XLA Modules:
  0.0 382.8 jit_solution(14764914481989570034)
XLA Ops:
  0.7 0.0 copy-start.2
  0.7 0.8 reshape.111
  1.5 0.8 reshape.117
  2.3 0.8 reshape.118
  3.0 1.3 fusion.3.refs_4_.refs_25_
  4.3 1.3 select_maximum_fusion
  5.7 1.1 copy.36
  6.8 0.0 copy-start.3
  6.8 2.2 pad_maximum_fusion.refs_0_.refs_24_
  9.0 0.0 copy-done.2
  9.0 1.2 copy.37
  10.2 0.0 copy-done.3
  10.2 1.2 copy.38
  11.3 0.0 copy-done.1
  11.3 1.3 pad.16.refs_2_
  12.6 0.6 broadcast_1_refs_5__refs_6_.2.refs_5_.refs_6_
  13.2 162.1 %forward.1 = (bf16[224,1024]{1,0:T(8,128)(2,1)}, f32[16,1024]{1,0:T(8,128)}, bf16[448,1024]{1,0:T(8,128)(2,1)}, bf16[2,224,1024]{2,1,0:T(8,128)(2,1)}, bf16[3,2,...) custom-call(bf16[16,128,256]{2,1,0:T(8,128)(2,1)} %pad_maximum_fusio, ...), custom_call_target="tpu_custom_call" | custom-call | tf_op jit(solution)/shard_map/forward/pallas_call | solution.py:746
  175.3 182.9 %backward.1 = (f32[8,128,256]{2,1,0:T(8,128)}, f32[8,128,256]{2,1,0:T(8,128)}, f32[224,1024]{1,0:T(8,128)}, f32[750,1024]{1,0:T(8,128)}, f32[16,128]{1,0:T(8,128...) custom-call(bf16[2,224,1024]{2,1,0:T(8,128)(2,1)} %get-tuple-element, ...), custom_call_target="tpu_custom_call" | custom-call | tf_op jit(solution)/shard_map/backward/pallas_call | solution.py:1588
  358.2 0.0 copy-start.10
  358.2 0.8 slice.30
  358.9 0.7 reshape.121
  359.6 0.7 slice.32
  360.3 0.7 reshape.124
  360.9 0.7 slice.34
  361.6 0.7 reshape.127
  362.3 0.7 slice.36
  363.0 0.7 reshape.130
  363.6 1.3 slice_bitcast_fusion
  364.9 3.0 copy.50
  367.9 0.0 copy-done.10
  367.9 1.6 copy.49
  369.5 0.0 copy-done.9
  369.5 1.6 copy.48
  371.2 0.0 copy-done.8
  371.2 1.6 copy.47
  372.8 0.8 copy.62
  373.6 0.9 copy.63
  374.5 1.6 copy.64
  376.2 0.3 copy-done.7
  376.5 1.0 copy.65
  377.5 0.6 copy.66
  378.1 0.0 copy-done.6
  378.1 1.0 copy.67
  379.1 0.6 copy.68
  379.7 1.0 copy.69
  380.6 0.6 copy.70
  381.2 1.0 copy.71
  382.2 0.6 copy.72
  (23 shorter events, 0.0 us)
Async XLA Ops:
  0.7 8.3 %copy-start.2 = (f32[2,128,4,256]{3,2,1,0:T(4,128)S(1)}, f32[2,128,4,256]{3,2,1,0:T(4,128)}, u32[]{:S(2)}) copy-start(f32[2,128,4,256]{3,2,1,0:T(4,128)} %param.23) | copy-start | bytes 3145732
  6.8 3.4 copy-start.3
  9.0 2.4 copy-start.1
  358.2 9.7 %copy-start.10 = (f32[8,128,256]{2,1,0:T(8,128)S(1)}, f32[8,128,256]{2,1,0:T(8,128)}, u32[]{:S(2)}) copy-start(f32[8,128,256]{2,1,0:T(8,128)} %get-tuple-element.84) | copy-start | bytes 3145732
  364.9 4.6 %copy-start.9 = (f32[8,128,256]{2,1,0:T(8,128)S(1)}, f32[8,128,256]{2,1,0:T(8,128)}, u32[]{:S(2)}) copy-start(f32[8,128,256]{2,1,0:T(8,128)} %get-tuple-element.87) | copy-start | bytes 3145732
  367.9 3.3 copy-start.8
  369.5 3.3 copy-start.12
  371.2 2.4 copy-start.11
  371.2 3.3 copy-start
  374.5 2.0 copy-start.7
  374.5 2.9 copy-start.16
  376.5 1.6 copy-start.6
  376.5 2.6 copy-start.15
  376.5 3.2 copy-start.5
  378.1 2.6 copy-start.14
  378.1 3.2 copy-start.4
  379.7 2.5 copy-start.13

commit v6 on v5

--- a/solution.py
+++ b/solution.py
@@ -233,7 +233,7 @@
 BLOCK = 32
 SOFT_TURNS = 14
 NORM_TURNS = 7
-BACK_TURNS = 12
+BACK_TURNS = 6
 
 
 def dot(a, b, dims):
@@ -425,7 +425,7 @@
                     r.p[rows, 0:total] = (e * (1.0 / weight)).astype(bf)
                     lse[rows, :] = jnp.where(lane == t * 2 + sub, top + jnp.log(weight), lse[rows, :])
 
-                rows_loop(L, rows_body, SOFT_TURNS)
+                rows_loop(L, rows_body, 7 if causal else SOFT_TURNS)
                 for i in range(per_head):
                     tick((t * 2 + sub) * per_head + i)
                 acc = None
@@ -553,17 +553,19 @@
 
         loop(4, tile)
 
+    emit(r.wide_out.at[0:8], r.wide.at[0:8])
     for m in range(4):
         gather.need(8 + m)
         loop(2, lambda side: hidden(2 * m + side))
     emit(r.z_out, r.z)
     emit(r.slope_out, r.slope)
+    emit(r.wide_out.at[8:12], r.wide.at[8:12])
     for k in range(2):
         gather.need(12 + 2 * k)
         gather.need(13 + 2 * k)
         result(k)
 
-    emit(r.wide_out, r.wide)
+    emit(r.wide_out.at[12:16], r.wide.at[12:16])
 
     for half in range(2):
         @pl.when(c == half)
@@ -741,7 +743,7 @@
         pltpu.VMEM((peers, 16, 128) if fast else (1, 16, 128), f32), pltpu.VMEM((8, 2 * KEYS), f32),
         pltpu.VMEM((HALF, D), bf),
         sem((4,)), sem((3,)), sem((3,)), sem((3, 4)), sem((3, 4)), sem((peers,)), sem((peers,)),
-        sem((len(shapes),)),
+        sem((len(shapes) + 2,)),
     ]
     outs = pl.pallas_call(
         partial(forward_kernel, levels, groups, fast),
@@ -936,8 +938,10 @@
     square_dense: object
     shard: object
     pack: object
-    pack_mean: object
-    pack_square: object
+    norm_mean: object
+    unit_mean: object
+    norm_square: object
+    unit_square: object
 
 
 class BackwardOut(NamedTuple):
@@ -947,15 +951,8 @@
     frame_out: object
     small_out: object
     bcols_out: object
-    mean_attn: object
-    mean_dense: object
-    square_attn: object
-    square_dense: object
-    step_attn: object
-    step_dense: object
-    small_mean: object
-    small_square: object
-    small_step: object
+    norm_out: object
+    unit_out: object
     norms: object
 
 
@@ -966,15 +963,8 @@
     frame_out: object
     small_out: object
     bcols_out: object
-    mean_attn: object
-    mean_dense: object
-    square_attn: object
-    square_dense: object
-    step_attn: object
-    step_dense: object
-    small_mean: object
-    small_square: object
-    small_step: object
+    norm_out: object
+    unit_out: object
     norms: object
     part: object
     own: object
@@ -1029,7 +1019,6 @@
     sumsgot: object
     sumspair: object
     load_sem: object
-    store_sem: object
     step_sem: object
     pair_sem: object
     sums_send: object
@@ -1185,13 +1174,20 @@
         r.slope[t] = du
         r.bcols[pl.ds(8 + t, 1), :] = jnp.sum(du.astype(f32), axis=0, keepdims=True)
 
-    loop(8, hidden_back)
     loaded(get_z)
-    grads(
-        lambda cols: [r.dy[:, :, cols].reshape(L, COLS)],
-        [(12 + t // 2, t % 2, lambda t=t: [r.z[t]]) for t in range(8)],
-    )
-    scatter.send(4)
+
+    def down_grads(k):
+        m = 3 - k
+        loop(2, lambda side: hidden_back(2 * m + side))
+        grads(
+            lambda cols: [r.dy[:, :, cols].reshape(L, COLS)],
+            [(12 + m, side, lambda side=side: [r.z[2 * m + side]]) for side in range(2)],
+        )
+        for copy in scatter.first(k):
+            copy.start()
+
+    loop(4, down_grads)
+    scatter.sent = 4
     loaded(get_w1)
     send_back(0, [(lambda t=t: r.slope[t], 8 + t // 2, t % 2) for t in range(8)])
     loaded(get_a3, get_h2, get_norm)
@@ -1405,14 +1401,6 @@
             either(m, lambda: copy(attn, m), lambda: copy(dense, m - 8), action)
         action(pltpu.make_async_copy(given.shard.at[m], r.held.at[slot], r.load_sem.at[slot, 2]))
 
-    def moment_stores(g, action):
-        m, slot = MATS - 1 - g, lax.rem(g, 2)
-        for k, (attn, dense) in enumerate(((r.mean_attn, r.mean_dense), (r.square_attn, r.square_dense))):
-            def copy(dst, at):
-                return pltpu.make_async_copy(r.moments.at[slot, k], dst.at[at], r.store_sem.at[slot, k])
-
-            either(m, lambda: copy(attn, m), lambda: copy(dense, m - 8), action)
-
     def begin(copy):
         copy.start()
 
@@ -1425,42 +1413,31 @@
 
         either(m, lambda: copy(attn, m), lambda: copy(dense, m - 8), action)
 
-    def adapted(gradient, moment, second, weight):
+    def direction(gradient, moment, second, weight):
         scaled = gradient / token_total
         moment = 0.5 * moment + 0.5 * scaled
         second = 0.5 * second + 0.5 * scaled * scaled
-        return moment, second, moment / (jnp.sqrt(second) + 1e-06) + 0.01 * weight
+        return moment / (jnp.sqrt(second) + 1e-06) + 0.01 * weight
 
     def update(g):
         m, slot = MATS - 1 - g, lax.rem(g, 2)
         whole_store(m, r.owned_attn, r.owned_dense, begin)
         moment_loads(g, end)
 
-        @pl.when(g >= 1)
-        def _():
-            moment_stores(g - 1, end)
-
         @pl.when(g + 1 < MATS)
         def _():
             moment_loads(g + 1, begin)
 
-        whole_store(m, r.owned_attn, r.owned_dense, end)
         r.squares[pl.ds(m, 1), :] = jnp.zeros((1, COLS), f32)
         r.squares[pl.ds(MATS + m, 1), :] = jnp.zeros((1, COLS), f32)
 
         def block(rows, i):
             weight = r.held[slot, rows, :].astype(f32)
-            moment, second, direction = adapted(
-                r.own[m, rows, :], r.moments[slot, 0, rows, :], r.moments[slot, 1, rows, :], weight
-            )
-            r.moments[slot, 0, rows, :] = moment
-            r.moments[slot, 1, rows, :] = second
-            r.own[m, rows, :] = direction
-            r.squares[pl.ds(m, 1), :] += jnp.sum(direction * direction, axis=0, keepdims=True)
+            step = direction(r.own[m, rows, :], r.moments[slot, 0, rows, :], r.moments[slot, 1, rows, :], weight)
+            r.squares[pl.ds(m, 1), :] += jnp.sum(step * step, axis=0, keepdims=True)
             r.squares[pl.ds(MATS + m, 1), :] += jnp.sum(weight * weight, axis=0, keepdims=True)
 
         rows_loop(rows_of, block, 2)
-        moment_stores(g, begin)
 
     if fast:
         moment_loads(0, begin)
@@ -1486,26 +1463,33 @@
         for k in range(1, 4 * levels):
             total = total + r.smallgot[k]
         r.smallsum[...] = total
-        moment, second, direction = adapted(total, given.pack_mean[...], given.pack_square[...], given.pack[...])
-        r.small_mean[...] = moment
-        r.small_square[...] = second
+
+        def units(pack):
+            return jnp.concatenate([pack[9 + k // 2 : 10 + k // 2, k % 2 * HD : k % 2 * HD + HD] for k in range(4)])
+
+        weights = given.pack[...]
+        r.norm_out[...] = total[0:9]
+        r.unit_out[...] = units(total)
+        norm_step = direction(total[0:9], given.norm_mean[...], given.norm_square[...], weights[0:9])
+        unit_step = direction(units(total), given.unit_mean[...], given.unit_square[...], units(weights))
         lanes = lax.broadcasted_iota(jnp.int32, (1, 128), 1)
-        wide_lane = lax.broadcasted_iota(jnp.int32, (16, 128), 1)
-        row = lax.broadcasted_iota(jnp.int32, (16, 128), 0)
-        place_of = jnp.where(row < 9, 18 + row, jnp.where(row < 11, 10 + dp, 127))
-        counted = jnp.where(row < 9, jnp.where((x == 0) & (c == 0), 1.0, 0.0), 1.0)
-
-        def spread(first_row, small):
+        wide_lane = lax.broadcasted_iota(jnp.int32, (9, 128), 1)
+        row = lax.broadcasted_iota(jnp.int32, (9, 128), 0)
+        leader = jnp.where((x == 0) & (c == 0), 1.0, 0.0)
+
+        def spread(first_row, norm, unit):
             line = jnp.zeros((1, 128), f32)
             for m in range(MATS):
                 k = first_row + m
                 one = jnp.sum(r.squares[k : k + 1, :], axis=1, keepdims=True)
                 line = line + jnp.where(lanes == (m if m < 8 else 8 + (m - 8) // 4), one, 0.0)
-            per_row = jnp.sum(small * small * counted, axis=1, keepdims=True)
-            return line + jnp.sum(jnp.where(wide_lane == place_of, per_row, 0.0), axis=0, keepdims=True)
-
-        r.sums[0, 0:1, :] = spread(MATS, given.pack[...])
-        r.sums[0, 1:2, :] = spread(0, direction)
+            per_row = jnp.sum(norm * norm * leader, axis=1, keepdims=True)
+            line = line + jnp.sum(jnp.where(wide_lane == 18 + row, per_row, 0.0), axis=0, keepdims=True)
+            one = jnp.sum(jnp.sum(unit * unit, axis=1, keepdims=True), axis=0, keepdims=True)
+            return line + jnp.where(lanes == 10 + dp, one, 0.0)
+
+        r.sums[0, 0:1, :] = spread(MATS, weights[0:9], units(weights))
+        r.sums[0, 1:2, :] = spread(0, norm_step, unit_step)
         pair = remote(r.sums.at[0], r.sumspair, r.pair_sem.at[0], r.pair_sem.at[1], mate)
         pair.start()
         pair.wait_recv()
@@ -1521,23 +1505,10 @@
         all_sums = r.sumsgot[0]
         for k in range(1, 4 * levels):
             all_sums = all_sums + r.sumsgot[k]
-        norms = jnp.sqrt(all_sums)
-        r.norms[...] = norms
-        trust = norms[0:1] / norms[1:2]
-
-        def scale(m):
-            at = jnp.where(m < 8, m, 8 + (m - 8) // 4)
-            factor = -learning_rate * jnp.sum(jnp.where(lanes == at, trust, 0.0), axis=1, keepdims=True)
-            r.own[m] = r.own[m] * factor
-            whole_store(m, r.step_attn, r.step_dense, begin)
-
-        loop(MATS, scale)
-        small_factor = jnp.sum(jnp.where(wide_lane == place_of, trust, 0.0), axis=1, keepdims=True)
-        r.small_step[...] = jnp.where(row < 11, -learning_rate * small_factor * direction, 0.0)
+        r.norms[...] = jnp.sqrt(all_sums)
         pair.wait_send()
         loop(count - 1, lambda k: small_copy(k, me).wait_send())
         loop(count - 1, lambda k: sums_copy(k, me).wait_send())
-        moment_stores(MATS - 1, end)
     small_store = pltpu.make_async_copy(r.smallsum, r.small_out, r.out_sem.at[2])
     bcols_store = pltpu.make_async_copy(r.bcols, r.bcols_out, r.out_sem.at[3])
     small_store.start()
@@ -1552,7 +1523,7 @@
     scatter.drain()
     input_copy.wait()
     if fast:
-        loop(MATS, lambda m: whole_store(m, r.step_attn, r.step_dense, end))
+        loop(MATS, lambda m: whole_store(m, r.owned_attn, r.owned_dense, end))
 
 
 def backward(kept, state, token_total, shards):
@@ -1565,7 +1536,7 @@
     half = ((8, rows, COLS), f32)
     shapes = [half, half, ((HALF, D), f32), ((HALF_FRAMES, D), f32)]
     shapes += [((16, 128) if fast else (16, D), f32), ((16, COLS), f32)]
-    shapes += [half] * 6 + [((16, 128), f32)] * 3 + [((8, 128), f32)]
+    shapes += [((9, 128), f32), ((4, HD), f32), ((8, 128), f32)]
     small = (peers, 16, 128) if fast else (1, 16, 128)
     vm = pltpu.VMEM
     inside = pl.BlockSpec(memory_space=pltpu.VMEM)
@@ -1582,14 +1553,14 @@
         vm((16, 128) if fast else (16, D), f32),
         sem((24,)), sem((3, 4)), sem((3, 4)), sem((4,)), sem((4,)), sem((4,)), sem((peers,)), sem((peers,)), sem((4,)),
         vm((2, 2, rows, COLS), f32), vm((2, rows, COLS), bf), vm((2 * MATS, COLS), f32), vm((2, 8, 128), f32),
-        vm((peers if fast else 1, 8, 128), f32), vm((8, 128), f32), sem((2, 3)), sem((2, 2)), sem((MATS,)), sem((2,)),
+        vm((peers if fast else 1, 8, 128), f32), vm((8, 128), f32), sem((2, 3)), sem((MATS,)), sem((2,)),
         sem((peers,)), sem((peers,)),
     ]
     return pl.pallas_call(
         partial(backward_kernel, levels, fast, token_total),
         out_shape=[jax.ShapeDtypeStruct(s, t) for s, t in shapes],
-        in_specs=[hbm] * (len(BackwardIn._fields) - 3) + [inside] * 3,
-        out_specs=[hbm] * (len(shapes) - 4) + [inside] * 4,
+        in_specs=[hbm] * (len(BackwardIn._fields) - 5) + [inside] * 5,
+        out_specs=[hbm] * (len(shapes) - 3) + [inside] * 3,
         scratch_shapes=scratch + Scatter.buffers(levels, rows) + Scatter.semaphores(levels),
         compiler_params=pltpu.CompilerParams(
             collective_id=1, has_side_effects=True, vmem_limit_bytes=63 * 2**20
@@ -1728,18 +1699,10 @@
     def from_matrix(attn, dense):
         return attn.reshape(2, 4, rows, COLS), dense.reshape(2, 4, rows, COLS).transpose(0, 2, 1, 3)
 
-    def small_pack(norm, unit):
-        if rows != 128:
-            return jnp.zeros((16, 128), f32)
-        return jnp.pad(jnp.concatenate([norm, unit.reshape(2, 128)]), ((0, 5), (0, 0)))
-
-    def from_pack(pack):
-        return pack[9:11].reshape(4, unit_cols), pack[:9]
-
     token_total = float(tokens.shape[0] * shards * 4)
     state = (
         *by_matrix(attention_mean, dense_mean), *by_matrix(attention_square, dense_square), shard, small[0],
-        small_pack(norm_mean, unit_mean), small_pack(norm_square, unit_square),
+        norm_mean, unit_mean, norm_square, unit_square,
     )
     done = BackwardOut(*backward(kept, state, token_total, shards))
     input_gradient, frame_gradient = done.input_out, done.frame_out
@@ -1747,14 +1710,7 @@
     small_grads = (done.small_out, done.bcols_out)
 
     if rows == 128:
-        unit_owned, norm_owned = from_pack(done.small_out)
-        means = (*from_matrix(done.mean_attn, done.mean_dense), *from_pack(done.small_mean))
-        seconds = (*from_matrix(done.square_attn, done.square_dense), *from_pack(done.small_square))
-        steps = (*from_matrix(done.step_attn, done.step_dense), *from_pack(done.small_step))
-        return (
-            layer_out, input_gradient, frame_gradient, attention_owned, dense_owned, unit_owned, norm_owned,
-            *means, *seconds, *steps, done.norms[0, :27], done.norms[1, :27],
-        )
+        unit_owned, norm_owned = done.unit_out, done.norm_out
     else:
         norm_parts = small_grads[0][:9].reshape(9, shards, rows).transpose(1, 0, 2).reshape(shards, 1, 9 * rows)
         unit_parts = small_grads[1].reshape(8, 2, 4, HD).transpose(1, 2, 0, 3).reshape(2, 4, shards, unit_cols)
@@ -1777,16 +1733,19 @@
     norm_moment, norm_second, norm_dir = adapt(
         own_norm, norm_owned, norm_mean, norm_square, token_total
     )
-    sums = jnp.concatenate(
-        [
-            square_rows(own_attn, own_dense, own_unit, own_norm),
-            square_rows(attn_dir, dense_dir, unit_dir, norm_dir),
-        ]
-    )
-    sums = jnp.pad(sums, (0, 1024 - 54)).reshape(8, 128)
-    sums = jnp.sum(small_exchange(sums, shards, True, False, 14), axis=0).reshape(1024)
-    weight_norms = jnp.sqrt(sums[:27])
-    step_norms = jnp.sqrt(sums[27:54])
+    if rows == 128:
+        weight_norms, step_norms = done.norms[0, :27], done.norms[1, :27]
+    else:
+        sums = jnp.concatenate(
+            [
+                square_rows(own_attn, own_dense, own_unit, own_norm),
+                square_rows(attn_dir, dense_dir, unit_dir, norm_dir),
+            ]
+        )
+        sums = jnp.pad(sums, (0, 1024 - 54)).reshape(8, 128)
+        sums = jnp.sum(small_exchange(sums, shards, True, False, 14), axis=0).reshape(1024)
+        weight_norms = jnp.sqrt(sums[:27])
+        step_norms = jnp.sqrt(sums[27:54])
     trust = weight_norms / step_norms
     attention_step = -learning_rate * trust[0:8].reshape(2, 4, 1, 1) * attn_dir
     dense_step = -learning_rate * trust[8:10].reshape(2, 1, 1, 1) * dense_dir

time: 384 us -> 366 us (0.953)
  local copies, waits for them, and re-layouts: 32.3 us -> 17.1 us
  Pallas kernels: 345 us -> 332 us
  other arithmetic: 4.81 us -> 14.9 us
    reshape x10 -> x0, local copies, waits for them, and re-layouts: 12.1 us -> none  [the longest x4 7.9 us: from_matrix(): dense.reshape(2, 4, rows, COLS).transpose(0, 2, 1, 3)]
    pallas_call x1, Pallas kernels: 183 us -> 171 us  [backward(): pl.pallas_call(partial(backward_kernel, levels, fast, token_total), out_s...]
    mul x0 -> x7, other arithmetic: none -> 10.7 us  [the longest x2 6.16 us: shards_fn(): dense_step = -learning_rate * trust[8:10].reshape(2, 1, 1, 1) * dense_dir]
    unnamed x45 -> x32, local copies, waits for them, and re-layouts: 10 us -> 10.1 us
where the time goes in v6:
time: 366 us; the launch traced here: 365 us
  Pallas kernels  332 us (91%)
  local copies, waits for them, and re-layouts  17.1 us (5%)
  other arithmetic  14.9 us (4%)
    pallas_call x1, Pallas kernels, backward(): pl.pallas_call(partial(backward_kernel, levels, fast, token_total), out_s...  171 us
    pallas_call x1, Pallas kernels, forward(): pl.pallas_call(partial(forward_kernel, levels, groups, fast), out_shape=[...  161 us
    unnamed x32, local copies, waits for them, and re-layouts  10.1 us

profile of v6, /device:TPU:0, one launch (start us, length us, event | category | flops | bytes accessed | tf_op | source)
XLA Modules:
  0.0 365.0 jit_solution(5584621285984118551)
XLA Ops:
  0.7 0.0 copy-start.4
  0.7 1.2 copy.40
  1.9 2.1 pad_maximum_fusion.refs_0_.refs_24_
  4.0 0.0 copy-done.4
  4.0 0.0 copy-start.12
  4.0 1.3 pad.8.refs_2_
  5.3 0.0 copy-done.12
  5.3 0.1 reshape.113
  5.4 0.0 copy-done.8
  5.4 0.6 select_maximum_fusion.refs_4_.refs_25_
  6.0 0.6 broadcast_15_refs_5__refs_6_.2.refs_5_.refs_6_
  6.6 161.0 %forward.1 = (bf16[224,1024]{1,0:T(8,128)(2,1)}, f32[16,1024]{1,0:T(8,128)}, bf16[448,1024]{1,0:T(8,128)(2,1)}, bf16[2,224,1024]{2,1,0:T(8,128)(2,1)}, bf16[3,2,...) custom-call(bf16[16,128,256]{2,1,0:T(8,128)(2,1)} %pad_maximum_fusio, ...), custom_call_target="tpu_custom_call" | custom-call | tf_op jit(solution)/shard_map/forward/pallas_call | solution.py:748
  167.6 0.0 copy-start
  167.6 2.5 copy.41
  170.1 0.0 copy-done
  170.1 1.2 copy.42
  171.3 171.3 %backward.1 = (f32[8,128,256]{2,1,0:T(8,128)}, f32[8,128,256]{2,1,0:T(8,128)}, f32[224,1024]{1,0:T(8,128)}, f32[750,1024]{1,0:T(8,128)}, f32[16,128]{1,0:T(8,128...) custom-call(bf16[2,224,1024]{2,1,0:T(8,128)(2,1)} %get-tuple-element.50.refs_0_, ...), custom_call_target="tpu_custom_call" | custom-call | tf_op jit(solution)/shard_map/backward/pallas_call | solution.py:1559
  342.6 1.3 fusion
  343.9 0.1 slice_multiply_fusion.1
  344.0 6.1 %add_multiply_fusion = (f32[2,128,4,256]{3,2,1,0:T(4,128)}, f32[2,128,4,256]{3,2,1,0:T(4,128)}, f32[2,128,4,256]{3,2,1,0:T(4,128)}, f32[2,128,4,256]{3,2,1,0:T(4,128)}) fusion(bf16[2,128,4,256]{3,2,1,0:T(4,128)(2,1)} %param.19, f32[2]{0:T(128)S(1)} %slice_multiply_fusion.1, f32[2,128,4,256]{3,2,1,0:T(4,128)} %param.27, f32[2,128,4,256]{3,2,1,0:T(4,128)} %param.23, ...), kind=kLoop, calls=%fused_computation.2 | loop fusion | flops 3407872 | bytes 7864328 | tf_op jit(solution)/shard_map/mul | solution.py:1751
  350.1 0.1 fusion.1
  350.1 0.1 mul.178
  350.2 0.0 copy-done.1
  350.2 0.0 copy-done.2
  350.2 0.0 copy-done.3
  350.2 0.0 copy-start.9
  350.2 0.0 copy-start.10
  350.2 0.0 copy-start.11
  350.2 0.0 copy-start.5
  350.3 0.0 copy-start.6
  350.3 0.0 copy-start.7
  350.3 3.2 add_multiply_fusion.1
  353.5 0.1 select_reduce_fusion
  353.6 0.0 copy-done.9
  353.6 0.0 copy-done.10
  353.6 0.0 copy-done.11
  353.6 0.6 add_multiply_fusion.3
  354.2 0.1 slice_multiply_fusion
  354.3 0.0 copy-done.5
  354.3 0.0 copy-done.6
  354.3 0.0 copy-done.7
  354.3 0.7 add_multiply_fusion.2
  355.0 1.8 copy.52
  356.8 2.2 copy.53
  359.0 3.9 %copy.54 = f32[750,1024]{1,0:T(8,128)} copy(f32[750,1024]{1,0:T(8,128)} %get-tuple-element.118) | data formatting | bytes 6144000
  362.9 1.0 copy.55
  363.9 0.6 copy.56
  364.4 0.6 copy.57
  (7 shorter events, 0.0 us)
Async XLA Ops:
  0.7 3.4 copy-start.4
  4.0 1.3 copy-start.12
  4.0 1.4 copy-start.8
  167.6 2.5 copy-start
  344.0 6.2 %copy-start.1 = (f32[2,4,128,256]{3,2,1,0:T(8,128)S(1)}, f32[2,4,128,256]{3,2,1,0:T(8,128)}, u32[]{:S(2)}) copy-start(f32[2,4,128,256]{3,2,1,0:T(8,128)} %param.22) | copy-start | bytes 3145732
  344.0 6.2 %copy-start.2 = (f32[2,4,128,256]{3,2,1,0:T(8,128)S(1)}, f32[2,4,128,256]{3,2,1,0:T(8,128)}, u32[]{:S(2)}) copy-start(f32[2,4,128,256]{3,2,1,0:T(8,128)} %param.26) | copy-start | bytes 3145732
  344.0 6.2 %copy-start.3 = (f32[8,128,256]{2,1,0:T(8,128)S(1)}, f32[8,128,256]{2,1,0:T(8,128)}, u32[]{:S(2)}) copy-start(f32[8,128,256]{2,1,0:T(8,128)} %get-tuple-element.72) | copy-start | bytes 3145732
  350.2 3.4 copy-start.9
  350.2 3.4 copy-start.10
  350.2 3.4 copy-start.11
  350.2 4.0 %copy-start.5 = (f32[9,128]{1,0:T(8,128)S(1)}, f32[9,128]{1,0:T(8,128)}, u32[]{:S(2)}) copy-start(f32[9,128]{1,0:T(8,128)} %refs_26_.1) | copy-start | bytes 13828
  350.3 4.0 %copy-start.6 = (f32[9,128]{1,0:T(8,128)S(1)}, f32[9,128]{1,0:T(8,128)}, u32[]{:S(2)}) copy-start(f32[9,128]{1,0:T(8,128)} %refs_28_.1) | copy-start | bytes 13828
  350.3 4.0 %copy-start.7 = (f32[9,128]{1,0:T(8,128)S(1)}, f32[9,128]{1,0:T(8,128)}, u32[]{:S(2)}) copy-start(f32[9,128]{1,0:T(8,128)} %get-tuple-element.122) | copy-start | bytes 13828
